TPU v7x, 256 devices: a 8x8x2 block of a 8x8x16 slice. The times are simulated.
256 devices in a mesh: beam: 2 (over z), tm: 16 (over x, core), dm: 8 (over y).
Axes of the slice: x: 8, y: 8, z: 2, core: 2. Of those that a mesh axis runs over, the one named last changes fastest.
The devices are a block of a 8x8x16 slice.
Arguments:
- series: float32 [32, 524288], P(('beam', 'dm'), 'tm'), parts along dimension 0, may hold values from -16 to 16
- cand_start: int32 [32, 8, 8, 16], P(('beam', 'tm'), 'dm'), parts along dimension 0, may hold values from 0 to 1920
- cand_count: int32 [32, 8, 8], P(('beam', 'tm'), 'dm'), parts along dimension 0, may hold values from 0 to 16, as said below
Outputs:
- harmonic_sum: float32 [32, 32768], P(('beam', 'dm'), 'tm'), parts along dimension 0
- sifted: float32 [32, 8, 8, 16, 128], P(('beam', 'tm'), 'dm'), parts along dimension 0
There are 2 independent parts, one for each index of `beam`. A program takes and returns all parts, laid end to end along the dimension named above; each array names one. Nothing has to cross between parts.
Inputs may be any that keep to these rules, and one draw needn't show every extreme that they name: `cand_count`: in every draw some destination band receives 16 live slots from every source band and frequency shard.
All inputs are finite; a program needn't handle non-finite values.
Results may differ from a plain program's by a relative error of at most 0.00015.
Values sent between devices are 32-bit elements; how exact they have to be, the bound alone decides.
No kernel may reach another device: no remote copies, remote signals or barrier semaphores. Data moves between devices by JAX's collectives and lax.ppermute only.
A program may use at most 128 MiB of HBM per device.

v0:
```python
import functools
import math

import jax
import jax.numpy as jnp
import numpy as np
from jax import lax
from jax.experimental import pallas as pl
from jax.experimental.pallas import tpu as pltpu
from jax.sharding import PartitionSpec as P

HARM = 8
BW = 128
EPSILON = 1e-06

LANES = 128
SUB = 8
COARSE = 256
SLOTS = 8
PIECE = 32
PIECES = [(h, c) for h in range(1, HARM + 1) for c in range(h)]
CHUNKS = len(PIECES) // 4

F32 = jnp.float32
BF16 = jnp.bfloat16


def halves(value):
    top = value.astype(BF16)
    return top, (value - top.astype(F32)).astype(BF16)


def np_halves(value):
    top = value.astype(np.float32).astype(BF16)
    rest = (value - top.astype(np.float64)).astype(np.float32).astype(BF16)
    return top, rest


def unit(turns, period):
    angle = -2.0 * math.pi * (turns % period) / period
    return np.cos(angle), np.sin(angle)


@functools.cache
def tables(shards, samples):
    inner = samples // COARSE
    a = np.arange(COARSE)
    r = np.arange(COARSE // 2)
    c1, s1 = unit(r[:, None] * a[None, :], COARSE)
    s1[0] = np.where(a % 2 == 0, 1.0, -1.0)
    first = np_halves(np.concatenate([c1, s1], axis=0))
    b = np.arange(LANES)
    j = np.arange(LANES // 2)
    rows = []
    for q2 in (j, LANES - 1 - j):
        c2, s2 = unit(q2[:, None] * b[None, :], LANES)
        rows += [np.concatenate([c2, -s2], axis=1), np.concatenate([s2, c2], axis=1)]
    second = np_halves(np.concatenate(rows, axis=0))
    s = np.arange(shards)
    pos = LANES * s[:, None] + b[None, :]
    slot = np.arange(SLOTS)
    by_slot = np.stack(unit(pos[:, None, :] * slot[None, :, None], samples))
    by_shard = np.stack(unit(SLOTS * s[:, None, None] * pos[None], samples), axis=1)
    by_extra = np.stack(unit((COARSE // 2) * pos, samples))
    between = np.stack(unit(s[:, None] * b[None, :], inner))
    small = [t.astype(np.float32) for t in (by_slot, by_shard, by_extra, between)]
    return first, second, small


def pack_kernel(x_ref, o_ref):
    shards = o_ref.shape[0] // 32
    chunks = x_ref.shape[1] // (LANES * shards)
    for d in range(shards):
        for a in range(chunks):
            piece = x_ref[:, pl.ds((a * shards + d) * LANES, LANES)]
            o_ref[pl.ds(d * 2 * chunks + a, 2, stride=chunks), :] = piece


def first_kernel(x_ref, th_ref, tl_ref, o_ref):
    shards = x_ref.shape[0]
    part = x_ref.shape[1] // 2
    tops, rests = [], []
    for row in range(2):
        top, rest = halves(x_ref[:, row * part : (row + 1) * part, :].reshape(COARSE, LANES))
        tops.append(top)
        rests.append(rest)
    top = jnp.concatenate(tops, axis=1)
    rest = jnp.concatenate(rests, axis=1)
    dot = functools.partial(jnp.dot, preferred_element_type=F32)
    y = dot(th_ref[...], top) + dot(th_ref[...], rest) + dot(tl_ref[...], top)
    half = COARSE // 2
    for part_id in range(2):
        for row in range(2):
            block = y[part_id * half : (part_id + 1) * half, row * LANES : (row + 1) * LANES]
            at = (part_id * 2 + row) * SUB
            o_ref[:, at : at + SUB, :] = block.reshape(shards, SUB, LANES)


def cmul(x, y):
    return x[0] * y[0] - x[1] * y[1], x[0] * y[1] + x[1] * y[0]


def cadd(x, y):
    return x[0] + y[0], x[1] + y[1]


def csub(x, y):
    return x[0] - y[0], x[1] - y[1]


def turn_back(x):
    return x[1], -x[0]


def four(x0, x1, x2, x3):
    s, d = cadd(x0, x2), csub(x0, x2)
    t, u = cadd(x1, x3), turn_back(csub(x1, x3))
    return cadd(s, t), cadd(d, u), csub(s, t), csub(d, u)


def sixteen(values):
    columns = [four(*values[low::4]) for low in range(4)]
    out = [None] * 16
    for k1 in range(4):
        terms = []
        for low in range(4):
            term = columns[low][k1]
            if low * k1:
                c, s = unit(np.float64(low * k1), 16)
                if abs(s + 1.0) < 1e-12:
                    term = turn_back(term)
                else:
                    term = cmul(term, (F32(c), F32(s)))
            terms.append(term)
        for k2, value in enumerate(four(*terms)):
            out[k1 + 4 * k2] = value
    return out


def second_kernel(d_ref, x_ref, ws_ref, wd_ref, wx_ref, a_ref, th_ref, tl_ref, o_ref, t_scr, dh_scr, dl_scr, r_scr, l_scr, s_scr, h_scr):
    shards = x_ref.shape[0]
    me = d_ref[0]
    is_first = me == 0
    sub = lax.broadcasted_iota(jnp.int32, (SUB, LANES), 0)
    lead = jnp.logical_and(sub == 0, is_first)

    for row in range(2):
        main, extra = [], []
        for s in range(shards):
            re = x_ref[s, row * SUB : (row + 1) * SUB, :]
            im = x_ref[s, (2 + row) * SUB : (3 + row) * SUB, :]
            own = wd_ref[0, 0, s : s + 1, :], wd_ref[0, 1, s : s + 1, :]
            twiddle = cmul((ws_ref[0, s], ws_ref[1, s]), own)
            main.append(cmul((re, jnp.where(lead, 0.0, im)), twiddle))
            extra.append((im * wx_ref[0, s : s + 1, :], im * wx_ref[1, s : s + 1, :]))
        for kind, values in enumerate((main, extra)):
            for rho, value in enumerate(sixteen(values)):
                value = cmul(value, (a_ref[0, rho : rho + 1, :], a_ref[1, rho : rho + 1, :]))
                t_scr[kind * 2 + row, rho, 0] = value[0]
                t_scr[kind * 2 + row, rho, 1] = value[1]

    for rho in range(shards):
        for part in range(2):
            low = jnp.concatenate([t_scr[0, rho, part], t_scr[1, rho, part]], axis=0)
            high = jnp.concatenate(
                [jnp.where(lead, t_scr[2 + row, rho, part], t_scr[row, shards - 1 - rho, part]) for row in range(2)],
                axis=0,
            )
            for k, tile in enumerate((low, high)):
                top, rest = halves(tile)
                rows = pl.ds(rho * PIECE + k * 16, 16)
                cols = pl.ds(part * LANES, LANES)
                dh_scr[rows, cols] = top
                dl_scr[rows, cols] = rest
    dims = (((1,), (1,)), ((), ()))
    dot_t = functools.partial(lax.dot_general, dimension_numbers=dims, preferred_element_type=F32)
    half = LANES // 2
    lane = lax.broadcasted_iota(jnp.int32, (half, 2 * LANES), 1)
    within = lane % PIECE
    from_low = jnp.logical_or(within < 16, jnp.logical_and(within % SUB == 0, is_first))
    scale = 1.0 / (shards * LANES * COARSE)
    powers = []
    for part in range(2):
        top = dh_scr[part * 256 : (part + 1) * 256, :]
        rest = dl_scr[part * 256 : (part + 1) * 256, :]
        z = dot_t(th_ref[...], top) + dot_t(th_ref[...], rest) + dot_t(tl_ref[...], top)
        z = z * z
        low = z[0:half] + z[half : 2 * half]
        high = z[2 * half : 3 * half] + z[3 * half :]
        powers.append(jnp.where(from_low, low, high) * scale)

    count = 2 * SLOTS * LANES * shards // 2
    one_row = (lane // SUB) % 2 == 1
    column = jnp.sum(powers[0] + powers[1], axis=0, keepdims=True)
    row_lane = one_row[0:1, :]
    mean0 = jnp.sum(jnp.where(row_lane, 0.0, column), axis=1, keepdims=True) / count
    mean1 = jnp.sum(jnp.where(row_lane, column, 0.0), axis=1, keepdims=True) / count
    centre = jnp.where(row_lane, mean1, mean0)
    off0 = powers[0] - centre
    off1 = powers[1] - centre
    column = jnp.sum(off0 * off0 + off1 * off1, axis=0, keepdims=True)
    dev0 = jnp.sum(jnp.where(row_lane, 0.0, column), axis=1, keepdims=True)
    dev1 = jnp.sum(jnp.where(row_lane, column, 0.0), axis=1, keepdims=True)
    stats = jnp.where(sub == 0, mean0, jnp.where(sub == 1, mean1, jnp.where(sub == 2, dev0, dev1)))
    for t in range(shards):
        o_ref[t, 4 * SUB : 5 * SUB, :] = stats

    for group in range(4):
        value = powers[group // 2][:, (group % 2) * LANES : (group % 2 + 1) * LANES]
        for shift in range(4):
            at = (group * 4 + shift) * half
            r_scr[at : at + half, :] = pltpu.roll(value, shift * PIECE, 1) if shift else value
    lane8 = lax.broadcasted_iota(jnp.int32, (SUB, LANES), 1) // PIECE
    for chunk in range(CHUNKS):
        for g_pair in range(shards // 2):
            tiles = []
            for g0 in (2 * g_pair, 2 * g_pair + 1):
                tile = None
                for place in range(4):
                    h, c = PIECES[chunk * 4 + place]
                    rho, e = (h * g0 + c) % shards, (h * g0 + c) // shards
                    shift = (place - rho % 4) % 4
                    rows = pl.ds((rho // 4 * 4 + shift) * half + e, SUB, stride=h)
                    got = r_scr[rows, :]
                    tile = got if tile is None else jnp.where(lane8 == place, got, tile)
                tiles.append(tile)
            top, rest = halves(jnp.concatenate(tiles, axis=0))
            cols = pl.ds(chunk * LANES, LANES)
            l_scr[pl.ds(g_pair * 16, 16), cols] = top
            l_scr[pl.ds(LANES + g_pair * 16, 16), cols] = rest
    phi = lax.broadcasted_iota(jnp.int32, (SUB, COARSE), 1)
    slot = lax.broadcasted_iota(jnp.int32, (SUB, COARSE), 0)
    mine = me * SLOTS + slot
    mirror = jnp.where(mine == 0, COARSE // 2, COARSE - mine)
    none = jnp.zeros((SUB, COARSE), F32)
    for index, (h, c) in enumerate(PIECES):
        for k, residue in enumerate((mine, mirror)):
            hit = jnp.where(h * phi - COARSE * c == residue, 1.0, 0.0)
            rows = pl.ds(index * PIECE + k * 16, 16)
            s_scr[rows, 0:COARSE] = jnp.concatenate([hit, none], axis=0).astype(BF16)
            s_scr[rows, COARSE : 2 * COARSE] = jnp.concatenate([none, hit], axis=0).astype(BF16)
    both = jnp.dot(l_scr[...], s_scr[...], preferred_element_type=F32)
    for tile in range(4):
        cols = slice(tile * LANES, (tile + 1) * LANES)
        h_scr[tile * LANES : (tile + 1) * LANES, :] = both[:LANES, cols] + both[LANES:, cols]
    for t in range(shards):
        for tile in range(4):
            rows = pl.ds(tile * LANES + (t % 2) * 64 + t // 2, SUB, stride=SUB)
            o_ref[t, tile * SUB : (tile + 1) * SUB, :] = h_scr[rows, :]


def third_kernel(x_ref, m_ref, hs_ref, msg_ref, level_ref):
    shards = x_ref.shape[0]
    total = x_ref[0]
    for s in range(1, shards):
        total = total + x_ref[s]
    mean = total[4 * SUB : 5 * SUB] / shards
    count = 2 * SLOTS * LANES * shards // 2
    between = jnp.zeros((SUB, LANES), F32)
    for s in range(shards):
        off = x_ref[s, 4 * SUB : 5 * SUB, :] - mean
        between = between + off * off
    tiles = []
    for row in range(2):
        deviation = total[4 * SUB + 2 + row : 4 * SUB + 3 + row] + count * between[row : row + 1]
        scale = 1.0 / jnp.sqrt(deviation / (count * shards) + EPSILON)
        shift = HARM * mean[row : row + 1]
        tiles.append([(total[(2 * row + k) * SUB : (2 * row + k + 1) * SUB] - shift) * scale for k in range(2)])
    for row in range(2):
        for k in range(2):
            for g in range(SUB):
                hs_ref[row : row + 1, pl.ds(g * COARSE + k * LANES, LANES)] = tiles[row][k][g : g + 1]
    for k in range(2):
        level_ref[k * SUB : (k + 1) * SUB, :] = (tiles[0][k] + tiles[1][k]) / 2
        peak = jnp.maximum(tiles[0][k], tiles[1][k])
        for e in range(msg_ref.shape[0]):
            msg_ref[e, k * SUB : (k + 1) * SUB, :] = peak
    for e in range(msg_ref.shape[0]):
        msg_ref[e, 2 * SUB : 3 * SUB, :] = m_ref[e]


def sift_kernel(x_ref, level_ref, o_ref):
    bands = x_ref.shape[0]
    level = level_ref[...]
    diff = jnp.concatenate([x_ref[d, 0:16, :] - level for d in range(bands)], axis=0)
    columns = []
    for d in range(bands):
        tile = x_ref[d, 16:24, :]
        for k in range(2):
            at = k * (LANES // 2)
            columns.append(jnp.broadcast_to(tile[:, at : at + 1], (SUB, LANES)))
    start = jnp.concatenate(columns, axis=0).astype(jnp.int32)
    rows = bands * 16
    lane = lax.broadcasted_iota(jnp.int32, (rows, LANES), 1)
    owner = lax.broadcasted_iota(jnp.int32, (rows, LANES), 0) // 16
    block = jnp.maximum(start, 0)
    tile_id, offset = block // LANES, block % LANES

    def pick(which):
        place = (which % 2) * SUB + which // 2
        hit = jnp.logical_and(jnp.logical_and(lane // 16 == owner, lane % 16 == place), which < 16)
        return jnp.where(hit, 1.0, 0.0).astype(BF16)

    top, rest = halves(diff)
    last = (diff - top.astype(F32) - rest.astype(F32)).astype(BF16)
    dot = functools.partial(jnp.dot, preferred_element_type=F32)
    here, after = pick(tile_id), pick(tile_id + 1)
    first = dot(here, top) + dot(here, rest) + dot(here, last)
    second = dot(after, top) + dot(after, rest) + dot(after, last)
    joined = jnp.where(lane >= offset, first, second)
    index = (lane + offset) % LANES
    moved = jnp.take_along_axis(joined, index, axis=1)
    moved = jnp.where(start >= 0, moved, 0.0)
    o_ref[...] = moved.reshape(bands, 16, LANES)


def call(kernel, out, inputs, scratch=()):
    vmem = pl.BlockSpec(memory_space=pltpu.VMEM)
    many = isinstance(out, (tuple, list))
    return pl.pallas_call(
        kernel,
        out_shape=out,
        in_specs=[vmem] * len(inputs),
        out_specs=[vmem] * len(out) if many else vmem,
        scratch_shapes=list(scratch),
    )(*inputs)


def shape(*dims):
    return jax.ShapeDtypeStruct(dims, F32)


def run_pack(series, shards):
    return call(pack_kernel, shape(shards * 32, LANES), [series]).reshape(shards, 32, LANES)


def run_first(received, first):
    return call(first_kernel, shape(*received.shape), [received, *map(jnp.asarray, first)])


def run_second(me, received, second, small):
    shards = received.shape[0]
    by_slot, by_shard, by_extra, between = map(jnp.asarray, small)
    inputs = [received, by_slot, by_shard, by_extra, between, *map(jnp.asarray, second)]

    def whole(array):
        return pl.BlockSpec(array.shape, lambda i, d: (0,) * array.ndim)

    specs = [whole(x) for x in inputs]
    specs[2] = pl.BlockSpec((1, *by_shard.shape[1:]), lambda i, d: (d[0], 0, 0, 0))
    out = shape(shards, 5 * SUB, LANES)
    return pl.pallas_call(
        second_kernel,
        out_shape=out,
        grid_spec=pltpu.PrefetchScalarGridSpec(
            num_scalar_prefetch=1,
            grid=(1,),
            in_specs=specs,
            out_specs=whole(out),
            scratch_shapes=[
                pltpu.VMEM((4, shards, 2, SUB, LANES), F32),
                pltpu.VMEM((shards * PIECE, 2 * LANES), BF16),
                pltpu.VMEM((shards * PIECE, 2 * LANES), BF16),
                pltpu.VMEM((16 * LANES // 2, LANES), F32),
                pltpu.VMEM((2 * LANES, CHUNKS * LANES), BF16),
                pltpu.VMEM((CHUNKS * LANES, 2 * COARSE), BF16),
                pltpu.VMEM((4 * LANES, LANES), F32),
            ],
        ),
    )(me, *inputs)


def run_third(received, markers):
    bands = markers.shape[0]
    out = (shape(2, SUB * COARSE), shape(bands, 3 * SUB, LANES), shape(2 * SUB, LANES))
    return call(third_kernel, out, [received, markers])


def run_sift(received, level):
    return call(sift_kernel, shape(received.shape[0], 16, LANES), [received, level])


def make_markers(cand_start, cand_count):
    starts = cand_start[0, 0]
    counts = cand_count[0, 0]
    bands, slot_total = starts.shape
    live = jnp.arange(slot_total, dtype=jnp.int32)[None, :] < counts[:, None]
    markers = jnp.where(live, starts, -1).astype(F32)
    tiles = jnp.swapaxes(markers.reshape(bands, 2, SUB), 1, 2)[..., None]
    return jnp.broadcast_to(tiles, (bands, SUB, 2, LANES // 2)).reshape(bands, SUB, LANES)


def per_device(series, cand_start, cand_count):
    shards = lax.axis_size("tm")
    first, second, small = tables(shards, shards * series.shape[1])
    me = lax.axis_index("tm").astype(jnp.int32).reshape(1)
    markers = make_markers(cand_start, cand_count)
    swap = functools.partial(lax.all_to_all, split_axis=0, concat_axis=0, tiled=True)
    samples = swap(run_pack(series, shards), "tm")
    partial = swap(run_first(samples, first), "tm")
    sums = swap(run_second(me, partial, second, small), "tm")
    harmonic_sum, message, level = run_third(sums, markers)
    sifted = run_sift(swap(message, "dm"), level)
    return harmonic_sum, sifted[None, None]


def solution(mesh):
    return jax.shard_map(
        per_device,
        mesh=mesh,
        in_specs=(
            P(("beam", "dm"), "tm"),
            P(("beam", "tm"), "dm", None, None),
            P(("beam", "tm"), "dm", None),
        ),
        out_specs=(P(("beam", "dm"), "tm"), P(("beam", "tm"), "dm", None, None, None)),
        check_vma=False,
    )
```

profile of v0, /device:TPU:513, one launch (start us, length us, event | category | flops | bytes accessed | tf_op | source)
XLA Modules:
  0.0 92.3 jit_solution(12679876924476270392)
XLA Ops:
  0.6 1.8 %shard_map.122 = f32[512,128]{1,0:T(8,128)} custom-call(f32[2,32768]{1,0:T(2,128)} %x_ref.1), custom_call_target="tpu_custom_call" | custom-call | tf_op jit(solution)/shard_map/pallas_call | solution.py:320
  2.4 36.4 %all_to_all.20.x_ref = f32[16,32,128]{2,1,0:T(8,128)} all-to-all(f32[16,32,128]{2,1,0:T(8,128)} %bitcast.8), channel_id=1, replica_groups=mesh['beam'=2,'tm'=16,'dm'=8] {'tm'}, dimensions={0} | all-to-all | bytes 524288 | tf_op jit(solution)/shard_map/all_to_all | solution.py:399
  38.8 2.0 %shard_map.123 = f32[16,32,128]{2,1,0:T(8,128)} custom-call(f32[16,32,128]{2,1,0:T(8,128)} %all_to_all.20.x_ref, bf16[256,256]{1,0:T(8,128)(2,1)} %constant.26.clone.th_ref, bf16[256,256]{1,0:T(8,128)(2,1)} %constant.27.clone.tl_ref), custom_call_target="tpu_custom_call" | custom-call | tf_op jit(solution)/shard_map/pallas_call | solution.py:320
  40.9 3.7 %all-to-all-start.1 = ((f32[16,32,128]{2,1,0:T(8,128)}), f32[16,32,128]{2,1,0:T(8,128)S(1)}, u32[]{:S(2)}, u32[]{:S(2)}) async-start(f32[16,32,128]{2,1,0:T(8,128)} %shard_map.123), calls=%async_computation.1 | async-start | bytes 524288 | tf_op jit(solution)/shard_map/all_to_all | solution.py:400
  44.6 10.7 %all-to-all-done.1.x_ref = f32[16,32,128]{2,1,0:T(8,128)S(1)} async-done(((f32[16,32,128]{2,1,0:T(8,128)}), f32[16,32,128]{2,1,0:T(8,128)S(1)}, u32[]{:S(2)}, u32[]{:S(2)}) %all-to-all-start.1) | async-done | bytes 262176 | tf_op jit(solution)/shard_map/all_to_all | solution.py:400
  55.2 0.0 copy-start.1
  55.2 0.7 copy-done.1
  55.9 3.3 %shard_map.124 = f32[16,40,128]{2,1,0:T(8,128)} custom-call(s32[1]{0:T(128)} %bitcast.d_ref, f32[16,32,128]{2,1,0:T(8,128)} %copy-done.1, f32[2,16,8,128]{3,2,1,0:T(8,128)} %constant.28.clone.ws_ref, f32[16,2,16,128]{3,2,1,0:T(8,128)} %constant.29.clone.wd_ref, f32[2,16,128]{2,1,0:T(8,128)} %constant.30.clone.wx_ref, f32[2,16,128]{2,1,0:T(8,128)} %constant.31.clone.a_ref, ...), custom_call_target="tpu_custom_call" | custom-call | tf_op jit(solution)/shard_map/pallas_call | solution.py:352
  59.2 0.0 copy-start.2
  59.2 3.8 %all-to-all-start.2 = ((f32[16,40,128]{2,1,0:T(8,128)}), f32[16,40,128]{2,1,0:T(8,128)S(1)}, u32[]{:S(2)}, u32[]{:S(2)}) async-start(f32[16,40,128]{2,1,0:T(8,128)} %shard_map.124), calls=%async_computation.2 | async-start | bytes 655360 | tf_op jit(solution)/shard_map/all_to_all | solution.py:401
  63.0 0.0 copy-done.2
  63.1 0.1 squeeze.3
  63.1 0.0 copy-start.3
  63.1 0.7 copy-done.3
  63.8 0.1 fusion.1
  63.9 0.1 copy.13
  64.0 0.1 broadcast_in_dim.15
  64.1 0.7 reshape.33.m_ref
  64.8 10.7 %all-to-all-done.2.x_ref = f32[16,40,128]{2,1,0:T(8,128)S(1)} async-done(((f32[16,40,128]{2,1,0:T(8,128)}), f32[16,40,128]{2,1,0:T(8,128)S(1)}, u32[]{:S(2)}, u32[]{:S(2)}) %all-to-all-start.2) | async-done | bytes 327712 | tf_op jit(solution)/shard_map/all_to_all | solution.py:401
  75.6 0.0 copy-start
  75.6 0.7 copy-done
  76.3 1.7 %shard_map.125 = (f32[2,2048]{1,0:T(2,128)}, f32[8,24,128]{2,1,0:T(8,128)}, f32[16,128]{1,0:T(8,128)}) custom-call(f32[16,40,128]{2,1,0:T(8,128)} %copy-done, f32[8,8,128]{2,1,0:T(8,128)} %reshape.33.m_ref), custom_call_target="tpu_custom_call" | custom-call | tf_op jit(solution)/shard_map/pallas_call | solution.py:320
  78.0 12.3 %all_to_all.21.x_ref = f32[8,24,128]{2,1,0:T(8,128)} all-to-all(f32[8,24,128]{2,1,0:T(8,128)} %get-tuple-element.6), channel_id=1, replica_groups=mesh['beam'=2,'tm'=16,'dm'=8] {'dm'}, dimensions={0} | all-to-all | bytes 196608 | tf_op jit(solution)/shard_map/all_to_all | solution.py:403
  90.2 2.0 %shard_map.126 = f32[8,16,128]{2,1,0:T(8,128)} custom-call(f32[8,24,128]{2,1,0:T(8,128)} %all_to_all.21.x_ref, f32[16,128]{1,0:T(8,128)} %get-tuple-element.7.level_ref), custom_call_target="tpu_custom_call" | custom-call | tf_op jit(solution)/shard_map/pallas_call | solution.py:320
  (1 shorter events, 0.0 us)
Async XLA Ops:
  40.9 14.4 %all-to-all-start.1 = ((f32[16,32,128]{2,1,0:T(8,128)}), f32[16,32,128]{2,1,0:T(8,128)S(1)}, u32[]{:S(2)}, u32[]{:S(2)}) async-start(f32[16,32,128]{2,1,0:T(8,128)} %shard_map.123), calls=%async_computation.1 | async-start | bytes 524288 | tf_op jit(solution)/shard_map/all_to_all | solution.py:400
  55.2 0.7 copy-start.1
  59.2 3.8 %copy-start.2 = (s32[1,1,8,16]{3,2,1,0:T(8,128)S(1)}, s32[1,1,8,16]{3,2,1,0:T(8,128)}, u32[]{:S(2)}) copy-start(s32[1,1,8,16]{3,2,1,0:T(8,128)} %param.12) | copy-start | bytes 1540
  59.2 16.4 %all-to-all-start.2 = ((f32[16,40,128]{2,1,0:T(8,128)}), f32[16,40,128]{2,1,0:T(8,128)S(1)}, u32[]{:S(2)}, u32[]{:S(2)}) async-start(f32[16,40,128]{2,1,0:T(8,128)} %shard_map.124), calls=%async_computation.2 | async-start | bytes 655360 | tf_op jit(solution)/shard_map/all_to_all | solution.py:401
  63.1 0.7 copy-start.3
  75.6 0.7 copy-start
where the time goes:
time: 92.9 us; the launch traced here: 92.3 us
  blocking collectives  48.7 us (52%)
  waiting for transfers between devices  21.4 us (23%)
  Pallas kernels  10.8 us (12%)
  starting transfers between devices  7.52 us (8%)
  local copies, waits for them, and re-layouts  3.14 us (3%)
    all_to_all x1, blocking collectives, per_device(): samples = swap(run_pack(series, shards), 'tm')  36.4 us
    all_to_all x1, blocking collectives, per_device(): sifted = run_sift(swap(message, 'dm'), level)  12.3 us
    all_to_all x1, waiting for transfers between devices, per_device(): sums = swap(run_second(me, partial, second, small), 'tm')  10.7 us
    all_to_all x1, waiting for transfers between devices, per_device(): partial = swap(run_first(samples, first), 'tm')  10.7 us
    pallas_call x4, Pallas kernels, call(): pl.pallas_call(kernel, out_shape=out, in_specs=[vmem] * len(inputs), out_...  7.56 us
    all_to_all x1, starting transfers between devices, per_device(): sums = swap(run_second(me, partial, second, small), 'tm')  3.83 us
    all_to_all x1, starting transfers between devices, per_device(): partial = swap(run_first(samples, first), 'tm')  3.69 us
    pallas_call x1, Pallas kernels, run_second(): pl.pallas_call(second_kernel, out_shape=out, grid_spec=pltpu.PrefetchScal...  3.26 us
  transfers between devices with their start and end apart: 2, of which 2 were waited for; matrix products, arithmetic and copies ran while one was open for 1% of the time, Pallas kernels for 0%

commit v1 on v0

--- a/solution.py
+++ b/solution.py
@@ -67,13 +67,21 @@
     return first, second, small
 
 
-def pack_kernel(x_ref, o_ref):
+def pack_kernel(start_ref, count_ref, x_ref, o_ref, m_ref):
     shards = o_ref.shape[0] // 32
     chunks = x_ref.shape[1] // (LANES * shards)
     for d in range(shards):
         for a in range(chunks):
             piece = x_ref[:, pl.ds((a * shards + d) * LANES, LANES)]
             o_ref[pl.ds(d * 2 * chunks + a, 2, stride=chunks), :] = piece
+    sub = lax.broadcasted_iota(jnp.int32, (SUB, LANES), 0)
+    half = lax.broadcasted_iota(jnp.int32, (SUB, LANES), 1) // (LANES // 2)
+    place = half * SUB + sub
+    for e in range(m_ref.shape[0]):
+        tile = jnp.zeros((SUB, LANES), jnp.int32)
+        for c in range(2 * SUB):
+            tile = jnp.where(place == c, start_ref[e, c], tile)
+        m_ref[e] = jnp.where(place < count_ref[e], tile, -1).astype(F32)
 
 
 def first_kernel(x_ref, th_ref, tl_ref, o_ref):
@@ -149,7 +157,7 @@
         for s in range(shards):
             re = x_ref[s, row * SUB : (row + 1) * SUB, :]
             im = x_ref[s, (2 + row) * SUB : (3 + row) * SUB, :]
-            own = wd_ref[0, 0, s : s + 1, :], wd_ref[0, 1, s : s + 1, :]
+            own = wd_ref[me, 0, s : s + 1, :], wd_ref[me, 1, s : s + 1, :]
             twiddle = cmul((ws_ref[0, s], ws_ref[1, s]), own)
             main.append(cmul((re, jnp.where(lead, 0.0, im)), twiddle))
             extra.append((im * wx_ref[0, s : s + 1, :], im * wx_ref[1, s : s + 1, :]))
@@ -314,7 +322,14 @@
     o_ref[...] = moved.reshape(bands, 16, LANES)
 
 
-def call(kernel, out, inputs, scratch=()):
+PARAMS = pltpu.CompilerParams(vmem_limit_bytes=16 * 2**20)
+
+
+def near(array):
+    return pltpu.with_memory_space_constraint(array, pltpu.VMEM)
+
+
+def call(kernel, out, inputs):
     vmem = pl.BlockSpec(memory_space=pltpu.VMEM)
     many = isinstance(out, (tuple, list))
     return pl.pallas_call(
@@ -322,81 +337,71 @@
         out_shape=out,
         in_specs=[vmem] * len(inputs),
         out_specs=[vmem] * len(out) if many else vmem,
-        scratch_shapes=list(scratch),
+        compiler_params=PARAMS,
     )(*inputs)
 
 
 def shape(*dims):
-    return jax.ShapeDtypeStruct(dims, F32)
-
-
-def run_pack(series, shards):
-    return call(pack_kernel, shape(shards * 32, LANES), [series]).reshape(shards, 32, LANES)
+    return pltpu.VMEM(dims, F32)
+
+
+def run_pack(series, starts, counts, shards):
+    vmem = pl.BlockSpec(memory_space=pltpu.VMEM)
+    smem = pl.BlockSpec(memory_space=pltpu.SMEM)
+    packed, markers = pl.pallas_call(
+        pack_kernel,
+        out_shape=(shape(shards * 32, LANES), shape(counts.shape[0], SUB, LANES)),
+        in_specs=[smem, smem, vmem],
+        out_specs=[vmem, vmem],
+        compiler_params=PARAMS,
+    )(starts, counts, series)
+    return packed.reshape(shards, 32, LANES), markers
 
 
 def run_first(received, first):
-    return call(first_kernel, shape(*received.shape), [received, *map(jnp.asarray, first)])
+    return call(first_kernel, shape(*received.shape), [near(x) for x in (received, *map(jnp.asarray, first))])
 
 
 def run_second(me, received, second, small):
     shards = received.shape[0]
     by_slot, by_shard, by_extra, between = map(jnp.asarray, small)
-    inputs = [received, by_slot, by_shard, by_extra, between, *map(jnp.asarray, second)]
-
-    def whole(array):
-        return pl.BlockSpec(array.shape, lambda i, d: (0,) * array.ndim)
-
-    specs = [whole(x) for x in inputs]
-    specs[2] = pl.BlockSpec((1, *by_shard.shape[1:]), lambda i, d: (d[0], 0, 0, 0))
-    out = shape(shards, 5 * SUB, LANES)
+    inputs = [near(x) for x in (received, by_slot, by_shard, by_extra, between, *map(jnp.asarray, second))]
+    vmem = pl.BlockSpec(memory_space=pltpu.VMEM)
     return pl.pallas_call(
         second_kernel,
-        out_shape=out,
-        grid_spec=pltpu.PrefetchScalarGridSpec(
-            num_scalar_prefetch=1,
-            grid=(1,),
-            in_specs=specs,
-            out_specs=whole(out),
-            scratch_shapes=[
-                pltpu.VMEM((4, shards, 2, SUB, LANES), F32),
-                pltpu.VMEM((shards * PIECE, 2 * LANES), BF16),
-                pltpu.VMEM((shards * PIECE, 2 * LANES), BF16),
-                pltpu.VMEM((16 * LANES // 2, LANES), F32),
-                pltpu.VMEM((2 * LANES, CHUNKS * LANES), BF16),
-                pltpu.VMEM((CHUNKS * LANES, 2 * COARSE), BF16),
-                pltpu.VMEM((4 * LANES, LANES), F32),
-            ],
-        ),
+        out_shape=shape(shards, 5 * SUB, LANES),
+        in_specs=[pl.BlockSpec(memory_space=pltpu.SMEM)] + [vmem] * len(inputs),
+        out_specs=vmem,
+        scratch_shapes=[
+            pltpu.VMEM((4, shards, 2, SUB, LANES), F32),
+            pltpu.VMEM((shards * PIECE, 2 * LANES), BF16),
+            pltpu.VMEM((shards * PIECE, 2 * LANES), BF16),
+            pltpu.VMEM((16 * LANES // 2, LANES), F32),
+            pltpu.VMEM((2 * LANES, CHUNKS * LANES), BF16),
+            pltpu.VMEM((CHUNKS * LANES, 2 * COARSE), BF16),
+            pltpu.VMEM((4 * LANES, LANES), F32),
+        ],
+        compiler_params=PARAMS,
     )(me, *inputs)
 
 
 def run_third(received, markers):
     bands = markers.shape[0]
-    out = (shape(2, SUB * COARSE), shape(bands, 3 * SUB, LANES), shape(2 * SUB, LANES))
-    return call(third_kernel, out, [received, markers])
+    out = (jax.ShapeDtypeStruct((2, SUB * COARSE), F32), shape(bands, 3 * SUB, LANES), shape(2 * SUB, LANES))
+    return call(third_kernel, out, [near(received), near(markers)])
 
 
 def run_sift(received, level):
-    return call(sift_kernel, shape(received.shape[0], 16, LANES), [received, level])
-
-
-def make_markers(cand_start, cand_count):
-    starts = cand_start[0, 0]
-    counts = cand_count[0, 0]
-    bands, slot_total = starts.shape
-    live = jnp.arange(slot_total, dtype=jnp.int32)[None, :] < counts[:, None]
-    markers = jnp.where(live, starts, -1).astype(F32)
-    tiles = jnp.swapaxes(markers.reshape(bands, 2, SUB), 1, 2)[..., None]
-    return jnp.broadcast_to(tiles, (bands, SUB, 2, LANES // 2)).reshape(bands, SUB, LANES)
+    return call(sift_kernel, jax.ShapeDtypeStruct((received.shape[0], 16, LANES), F32), [near(received), near(level)])
 
 
 def per_device(series, cand_start, cand_count):
     shards = lax.axis_size("tm")
     first, second, small = tables(shards, shards * series.shape[1])
-    me = lax.axis_index("tm").astype(jnp.int32).reshape(1)
-    markers = make_markers(cand_start, cand_count)
+    me, series = lax.optimization_barrier((lax.axis_index("tm").astype(jnp.int32).reshape(1), series))
     swap = functools.partial(lax.all_to_all, split_axis=0, concat_axis=0, tiled=True)
-    samples = swap(run_pack(series, shards), "tm")
+    packed, markers = run_pack(series, cand_start[0, 0], cand_count[0, 0], shards)
+    samples = swap(packed, "tm")
     partial = swap(run_first(samples, first), "tm")
     sums = swap(run_second(me, partial, second, small), "tm")
     harmonic_sum, message, level = run_third(sums, markers)

time: 92.9 us -> 83.2 us (0.90)
  blocking collectives: 48.7 us -> 76.3 us
  waiting for transfers between devices: 21.4 us -> 0 us
  starting transfers between devices: 7.52 us -> 0 us
  Pallas kernels: 10.8 us -> 4.24 us
  local copies, waits for them, and re-layouts: 3.14 us -> 1.67 us
    all_to_all x1 -> x3, blocking collectives: 36.4 us -> 64.9 us  [the longest x1 34.9 us: per_device(): samples = swap(packed, 'tm')]
    all_to_all x2 -> x0, waiting for transfers between devices: 21.4 us -> none  [the longest x1 10.7 us: per_device(): sums = swap(run_second(me, partial, second, small), 'tm')]
    all_to_all x2 -> x0, starting transfers between devices: 7.52 us -> none  [the longest x1 3.83 us: per_device(): sums = swap(run_second(me, partial, second, small), 'tm')]
    pallas_call x4 -> x3, Pallas kernels: 7.56 us -> 2.09 us  [call(): pl.pallas_call(kernel, out_shape=out, in_specs=[vmem] * len(inputs), out_...]
    pallas_call x1 -> x2, Pallas kernels: 3.26 us -> 2.14 us  [the longest x1 1.37 us: run_second(): pl.pallas_call(second_kernel, out_shape=shape(shards, 5 * SUB, LANES), in...]
    all_to_all x1, blocking collectives: 12.3 us -> 11.3 us  [per_device(): sifted = run_sift(swap(message, 'dm'), level)]
    unnamed x8 -> x22, local copies, waits for them, and re-layouts: 2.09 us -> 1.67 us
  transfers between devices with their start and end apart: 2 -> 0, of which waited for: 2 -> 0; matrix products, arithmetic and copies ran while one was open for 1% -> 0% of each run, Pallas kernels for 0% -> 0%
where the time goes in v1:
time: 83.2 us; the launch traced here: 82.9 us
  blocking collectives  76.3 us (92%)
  Pallas kernels  4.24 us (5%)
  local copies, waits for them, and re-layouts  1.67 us (2%)
    all_to_all x1, blocking collectives, per_device(): samples = swap(packed, 'tm')  34.9 us
    all_to_all x1, blocking collectives, per_device(): sums = swap(run_second(me, partial, second, small), 'tm')  15.8 us
    all_to_all x1, blocking collectives, per_device(): partial = swap(run_first(samples, first), 'tm')  14.2 us
    all_to_all x1, blocking collectives, per_device(): sifted = run_sift(swap(message, 'dm'), level)  11.3 us
    pallas_call x3, Pallas kernels, call(): pl.pallas_call(kernel, out_shape=out, in_specs=[vmem] * len(inputs), out_...  2.09 us
    unnamed x22, local copies, waits for them, and re-layouts  1.67 us

profile of v1, /device:TPU:513, one launch (start us, length us, event | category | flops | bytes accessed | tf_op | source)
XLA Modules:
  0.0 82.9 jit_solution(8887410323467886186)
XLA Ops:
  0.6 0.0 copy-start.9
  0.6 0.0 copy-start.10
  0.7 0.7 copy-done.9
  1.3 0.0 copy-done.10
  1.3 0.0 copy-start
  1.3 0.9 %copy-done = f32[2,32768]{1,0:T(2,128)S(1)} copy-done((f32[2,32768]{1,0:T(2,128)S(1)}, f32[2,32768]{1,0:T(2,128)}, u32[]{:S(2)}) %copy-start) | copy-done | bytes 262168
  2.3 0.8 shard_map.122
  3.1 0.0 copy-start.5
  3.1 0.0 copy-start.6
  3.1 34.9 %all_to_all.20.x_ref = f32[16,32,128]{2,1,0:T(8,128)S(1)} all-to-all(f32[16,32,128]{2,1,0:T(8,128)S(1)} %bitcast.5), channel_id=1, replica_groups=mesh['beam'=2,'tm'=16,'dm'=8] {'tm'}, dimensions={0} | all-to-all | bytes 524288 | tf_op jit(solution)/shard_map/all_to_all | solution.py:404
  38.0 0.0 copy-done.5
  38.0 0.0 copy-done.6
  38.0 0.0 copy-start.4
  38.0 0.0 copy-start.7
  38.0 0.0 copy-start.8
  38.1 0.3 shard_map.123
  38.3 0.0 copy-start.1
  38.3 0.0 copy-start.2
  38.4 0.0 copy-start.3
  38.4 14.2 %all_to_all.21.x_ref = f32[16,32,128]{2,1,0:T(8,128)S(1)} all-to-all(f32[16,32,128]{2,1,0:T(8,128)S(1)} %shard_map.123), channel_id=1, replica_groups=mesh['beam'=2,'tm'=16,'dm'=8] {'tm'}, dimensions={0} | all-to-all | bytes 524288 | tf_op jit(solution)/shard_map/all_to_all | solution.py:405
  52.6 0.0 copy-done.4
  52.6 0.0 copy-done.7
  52.6 0.0 copy-done.8
  52.6 0.0 copy-done.1
  52.6 0.0 copy-done.2
  52.6 0.0 copy-done.3
  52.7 1.4 %shard_map.124 = f32[16,40,128]{2,1,0:T(8,128)S(1)} custom-call(s32[1]{0:T(128)} %bitcast.d_ref, f32[16,32,128]{2,1,0:T(8,128)S(1)} %all_to_all.21.x_ref, f32[2,16,8,128]{3,2,1,0:T(8,128)S(1)} %copy-done.4, f32[16,2,16,128]{3,2,1,0:T(8,128)S(1)} %copy-done.1, f32[2,16,128]{2,1,0:T(8,128)S(1)} %copy-done.8, f32[2,16,128]{2,1,0:T(8,128)S(1)} %copy-done.7, ...), custom_call_target="tpu_custom_call" | custom-call | tf_op jit(solution)/shard_map/pallas_call | solution.py:370
  54.0 15.8 %all_to_all.22.x_ref = f32[16,40,128]{2,1,0:T(8,128)S(1)} all-to-all(f32[16,40,128]{2,1,0:T(8,128)S(1)} %shard_map.124), channel_id=1, replica_groups=mesh['beam'=2,'tm'=16,'dm'=8] {'tm'}, dimensions={0} | all-to-all | bytes 655360 | tf_op jit(solution)/shard_map/all_to_all | solution.py:406
  69.8 0.7 shard_map.125
  70.5 11.3 %all_to_all.23.x_ref = f32[8,24,128]{2,1,0:T(8,128)S(1)} all-to-all(f32[8,24,128]{2,1,0:T(8,128)S(1)} %get-tuple-element.14), channel_id=1, replica_groups=mesh['beam'=2,'tm'=16,'dm'=8] {'dm'}, dimensions={0} | all-to-all | bytes 196608 | tf_op jit(solution)/shard_map/all_to_all | solution.py:408
  81.8 1.2 %shard_map.126 = f32[8,16,128]{2,1,0:T(8,128)} custom-call(f32[8,24,128]{2,1,0:T(8,128)S(1)} %all_to_all.23.x_ref, f32[16,128]{1,0:T(8,128)S(1)} %get-tuple-element.15.level_ref), custom_call_target="tpu_custom_call" | custom-call | tf_op jit(solution)/shard_map/pallas_call | solution.py:335
Async XLA Ops:
  0.6 0.7 copy-start.9
  0.6 0.7 copy-start.10
  1.3 1.0 %copy-start = (f32[2,32768]{1,0:T(2,128)S(1)}, f32[2,32768]{1,0:T(2,128)}, u32[]{:S(2)}) copy-start(f32[2,32768]{1,0:T(2,128)} %x_ref) | copy-start | bytes 786436
  3.1 35.0 %copy-start.5 = (bf16[256,256]{1,0:T(8,128)(2,1)S(1)}, bf16[256,256]{1,0:T(8,128)(2,1)}, u32[]{:S(2)}) copy-start(bf16[256,256]{1,0:T(8,128)(2,1)} %constant.23.clone.tl_ref) | copy-start | bytes 393220
  3.1 35.0 %copy-start.6 = (bf16[256,256]{1,0:T(8,128)(2,1)S(1)}, bf16[256,256]{1,0:T(8,128)(2,1)}, u32[]{:S(2)}) copy-start(bf16[256,256]{1,0:T(8,128)(2,1)} %constant.22.clone.th_ref) | copy-start | bytes 393220
  38.0 14.6 %copy-start.4 = (f32[2,16,8,128]{3,2,1,0:T(8,128)S(1)}, f32[2,16,8,128]{3,2,1,0:T(8,128)}, u32[]{:S(2)}) copy-start(f32[2,16,8,128]{3,2,1,0:T(8,128)} %constant.24.clone.ws_ref) | copy-start | bytes 393220
  38.0 14.6 %copy-start.7 = (f32[2,16,128]{2,1,0:T(8,128)S(1)}, f32[2,16,128]{2,1,0:T(8,128)}, u32[]{:S(2)}) copy-start(f32[2,16,128]{2,1,0:T(8,128)} %constant.27.clone.a_ref) | copy-start | bytes 49156
  38.0 14.6 %copy-start.8 = (f32[2,16,128]{2,1,0:T(8,128)S(1)}, f32[2,16,128]{2,1,0:T(8,128)}, u32[]{:S(2)}) copy-start(f32[2,16,128]{2,1,0:T(8,128)} %constant.26.clone.wx_ref) | copy-start | bytes 49156
  38.3 14.3 %copy-start.1 = (f32[16,2,16,128]{3,2,1,0:T(8,128)S(1)}, f32[16,2,16,128]{3,2,1,0:T(8,128)}, u32[]{:S(2)}) copy-start(f32[16,2,16,128]{3,2,1,0:T(8,128)} %constant.25.clone.wd_ref) | copy-start | bytes 786436
  38.3 14.3 %copy-start.2 = (bf16[256,256]{1,0:T(8,128)(2,1)S(1)}, bf16[256,256]{1,0:T(8,128)(2,1)}, u32[]{:S(2)}) copy-start(bf16[256,256]{1,0:T(8,128)(2,1)} %constant.29.clone.tl_ref) | copy-start | bytes 393220
  38.4 14.3 %copy-start.3 = (bf16[256,256]{1,0:T(8,128)(2,1)S(1)}, bf16[256,256]{1,0:T(8,128)(2,1)}, u32[]{:S(2)}) copy-start(bf16[256,256]{1,0:T(8,128)(2,1)} %constant.28.clone.th_ref) | copy-start | bytes 393220

commit v2 on v1

v2 whole, which is shorter than its diff:
```python
import functools
import math

import jax
import jax.numpy as jnp
import numpy as np
from jax import lax
from jax.experimental import pallas as pl
from jax.experimental.pallas import tpu as pltpu
from jax.sharding import PartitionSpec as P

HARM = 8
BW = 128
EPSILON = 1e-06

LANES = 128
SUB = 8
COARSE = 256
SLOTS = 16
PIECE = 32
PIECES = [(h, c) for h in range(1, HARM + 1) for c in range(h)]
CHUNKS = len(PIECES) // 4

F32 = jnp.float32
BF16 = jnp.bfloat16


def halves(value):
    top = value.astype(BF16)
    return top, (value - top.astype(F32)).astype(BF16)


def np_halves(value):
    top = value.astype(np.float32).astype(BF16)
    rest = (value - top.astype(np.float64)).astype(np.float32).astype(BF16)
    return top, rest


def unit(turns, period):
    angle = -2.0 * math.pi * (turns % period) / period
    return np.cos(angle), np.sin(angle)


@functools.cache
def tables(shards, samples):
    part = samples // (shards * shards)
    tiles = part // LANES
    m = np.arange(part)
    v = np.arange(LANES)
    s = np.arange(shards)
    half = shards // 2
    r = np.arange(half)
    within = np.stack(unit(r[:, None] * m[None, :], samples)).reshape(2, half, tiles, LANES)
    shift = np.stack(unit(s[:, None] * r[None, :], shards * shards), axis=1)
    shift = np.broadcast_to(shift[..., None], (shards, 2, half, LANES))
    after = np.stack(unit(s[:, None] * m[None, :], samples // shards)).reshape(2, shards, tiles, LANES)
    middle = (half + shards * r)[:, None] * m[None, :]
    middle = np.stack(unit(middle, samples)).reshape(2, half, tiles, LANES)
    between = np.stack(unit(s[:, None] * v[None, :], part))
    j = np.arange(LANES // 2)
    rows = []
    for q2 in (j, LANES - 1 - j):
        c2, s2 = unit(q2[:, None] * v[None, :], LANES)
        rows += [np.concatenate([c2, -s2], axis=1), np.concatenate([s2, c2], axis=1)]
    last = np_halves(np.concatenate(rows, axis=0))
    first = [x.astype(np.float32) for x in (within, shift)]
    second = [x.astype(np.float32) for x in (after, middle, between)] + list(last)
    return first, second


def cmul(x, y):
    if x[1] is None:
        return x[0] * y[0], x[0] * y[1]
    return x[0] * y[0] - x[1] * y[1], x[0] * y[1] + x[1] * y[0]


def plus(a, b):
    return b if a is None else a if b is None else a + b


def minus(a, b):
    return a if b is None else -b if a is None else a - b


def cadd(x, y):
    return plus(x[0], y[0]), plus(x[1], y[1])


def csub(x, y):
    return minus(x[0], y[0]), minus(x[1], y[1])


def turn_back(x):
    return x[1], minus(None, x[0])


def four(x0, x1, x2, x3):
    s, d = cadd(x0, x2), csub(x0, x2)
    t, u = cadd(x1, x3), turn_back(csub(x1, x3))
    return cadd(s, t), cadd(d, u), csub(s, t), csub(d, u)


def sixteen(values):
    columns = [four(*values[low::4]) for low in range(4)]
    out = [None] * 16
    for k1 in range(4):
        terms = []
        for low in range(4):
            term = columns[low][k1]
            if low * k1 == 4:
                term = turn_back(term)
            elif low * k1:
                c, s = unit(np.float64(low * k1), 16)
                term = cmul(term, (F32(c), F32(s)))
            terms.append(term)
        for k2, value in enumerate(four(*terms)):
            out[k1 + 4 * k2] = value
    return out


def first_kernel(d_ref, x_ref, within_ref, shift_ref, o_ref, w_scr):
    shards = x_ref.shape[0]
    me = d_ref[0]
    tiles = x_ref.shape[2] // LANES
    half = shards // 2
    for r in range(1, half):
        own = [shift_ref[me, part, r : r + 1, :] for part in range(2)]
        twiddle = cmul((within_ref[0, r], within_ref[1, r]), own)
        for part in range(2):
            w_scr[part, r] = twiddle[part]
    for u in range(tiles):
        values = [(x_ref[t, :, u * LANES : (u + 1) * LANES], None) for t in range(shards)]
        classes = sixteen(values)
        for r in range(half):
            if r:
                value = cmul(classes[r], [w_scr[part, r, u : u + 1, :] for part in range(2)])
            else:
                value = classes[0][0], classes[half][0]
            for part in range(2):
                at = r * 4 * tiles + part * tiles + u
                o_ref[pl.ds(at, 2, stride=2 * tiles), :] = value[part]


def second_kernel(d_ref, x_ref, after_ref, middle_ref, between_ref, th_ref, tl_ref, o_ref, v_scr, x_scr, t_scr, dh_scr, dl_scr, r_scr, l_scr, s_scr, h_scr):
    shards = x_ref.shape[0]
    tiles = x_ref.shape[1] // 2
    half = LANES // 2
    own_class = d_ref[0] // 2
    is_first = own_class == 0
    sub = lax.broadcasted_iota(jnp.int32, (SUB, LANES), 0)
    lead = jnp.logical_and(sub == 0, is_first)

    for k in range(tiles // SUB):
        rows = slice(k * SUB, (k + 1) * SUB)
        main, middle = [], []
        for s in range(shards):
            re = x_ref[s, k * SUB : (k + 1) * SUB, :]
            im = x_ref[s, tiles + k * SUB : tiles + (k + 1) * SUB, :]
            main.append((re, jnp.where(is_first, 0.0, im)))
            c, sn = unit(np.float64(s), 2 * shards)
            middle.append((im * F32(c), im * F32(sn) if s else None))
        for slot, value in enumerate(sixteen(main)):
            value = cmul(value, (after_ref[0, slot, rows, :], after_ref[1, slot, rows, :]))
            for part in range(2):
                v_scr[pl.ds(part * tiles * shards + k * SUB * shards + slot, SUB, stride=shards), :] = value[part]
        for slot, value in enumerate(sixteen(middle)[: shards // 2]):
            value = cmul(value, (middle_ref[0, slot, rows, :], middle_ref[1, slot, rows, :]))
            for part in range(2):
                at = part * tiles * SUB + k * SUB * SUB + slot
                x_scr[pl.ds(at, SUB, stride=SUB), :] = value[part]

    groups = [[], [], []]
    for u in range(tiles):
        low, high, mid = [], [], []
        for part in range(2):
            at = part * tiles * shards + u * shards
            low.append(v_scr[at : at + SUB, :])
            high.append(v_scr[at + SUB : at + 2 * SUB, :])
            at = part * tiles * SUB + u * SUB
            mid.append(x_scr[at : at + SUB, :])
        groups[0].append(tuple(low))
        groups[1].append(tuple(jnp.where(is_first, mid[part], high[part]) for part in range(2)))
        groups[2].append(tuple(high))
    for group, values in enumerate(groups):
        for rho, value in enumerate(sixteen(values)):
            value = cmul(value, (between_ref[0, rho : rho + 1, :], between_ref[1, rho : rho + 1, :]))
            for part in range(2):
                t_scr[group, rho, part] = value[part]

    for rho in range(tiles):
        for part in range(2):
            back = tiles - 1 - rho
            low = jnp.concatenate([t_scr[0, rho, part], t_scr[1, rho, part]], axis=0)
            turned = jnp.where(lead, t_scr[2, rho, part], t_scr[0, back, part])
            high = jnp.concatenate([turned, t_scr[1, back, part]], axis=0)
            for k, tile in enumerate((low, high)):
                top, rest = halves(tile)
                rows = pl.ds(rho * PIECE + k * SLOTS, SLOTS)
                cols = pl.ds(part * LANES, LANES)
                dh_scr[rows, cols] = top
                dl_scr[rows, cols] = rest
    dims = (((1,), (1,)), ((), ()))
    dot_t = functools.partial(lax.dot_general, dimension_numbers=dims, preferred_element_type=F32)
    lane = lax.broadcasted_iota(jnp.int32, (half, 2 * LANES), 1)
    within = lane % PIECE
    from_low = jnp.logical_or(within < SLOTS, jnp.logical_and(within == SLOTS, is_first))
    scale = 1.0 / (shards * shards * tiles * LANES)
    powers = []
    for part in range(2):
        top = dh_scr[part * 256 : (part + 1) * 256, :]
        rest = dl_scr[part * 256 : (part + 1) * 256, :]
        z = dot_t(th_ref[...], top) + dot_t(th_ref[...], rest) + dot_t(tl_ref[...], top)
        z = z * z
        low = z[0:half] + z[half : 2 * half]
        high = z[2 * half : 3 * half] + z[3 * half :]
        powers.append(jnp.where(from_low, low, high) * scale)

    count = 2 * SLOTS * half * tiles

    def over_all(value):
        column = jnp.sum(value, axis=0, keepdims=True)
        return jnp.sum(column, axis=1, keepdims=True)

    mean = over_all(powers[0] + powers[1]) / count
    off0, off1 = powers[0] - mean, powers[1] - mean
    deviation = over_all(off0 * off0 + off1 * off1)
    stats = jnp.where(sub == 0, mean, deviation)
    for t in range(shards):
        o_ref[t, 2 * SUB : 3 * SUB, :] = stats

    for group in range(4):
        value = powers[group // 2][:, (group % 2) * LANES : (group % 2 + 1) * LANES]
        for shift in range(4):
            at = (group * 4 + shift) * half
            r_scr[at : at + half, :] = pltpu.roll(value, shift * PIECE, 1) if shift else value
    lane8 = lax.broadcasted_iota(jnp.int32, (SUB, LANES), 1) // PIECE
    for chunk in range(CHUNKS):
        for g_pair in range(tiles // 2):
            parts = []
            for g0 in (2 * g_pair, 2 * g_pair + 1):
                tile = None
                for place in range(4):
                    h, c = PIECES[chunk * 4 + place]
                    rho, e = (h * g0 + c) % tiles, (h * g0 + c) // tiles
                    shift = (place - rho % 4) % 4
                    rows = pl.ds((rho // 4 * 4 + shift) * half + e, SUB, stride=h)
                    got = r_scr[rows, :]
                    tile = got if tile is None else jnp.where(lane8 == place, got, tile)
                parts.append(tile)
            top, rest = halves(jnp.concatenate(parts, axis=0))
            cols = pl.ds(chunk * LANES, LANES)
            l_scr[pl.ds(g_pair * 16, 16), cols] = top
            l_scr[pl.ds(LANES + g_pair * 16, 16), cols] = rest
    phi = lax.broadcasted_iota(jnp.int32, (SLOTS, COARSE), 1)
    slot = lax.broadcasted_iota(jnp.int32, (SLOTS, COARSE), 0)
    pairs = slot * SLOTS - jnp.where(slot < SUB, 0, SUB * SLOTS - SUB)
    mine = jnp.where(is_first, pairs, own_class + SLOTS * slot)
    mirror = jnp.where(mine == 0, COARSE // 2, COARSE - mine)
    for index, (h, c) in enumerate(PIECES):
        for k, residue in enumerate((mine, mirror)):
            hit = jnp.where(h * phi - COARSE * c == residue, 1.0, 0.0)
            s_scr[pl.ds(index * PIECE + k * SLOTS, SLOTS), :] = hit.astype(BF16)
    both = jnp.dot(l_scr[...], s_scr[...], preferred_element_type=F32)
    for tile in range(2):
        cols = slice(tile * LANES, (tile + 1) * LANES)
        h_scr[tile * LANES : (tile + 1) * LANES, :] = both[:LANES, cols] + both[LANES:, cols]
    for t in range(shards):
        for tile in range(2):
            rows = pl.ds(tile * LANES + (t % 2) * half + t // 2, SUB, stride=SUB)
            o_ref[t, tile * SUB : (tile + 1) * SUB, :] = h_scr[rows, :]


def third_kernel(start_ref, count_ref, x_ref, hs_ref, msg_ref, level_ref):
    shards = x_ref.shape[0]
    holders = shards // 2
    count = 2 * SLOTS * (LANES // 2) * SLOTS
    tiles = []
    for row in range(2):
        total = x_ref[row]
        for r in range(1, holders):
            total = total + x_ref[2 * r + row]
        mean = total[2 * SUB : 2 * SUB + 1] / holders
        spread = total[2 * SUB + 1 : 2 * SUB + 2]
        for r in range(holders):
            off = x_ref[2 * r + row, 2 * SUB : 2 * SUB + 1, :] - mean
            spread = spread + count * (off * off)
        scale = 1.0 / jnp.sqrt(spread / (count * holders) + EPSILON)
        tiles.append([(total[k * SUB : (k + 1) * SUB] - HARM * mean) * scale for k in range(2)])
    for row in range(2):
        for k in range(2):
            for g in range(SUB):
                hs_ref[row : row + 1, pl.ds(g * COARSE + k * LANES, LANES)] = tiles[row][k][g : g + 1]
    for k in range(2):
        level_ref[k * SUB : (k + 1) * SUB, :] = (tiles[0][k] + tiles[1][k]) / 2
        peak = jnp.maximum(tiles[0][k], tiles[1][k])
        for e in range(msg_ref.shape[0]):
            msg_ref[e, k * SUB : (k + 1) * SUB, :] = peak
    sub = lax.broadcasted_iota(jnp.int32, (SUB, LANES), 0)
    place = lax.broadcasted_iota(jnp.int32, (SUB, LANES), 1) // (LANES // 2) * SUB + sub
    for e in range(msg_ref.shape[0]):
        tile = jnp.zeros((SUB, LANES), jnp.int32)
        for c in range(2 * SUB):
            tile = jnp.where(place == c, start_ref[e, c], tile)
        msg_ref[e, 2 * SUB : 3 * SUB, :] = jnp.where(place < count_ref[e], tile, -1).astype(F32)


def sift_kernel(x_ref, level_ref, o_ref):
    bands = x_ref.shape[0]
    level = level_ref[...]
    diff = jnp.concatenate([x_ref[d, 0:16, :] - level for d in range(bands)], axis=0)
    columns = []
    for d in range(bands):
        tile = x_ref[d, 16:24, :]
        for k in range(2):
            at = k * (LANES // 2)
            columns.append(jnp.broadcast_to(tile[:, at : at + 1], (SUB, LANES)))
    start = jnp.concatenate(columns, axis=0).astype(jnp.int32)
    rows = bands * 16
    lane = lax.broadcasted_iota(jnp.int32, (rows, LANES), 1)
    owner = lax.broadcasted_iota(jnp.int32, (rows, LANES), 0) // 16
    block = jnp.maximum(start, 0)
    tile_id, offset = block // LANES, block % LANES

    def pick(which):
        place = (which % 2) * SUB + which // 2
        hit = jnp.logical_and(jnp.logical_and(lane // 16 == owner, lane % 16 == place), which < 16)
        return jnp.where(hit, 1.0, 0.0).astype(BF16)

    top, rest = halves(diff)
    last = (diff - top.astype(F32) - rest.astype(F32)).astype(BF16)
    dot = functools.partial(jnp.dot, preferred_element_type=F32)
    here, after = pick(tile_id), pick(tile_id + 1)
    first = dot(here, top) + dot(here, rest) + dot(here, last)
    second = dot(after, top) + dot(after, rest) + dot(after, last)
    joined = jnp.where(lane >= offset, first, second)
    index = (lane + offset) % LANES
    moved = jnp.take_along_axis(joined, index, axis=1)
    moved = jnp.where(start >= 0, moved, 0.0)
    o_ref[...] = moved.reshape(bands, 16, LANES)


PARAMS = pltpu.CompilerParams(vmem_limit_bytes=16 * 2**20)


def near(array):
    return pltpu.with_memory_space_constraint(array, pltpu.VMEM)


def shape(*dims):
    return pltpu.VMEM(dims, F32)


def spaces(*kinds):
    return [pl.BlockSpec(memory_space=pltpu.SMEM if kind == "s" else pltpu.VMEM) for kind in kinds]


def run_first(me, received, first):
    shards = received.shape[0]
    inputs = [near(x) for x in (received, *map(jnp.asarray, first))]
    sent = pl.pallas_call(
        first_kernel,
        out_shape=shape(shards * 32, LANES),
        in_specs=spaces(*"svvv"),
        out_specs=spaces("v")[0],
        scratch_shapes=[pltpu.VMEM((2, SUB, SLOTS, LANES), F32)],
        compiler_params=PARAMS,
    )(me, *inputs)
    return sent.reshape(shards, 32, LANES)


def run_second(me, received, second):
    shards = received.shape[0]
    inputs = [near(x) for x in (received, *map(jnp.asarray, second))]
    return pl.pallas_call(
        second_kernel,
        out_shape=shape(shards, 3 * SUB, LANES),
        in_specs=spaces("s", *"vvvvvv"),
        out_specs=spaces("v")[0],
        scratch_shapes=[
            pltpu.VMEM((2 * SLOTS * SLOTS, LANES), F32),
            pltpu.VMEM((2 * SLOTS * SUB, LANES), F32),
            pltpu.VMEM((3, SLOTS, 2, SUB, LANES), F32),
            pltpu.VMEM((SLOTS * PIECE, 2 * LANES), BF16),
            pltpu.VMEM((SLOTS * PIECE, 2 * LANES), BF16),
            pltpu.VMEM((16 * LANES // 2, LANES), F32),
            pltpu.VMEM((2 * LANES, CHUNKS * LANES), BF16),
            pltpu.VMEM((CHUNKS * LANES, COARSE), BF16),
            pltpu.VMEM((2 * LANES, LANES), F32),
        ],
        compiler_params=PARAMS,
    )(me, *inputs)


def run_third(received, starts, counts):
    bands = counts.shape[0]
    return pl.pallas_call(
        third_kernel,
        out_shape=(
            jax.ShapeDtypeStruct((2, SUB * COARSE), F32),
            shape(bands, 3 * SUB, LANES),
            shape(2 * SUB, LANES),
        ),
        in_specs=spaces(*"ssv"),
        out_specs=spaces(*"vvv"),
        compiler_params=PARAMS,
    )(starts, counts, near(received))


def run_sift(received, level):
    return pl.pallas_call(
        sift_kernel,
        out_shape=jax.ShapeDtypeStruct((received.shape[0], 16, LANES), F32),
        in_specs=spaces(*"vv"),
        out_specs=spaces("v")[0],
        compiler_params=PARAMS,
    )(near(received), near(level))


def per_device(series, cand_start, cand_count):
    shards = lax.axis_size("tm")
    first, second = tables(shards, shards * series.shape[1])
    me, series = lax.optimization_barrier((lax.axis_index("tm").astype(jnp.int32).reshape(1), series))
    swap = functools.partial(lax.all_to_all, split_axis=0, concat_axis=0, tiled=True)
    samples = swap(jnp.swapaxes(series.reshape(2, shards, -1), 0, 1), "tm")
    classes = swap(run_first(me, samples, first), "tm")
    sums = swap(run_second(me, classes, second), "tm")
    harmonic_sum, message, level = run_third(sums, cand_start[0, 0], cand_count[0, 0])
    sifted = run_sift(swap(message, "dm"), level)
    return harmonic_sum, sifted[None, None]


def solution(mesh):
    return jax.shard_map(
        per_device,
        mesh=mesh,
        in_specs=(
            P(("beam", "dm"), "tm"),
            P(("beam", "tm"), "dm", None, None),
            P(("beam", "tm"), "dm", None),
        ),
        out_specs=(P(("beam", "dm"), "tm"), P(("beam", "tm"), "dm", None, None, None)),
        check_vma=False,
    )
```

time: 83.2 us -> 80.4 us (0.966)
  blocking collectives: 76.3 us -> 74.3 us
  local copies, waits for them, and re-layouts: 1.67 us -> 0.7 us
    all_to_all x3, blocking collectives: 64.9 us -> 63.1 us  [the longest x1 35.8 us: per_device(): samples = swap(jnp.swapaxes(series.reshape(2, shards, -1), 0, 1), 'tm')]
    unnamed x22 -> x18, local copies, waits for them, and re-layouts: 1.67 us -> 0.7 us
    pallas_call x5 -> x4, Pallas kernels: 4.24 us -> 4.27 us  [the longest x1 1.46 us: run_second(): pl.pallas_call(second_kernel, out_shape=shape(shards, 3 * SUB, LANES), in...]
where the time goes in v2:
time: 80.4 us; the launch traced here: 80 us
  blocking collectives  74.3 us (92%)
  Pallas kernels  4.27 us (5%)
    all_to_all x1, blocking collectives, per_device(): samples = swap(jnp.swapaxes(series.reshape(2, shards, -1), 0, 1), 'tm')  35.8 us
    all_to_all x1, blocking collectives, per_device(): classes = swap(run_first(me, samples, first), 'tm')  14.2 us
    all_to_all x1, blocking collectives, per_device(): sums = swap(run_second(me, classes, second), 'tm')  13 us
    all_to_all x1, blocking collectives, per_device(): sifted = run_sift(swap(message, 'dm'), level)  11.2 us

profile of v2, /device:TPU:513, one launch (start us, length us, event | category | flops | bytes accessed | tf_op | source)
XLA Modules:
  0.0 80.0 jit_solution(3367902420180629119)
XLA Ops:
  0.6 0.0 copy-start.1
  0.6 0.0 copy-start.2
  0.7 35.8 %all_to_all.20.x_ref = f32[16,2,2048]{2,1,0:T(2,128)S(1)} all-to-all(f32[16,2,2048]{2,1,0:T(2,128)} %bitcast.11), channel_id=1, replica_groups=mesh['beam'=2,'tm'=16,'dm'=8] {'tm'}, dimensions={0} | all-to-all | bytes 524288 | tf_op jit(solution)/shard_map/all_to_all | solution.py:424
  36.5 0.0 copy-done.1
  36.5 0.0 copy-done.2
  36.5 0.0 copy-start.5
  36.5 0.0 copy-start.6
  36.5 0.4 shard_map.113
  36.9 0.0 copy-start
  36.9 0.0 copy-start.3
  36.9 0.0 copy-start.4
  37.0 14.2 %all_to_all.21.x_ref = f32[16,32,128]{2,1,0:T(8,128)S(1)} all-to-all(f32[16,32,128]{2,1,0:T(8,128)S(1)} %bitcast.8), channel_id=1, replica_groups=mesh['beam'=2,'tm'=16,'dm'=8] {'tm'}, dimensions={0} | all-to-all | bytes 524288 | tf_op jit(solution)/shard_map/all_to_all | solution.py:425
  51.2 0.0 copy-done.5
  51.2 0.0 copy-done.6
  51.2 0.0 copy-done
  51.2 0.0 copy-done.3
  51.2 0.0 copy-done.4
  51.2 1.5 %shard_map.114 = f32[16,24,128]{2,1,0:T(8,128)S(1)} custom-call(s32[1]{0:T(128)} %bitcast.2.d_ref, f32[16,32,128]{2,1,0:T(8,128)S(1)} %all_to_all.21.x_ref, f32[2,16,16,128]{3,2,1,0:T(8,128)S(1)} %copy-done, f32[2,8,16,128]{3,2,1,0:T(8,128)S(1)} %copy-done.5, f32[2,16,128]{2,1,0:T(8,128)S(1)} %copy-done.6, bf16[256,256]{1,0:T(8,128)(2,1)S(1)} %copy-done.4, ...), custom_call_target="tpu_custom_call" | custom-call | tf_op jit(solution)/shard_map/pallas_call | solution.py:374
  52.7 0.0 copy-start.7
  52.7 13.0 %all_to_all.22.x_ref = f32[16,24,128]{2,1,0:T(8,128)S(1)} all-to-all(f32[16,24,128]{2,1,0:T(8,128)S(1)} %shard_map.114), channel_id=1, replica_groups=mesh['beam'=2,'tm'=16,'dm'=8] {'tm'}, dimensions={0} | all-to-all | bytes 393216 | tf_op jit(solution)/shard_map/all_to_all | solution.py:426
  65.7 0.0 copy-start.8
  65.7 0.0 copy-done.7
  65.7 0.7 copy-done.8
  66.4 1.3 %shard_map.115 = (f32[2,2048]{1,0:T(2,128)}, f32[8,24,128]{2,1,0:T(8,128)S(1)}, f32[16,128]{1,0:T(8,128)S(1)}) custom-call(s32[8,16]{1,0:T(8,128)S(1)} %bitcast.9, s32[8]{0:T(128)S(1)} %bitcast.10, f32[16,24,128]{2,1,0:T(8,128)S(1)} %all_to_all.22.x_ref), custom_call_target="tpu_custom_call" | custom-call | tf_op jit(solution)/shard_map/pallas_call | solution.py:396
  67.6 11.2 %all_to_all.23.x_ref = f32[8,24,128]{2,1,0:T(8,128)S(1)} all-to-all(f32[8,24,128]{2,1,0:T(8,128)S(1)} %get-tuple-element.10), channel_id=1, replica_groups=mesh['beam'=2,'tm'=16,'dm'=8] {'dm'}, dimensions={0} | all-to-all | bytes 196608 | tf_op jit(solution)/shard_map/all_to_all | solution.py:428
  78.9 1.2 %shard_map.116 = f32[8,16,128]{2,1,0:T(8,128)} custom-call(f32[8,24,128]{2,1,0:T(8,128)S(1)} %all_to_all.23.x_ref, f32[16,128]{1,0:T(8,128)S(1)} %get-tuple-element.11.level_ref), custom_call_target="tpu_custom_call" | custom-call | tf_op jit(solution)/shard_map/pallas_call | solution.py:410
Async XLA Ops:
  0.6 35.9 %copy-start.1 = (f32[16,2,8,128]{3,2,1,0:T(8,128)S(1)}, f32[16,2,8,128]{3,2,1,0:T(8,128)}, u32[]{:S(2)}) copy-start(f32[16,2,8,128]{3,2,1,0:T(8,128)} %constant.21.clone.shift_ref) | copy-start | bytes 393220
  0.6 35.9 %copy-start.2 = (f32[2,8,16,128]{3,2,1,0:T(8,128)S(1)}, f32[2,8,16,128]{3,2,1,0:T(8,128)}, u32[]{:S(2)}) copy-start(f32[2,8,16,128]{3,2,1,0:T(8,128)} %constant.20.clone.within_ref) | copy-start | bytes 393220
  36.5 14.7 %copy-start.5 = (f32[2,8,16,128]{3,2,1,0:T(8,128)S(1)}, f32[2,8,16,128]{3,2,1,0:T(8,128)}, u32[]{:S(2)}) copy-start(f32[2,8,16,128]{3,2,1,0:T(8,128)} %constant.23.clone.middle_ref) | copy-start | bytes 393220
  36.5 14.7 %copy-start.6 = (f32[2,16,128]{2,1,0:T(8,128)S(1)}, f32[2,16,128]{2,1,0:T(8,128)}, u32[]{:S(2)}) copy-start(f32[2,16,128]{2,1,0:T(8,128)} %constant.24.clone.between_ref) | copy-start | bytes 49156
  36.9 14.3 %copy-start = (f32[2,16,16,128]{3,2,1,0:T(8,128)S(1)}, f32[2,16,16,128]{3,2,1,0:T(8,128)}, u32[]{:S(2)}) copy-start(f32[2,16,16,128]{3,2,1,0:T(8,128)} %constant.22.clone.after_ref) | copy-start | bytes 786436
  36.9 14.3 %copy-start.3 = (bf16[256,256]{1,0:T(8,128)(2,1)S(1)}, bf16[256,256]{1,0:T(8,128)(2,1)}, u32[]{:S(2)}) copy-start(bf16[256,256]{1,0:T(8,128)(2,1)} %constant.26.clone.tl_ref) | copy-start | bytes 393220
  36.9 14.3 %copy-start.4 = (bf16[256,256]{1,0:T(8,128)(2,1)S(1)}, bf16[256,256]{1,0:T(8,128)(2,1)}, u32[]{:S(2)}) copy-start(bf16[256,256]{1,0:T(8,128)(2,1)} %constant.25.clone.th_ref) | copy-start | bytes 393220
  52.7 13.0 %copy-start.7 = (s32[1,1,8,16]{3,2,1,0:T(8,128)S(1)}, s32[1,1,8,16]{3,2,1,0:T(8,128)}, u32[]{:S(2)}) copy-start(s32[1,1,8,16]{3,2,1,0:T(8,128)} %param.11) | copy-start | bytes 1540
  65.7 0.7 copy-start.8

commit v3 on v2

--- a/solution.py
+++ b/solution.py
@@ -20,6 +20,7 @@
 PIECE = 32
 PIECES = [(h, c) for h in range(1, HARM + 1) for c in range(h)]
 CHUNKS = len(PIECES) // 4
+ROWS = 2 * SUB + 1
 
 F32 = jnp.float32
 BF16 = jnp.bfloat16
@@ -118,7 +119,15 @@
     return out
 
 
-def first_kernel(d_ref, x_ref, within_ref, shift_ref, o_ref, w_scr):
+def first_kernel(d_ref, x_ref, within_ref, shift_ref, start_ref, count_ref, o_ref, m_ref, w_scr):
+    bands, slots = start_ref.shape
+    cell = [lax.broadcasted_iota(jnp.int32, (bands, bands), axis) for axis in range(2)]
+    counts = jnp.where(cell[0] == cell[1], count_ref[...].astype(F32), 0.0)
+    live = jnp.sum(counts, axis=1, keepdims=True).astype(jnp.int32)
+    slot = lax.broadcasted_iota(jnp.int32, (bands, slots), 1)
+    starts = jnp.where(slot < live, start_ref[...], -1).astype(F32)
+    m_ref[...] = jnp.concatenate([starts] * (LANES // slots), axis=1)
+
     shards = x_ref.shape[0]
     me = d_ref[0]
     tiles = x_ref.shape[2] // LANES
@@ -224,9 +233,9 @@
     mean = over_all(powers[0] + powers[1]) / count
     off0, off1 = powers[0] - mean, powers[1] - mean
     deviation = over_all(off0 * off0 + off1 * off1)
-    stats = jnp.where(sub == 0, mean, deviation)
+    stats = jnp.where(sub[0:1] + lax.broadcasted_iota(jnp.int32, (1, LANES), 1) < half, mean, deviation)
     for t in range(shards):
-        o_ref[t, 2 * SUB : 3 * SUB, :] = stats
+        o_ref[t * ROWS + 2 * SUB : (t + 1) * ROWS, :] = stats
 
     for group in range(4):
         value = powers[group // 2][:, (group % 2) * LANES : (group % 2 + 1) * LANES]
@@ -267,22 +276,25 @@
     for t in range(shards):
         for tile in range(2):
             rows = pl.ds(tile * LANES + (t % 2) * half + t // 2, SUB, stride=SUB)
-            o_ref[t, tile * SUB : (tile + 1) * SUB, :] = h_scr[rows, :]
-
-
-def third_kernel(start_ref, count_ref, x_ref, hs_ref, msg_ref, level_ref):
-    shards = x_ref.shape[0]
+            o_ref[t * ROWS + tile * SUB : t * ROWS + (tile + 1) * SUB, :] = h_scr[rows, :]
+
+
+def third_kernel(m_ref, x_ref, hs_ref, msg_ref, level_ref):
+    shards = x_ref.shape[0] // ROWS
     holders = shards // 2
     count = 2 * SLOTS * (LANES // 2) * SLOTS
     tiles = []
     for row in range(2):
-        total = x_ref[row]
+        blocks = [(2 * r + row) * ROWS for r in range(holders)]
+        sums = [x_ref[at : at + 2 * SUB, :] for at in blocks]
+        stats = [x_ref[at + 2 * SUB : at + ROWS, :] for at in blocks]
+        total, both = sums[0], stats[0]
         for r in range(1, holders):
-            total = total + x_ref[2 * r + row]
-        mean = total[2 * SUB : 2 * SUB + 1] / holders
-        spread = total[2 * SUB + 1 : 2 * SUB + 2]
+            total, both = total + sums[r], both + stats[r]
+        mean = both[:, 0:1] / holders
+        spread = both[:, LANES // 2 : LANES // 2 + 1]
         for r in range(holders):
-            off = x_ref[2 * r + row, 2 * SUB : 2 * SUB + 1, :] - mean
+            off = stats[r][:, 0:1] - mean
             spread = spread + count * (off * off)
         scale = 1.0 / jnp.sqrt(spread / (count * holders) + EPSILON)
         tiles.append([(total[k * SUB : (k + 1) * SUB] - HARM * mean) * scale for k in range(2)])
@@ -292,51 +304,38 @@
                 hs_ref[row : row + 1, pl.ds(g * COARSE + k * LANES, LANES)] = tiles[row][k][g : g + 1]
     for k in range(2):
         level_ref[k * SUB : (k + 1) * SUB, :] = (tiles[0][k] + tiles[1][k]) / 2
-        peak = jnp.maximum(tiles[0][k], tiles[1][k])
-        for e in range(msg_ref.shape[0]):
-            msg_ref[e, k * SUB : (k + 1) * SUB, :] = peak
-    sub = lax.broadcasted_iota(jnp.int32, (SUB, LANES), 0)
-    place = lax.broadcasted_iota(jnp.int32, (SUB, LANES), 1) // (LANES // 2) * SUB + sub
-    for e in range(msg_ref.shape[0]):
-        tile = jnp.zeros((SUB, LANES), jnp.int32)
-        for c in range(2 * SUB):
-            tile = jnp.where(place == c, start_ref[e, c], tile)
-        msg_ref[e, 2 * SUB : 3 * SUB, :] = jnp.where(place < count_ref[e], tile, -1).astype(F32)
-
-
-def sift_kernel(x_ref, level_ref, o_ref):
-    bands = x_ref.shape[0]
+    peak = jnp.concatenate([jnp.maximum(tiles[0][k], tiles[1][k]) for k in range(2)], axis=0)
+    for e in range(m_ref.shape[0]):
+        msg_ref[e * ROWS : e * ROWS + 2 * SUB, :] = peak
+        msg_ref[e * ROWS + 2 * SUB : (e + 1) * ROWS, :] = m_ref[e : e + 1, :]
+
+
+def sift_kernel(x_ref, level_ref, bins_ref, o_ref, hs_ref):
+    hs_ref[...] = bins_ref[...]
+    bands, slots = o_ref.shape[:2]
     level = level_ref[...]
-    diff = jnp.concatenate([x_ref[d, 0:16, :] - level for d in range(bands)], axis=0)
-    columns = []
-    for d in range(bands):
-        tile = x_ref[d, 16:24, :]
-        for k in range(2):
-            at = k * (LANES // 2)
-            columns.append(jnp.broadcast_to(tile[:, at : at + 1], (SUB, LANES)))
-    start = jnp.concatenate(columns, axis=0).astype(jnp.int32)
-    rows = bands * 16
+    rows = bands * slots
+    diff = jnp.concatenate([x_ref[d * ROWS : d * ROWS + 2 * SUB, :] - level for d in range(bands)], axis=0)
     lane = lax.broadcasted_iota(jnp.int32, (rows, LANES), 1)
-    owner = lax.broadcasted_iota(jnp.int32, (rows, LANES), 0) // 16
+    line = lax.broadcasted_iota(jnp.int32, (rows, LANES), 0)
+    listed = [x_ref[d * ROWS + 2 * SUB : (d + 1) * ROWS, :] for d in range(bands)]
+    listed = jnp.concatenate([jnp.broadcast_to(x, (slots, LANES)) for x in listed], axis=0)
+    start = jnp.sum(jnp.where(lane == line % slots, listed, 0.0), axis=1, keepdims=True).astype(jnp.int32)
     block = jnp.maximum(start, 0)
     tile_id, offset = block // LANES, block % LANES
 
     def pick(which):
-        place = (which % 2) * SUB + which // 2
-        hit = jnp.logical_and(jnp.logical_and(lane // 16 == owner, lane % 16 == place), which < 16)
+        place = (line // slots) * (2 * SUB) + (which % 2) * SUB + which // 2
+        hit = jnp.logical_and(lane == place, which < 2 * SUB)
         return jnp.where(hit, 1.0, 0.0).astype(BF16)
 
-    top, rest = halves(diff)
-    last = (diff - top.astype(F32) - rest.astype(F32)).astype(BF16)
-    dot = functools.partial(jnp.dot, preferred_element_type=F32)
-    here, after = pick(tile_id), pick(tile_id + 1)
-    first = dot(here, top) + dot(here, rest) + dot(here, last)
-    second = dot(after, top) + dot(after, rest) + dot(after, last)
-    joined = jnp.where(lane >= offset, first, second)
-    index = (lane + offset) % LANES
-    moved = jnp.take_along_axis(joined, index, axis=1)
+    both = jnp.concatenate([pick(tile_id), pick(tile_id + 1)], axis=0)
+    parts = jnp.dot(both, jnp.concatenate(halves(diff), axis=1), preferred_element_type=F32)
+    parts = parts[:, :LANES] + parts[:, LANES:]
+    joined = jnp.where(lane >= offset, parts[:rows], parts[rows:])
+    moved = jnp.take_along_axis(joined, (lane + offset) % LANES, axis=1)
     moved = jnp.where(start >= 0, moved, 0.0)
-    o_ref[...] = moved.reshape(bands, 16, LANES)
+    o_ref[...] = moved.reshape(bands, slots, LANES)
 
 
 PARAMS = pltpu.CompilerParams(vmem_limit_bytes=16 * 2**20)
@@ -354,26 +353,26 @@
     return [pl.BlockSpec(memory_space=pltpu.SMEM if kind == "s" else pltpu.VMEM) for kind in kinds]
 
 
-def run_first(me, received, first):
+def run_first(me, received, first, starts, counts):
     shards = received.shape[0]
-    inputs = [near(x) for x in (received, *map(jnp.asarray, first))]
-    sent = pl.pallas_call(
+    inputs = [near(x) for x in (received, *map(jnp.asarray, first), starts, counts)]
+    sent, markers = pl.pallas_call(
         first_kernel,
-        out_shape=shape(shards * 32, LANES),
-        in_specs=spaces(*"svvv"),
-        out_specs=spaces("v")[0],
+        out_shape=(shape(shards * 32, LANES), shape(starts.shape[0], LANES)),
+        in_specs=spaces("s", *"vvvvv"),
+        out_specs=spaces(*"vv"),
         scratch_shapes=[pltpu.VMEM((2, SUB, SLOTS, LANES), F32)],
         compiler_params=PARAMS,
     )(me, *inputs)
-    return sent.reshape(shards, 32, LANES)
+    return sent.reshape(shards, 32, LANES), markers
 
 
 def run_second(me, received, second):
     shards = received.shape[0]
     inputs = [near(x) for x in (received, *map(jnp.asarray, second))]
-    return pl.pallas_call(
+    sent = pl.pallas_call(
         second_kernel,
-        out_shape=shape(shards, 3 * SUB, LANES),
+        out_shape=shape(shards * ROWS, LANES),
         in_specs=spaces("s", *"vvvvvv"),
         out_specs=spaces("v")[0],
         scratch_shapes=[
@@ -389,31 +388,33 @@
         ],
         compiler_params=PARAMS,
     )(me, *inputs)
-
-
-def run_third(received, starts, counts):
-    bands = counts.shape[0]
-    return pl.pallas_call(
+    return sent.reshape(shards, 1, ROWS * LANES)
+
+
+def run_third(received, markers):
+    bands = markers.shape[0]
+    bins, message, level = pl.pallas_call(
         third_kernel,
-        out_shape=(
-            jax.ShapeDtypeStruct((2, SUB * COARSE), F32),
-            shape(bands, 3 * SUB, LANES),
-            shape(2 * SUB, LANES),
-        ),
-        in_specs=spaces(*"ssv"),
+        out_shape=(shape(2, SUB * COARSE), shape(bands * ROWS, LANES), shape(2 * SUB, LANES)),
+        in_specs=spaces(*"vv"),
         out_specs=spaces(*"vvv"),
         compiler_params=PARAMS,
-    )(starts, counts, near(received))
-
-
-def run_sift(received, level):
+    )(near(markers), near(received.reshape(-1, LANES)))
+    return bins, message.reshape(bands, 1, ROWS * LANES), level
+
+
+def run_sift(received, level, bins):
+    bands = received.shape[0]
     return pl.pallas_call(
         sift_kernel,
-        out_shape=jax.ShapeDtypeStruct((received.shape[0], 16, LANES), F32),
-        in_specs=spaces(*"vv"),
-        out_specs=spaces("v")[0],
+        out_shape=(
+            jax.ShapeDtypeStruct((bands, 2 * SUB, LANES), F32),
+            jax.ShapeDtypeStruct(bins.shape, F32),
+        ),
+        in_specs=spaces(*"vvv"),
+        out_specs=spaces(*"vv"),
         compiler_params=PARAMS,
-    )(near(received), near(level))
+    )(near(received.reshape(-1, LANES)), near(level), near(bins))
 
 
 def per_device(series, cand_start, cand_count):
@@ -422,10 +423,10 @@
     me, series = lax.optimization_barrier((lax.axis_index("tm").astype(jnp.int32).reshape(1), series))
     swap = functools.partial(lax.all_to_all, split_axis=0, concat_axis=0, tiled=True)
     samples = swap(jnp.swapaxes(series.reshape(2, shards, -1), 0, 1), "tm")
-    classes = swap(run_first(me, samples, first), "tm")
-    sums = swap(run_second(me, classes, second), "tm")
-    harmonic_sum, message, level = run_third(sums, cand_start[0, 0], cand_count[0, 0])
-    sifted = run_sift(swap(message, "dm"), level)
+    sent, markers = run_first(me, samples, first, cand_start[0, 0], cand_count[0])
+    sums = swap(run_second(me, swap(sent, "tm"), second), "tm")
+    bins, message, level = run_third(sums, markers)
+    sifted, harmonic_sum = run_sift(swap(message, "dm"), level, bins)
     return harmonic_sum, sifted[None, None]
 
 

time: 80.4 us -> 77.2 us (0.960)
  blocking collectives: 74.3 us -> 72.2 us
  Pallas kernels: 4.27 us -> 3.23 us
    all_to_all x3, blocking collectives: 38.5 us -> 36.4 us  [the longest x2 26.1 us: per_device(): sums = swap(run_second(me, swap(sent, 'tm'), second), 'tm')]
    pallas_call x4, Pallas kernels: 4.27 us -> 3.23 us  [the longest x1 1.46 us: run_second(): pl.pallas_call(second_kernel, out_shape=shape(shards * ROWS, LANES), in_s...]
where the time goes in v3:
time: 77.2 us; the launch traced here: 76.9 us
  blocking collectives  72.2 us (94%)
  Pallas kernels  3.23 us (4%)
    all_to_all x1, blocking collectives, per_device(): samples = swap(jnp.swapaxes(series.reshape(2, shards, -1), 0, 1), 'tm')  35.8 us
    all_to_all x2, blocking collectives, per_device(): sums = swap(run_second(me, swap(sent, 'tm'), second), 'tm')  26.1 us
    all_to_all x1, blocking collectives, per_device(): sifted, harmonic_sum = run_sift(swap(message, 'dm'), level, bins)  10.3 us

profile of v3, /device:TPU:513, one launch (start us, length us, event | category | flops | bytes accessed | tf_op | source)
XLA Modules:
  0.0 76.9 jit_solution(4620909448860672338)
XLA Ops:
  0.6 0.0 copy-start.1
  0.6 0.0 copy-start.2
  0.7 0.0 copy-start.7
  0.7 35.8 %all_to_all.20.x_ref = f32[16,2,2048]{2,1,0:T(2,128)S(1)} all-to-all(f32[16,2,2048]{2,1,0:T(2,128)} %bitcast.19), channel_id=1, replica_groups=mesh['beam'=2,'tm'=16,'dm'=8] {'tm'}, dimensions={0} | all-to-all | bytes 524288 | tf_op jit(solution)/shard_map/all_to_all | solution.py:425
  36.5 0.0 copy-start.8
  36.5 0.0 copy-done.1
  36.5 0.0 copy-done.2
  36.5 0.0 copy-done.7
  36.5 0.6 copy-done.8
  37.2 0.0 copy-start.5
  37.2 0.0 copy-start.6
  37.2 0.5 shard_map.113
  37.6 0.0 copy-start
  37.6 0.0 copy-start.3
  37.7 0.0 copy-start.4
  37.7 14.2 %all_to_all.21.x_ref = f32[16,32,128]{2,1,0:T(8,128)S(1)} all-to-all(f32[16,32,128]{2,1,0:T(8,128)S(1)} %bitcast.15), channel_id=1, replica_groups=mesh['beam'=2,'tm'=16,'dm'=8] {'tm'}, dimensions={0} | all-to-all | bytes 524288 | tf_op jit(solution)/shard_map/all_to_all | solution.py:427
  51.9 0.0 copy-done.5
  51.9 0.0 copy-done.6
  51.9 0.0 copy-done
  51.9 0.0 copy-done.3
  51.9 0.0 copy-done.4
  51.9 1.5 %shard_map.114 = f32[272,128]{1,0:T(8,128)S(1)} custom-call(s32[1]{0:T(128)} %bitcast.d_ref, f32[16,32,128]{2,1,0:T(8,128)S(1)} %all_to_all.21.x_ref, f32[2,16,16,128]{3,2,1,0:T(8,128)S(1)} %copy-done, f32[2,8,16,128]{3,2,1,0:T(8,128)S(1)} %copy-done.5, f32[2,16,128]{2,1,0:T(8,128)S(1)} %copy-done.6, bf16[256,256]{1,0:T(8,128)(2,1)S(1)} %copy-done.4, ...), custom_call_target="tpu_custom_call" | custom-call | tf_op jit(solution)/shard_map/pallas_call | solution.py:373
  53.4 11.9 %all_to_all.22 = f32[16,1,2176]{2,1,0:T(1,128)S(1)} all-to-all(f32[16,1,2176]{2,1,0:T(1,128)S(1)} %bitcast.13), channel_id=1, replica_groups=mesh['beam'=2,'tm'=16,'dm'=8] {'tm'}, dimensions={0} | all-to-all | bytes 278528 | tf_op jit(solution)/shard_map/all_to_all | solution.py:427
  65.3 0.2 shard_map.115
  65.5 10.3 %all_to_all.23 = f32[8,1,2176]{2,1,0:T(1,128)S(1)} all-to-all(f32[8,1,2176]{2,1,0:T(1,128)S(1)} %bitcast.16), channel_id=1, replica_groups=mesh['beam'=2,'tm'=16,'dm'=8] {'dm'}, dimensions={0} | all-to-all | bytes 139264 | tf_op jit(solution)/shard_map/all_to_all | solution.py:429
  75.8 1.1 %shard_map.116 = (f32[8,16,128]{2,1,0:T(8,128)}, f32[2,2048]{1,0:T(2,128)}) custom-call(f32[136,128]{1,0:T(8,128)S(1)} %bitcast.14, f32[16,128]{1,0:T(8,128)S(1)} %get-tuple-element.16.level_ref, f32[2,2048]{1,0:T(2,128)S(1)} %get-tuple-element.17.bins_ref), custom_call_target="tpu_custom_call" | custom-call | tf_op jit(solution)/shard_map/pallas_call | solution.py:408
Async XLA Ops:
  0.6 35.9 %copy-start.1 = (f32[16,2,8,128]{3,2,1,0:T(8,128)S(1)}, f32[16,2,8,128]{3,2,1,0:T(8,128)}, u32[]{:S(2)}) copy-start(f32[16,2,8,128]{3,2,1,0:T(8,128)} %constant.21.clone.shift_ref) | copy-start | bytes 393220
  0.6 35.9 %copy-start.2 = (f32[2,8,16,128]{3,2,1,0:T(8,128)S(1)}, f32[2,8,16,128]{3,2,1,0:T(8,128)}, u32[]{:S(2)}) copy-start(f32[2,8,16,128]{3,2,1,0:T(8,128)} %constant.20.clone.within_ref) | copy-start | bytes 393220
  0.7 35.9 %copy-start.7 = (s32[1,1,8,16]{3,2,1,0:T(8,128)S(1)}, s32[1,1,8,16]{3,2,1,0:T(8,128)}, u32[]{:S(2)}) copy-start(s32[1,1,8,16]{3,2,1,0:T(8,128)} %param.11) | copy-start | bytes 1540
  36.5 0.7 copy-start.8
  37.2 14.7 %copy-start.5 = (f32[2,8,16,128]{3,2,1,0:T(8,128)S(1)}, f32[2,8,16,128]{3,2,1,0:T(8,128)}, u32[]{:S(2)}) copy-start(f32[2,8,16,128]{3,2,1,0:T(8,128)} %constant.23.clone.middle_ref) | copy-start | bytes 393220
  37.2 14.7 %copy-start.6 = (f32[2,16,128]{2,1,0:T(8,128)S(1)}, f32[2,16,128]{2,1,0:T(8,128)}, u32[]{:S(2)}) copy-start(f32[2,16,128]{2,1,0:T(8,128)} %constant.24.clone.between_ref) | copy-start | bytes 49156
  37.6 14.3 %copy-start = (f32[2,16,16,128]{3,2,1,0:T(8,128)S(1)}, f32[2,16,16,128]{3,2,1,0:T(8,128)}, u32[]{:S(2)}) copy-start(f32[2,16,16,128]{3,2,1,0:T(8,128)} %constant.22.clone.after_ref) | copy-start | bytes 786436
  37.6 14.3 %copy-start.3 = (bf16[256,256]{1,0:T(8,128)(2,1)S(1)}, bf16[256,256]{1,0:T(8,128)(2,1)}, u32[]{:S(2)}) copy-start(bf16[256,256]{1,0:T(8,128)(2,1)} %constant.26.clone.tl_ref) | copy-start | bytes 393220
  37.7 14.3 %copy-start.4 = (bf16[256,256]{1,0:T(8,128)(2,1)S(1)}, bf16[256,256]{1,0:T(8,128)(2,1)}, u32[]{:S(2)}) copy-start(bf16[256,256]{1,0:T(8,128)(2,1)} %constant.25.clone.th_ref) | copy-start | bytes 393220

commit v4 on v3

--- a/solution.py
+++ b/solution.py
@@ -119,7 +119,25 @@
     return out
 
 
-def first_kernel(d_ref, x_ref, within_ref, shift_ref, start_ref, count_ref, o_ref, m_ref, w_scr):
+def prepare_kernel(d_ref, within_ref, shift_ref, start_ref, count_ref, w_ref, s_ref, m_ref):
+    me = d_ref[0]
+    own_class = me // 2
+    for r in range(1, w_ref.shape[1]):
+        own = [shift_ref[me, part, r : r + 1, :] for part in range(2)]
+        twiddle = cmul((within_ref[0, r], within_ref[1, r]), own)
+        for part in range(2):
+            w_ref[part, r] = twiddle[part]
+
+    phi = lax.broadcasted_iota(jnp.int32, (SLOTS, COARSE), 1)
+    slot = lax.broadcasted_iota(jnp.int32, (SLOTS, COARSE), 0)
+    pairs = slot * SLOTS - jnp.where(slot < SUB, 0, SUB * SLOTS - SUB)
+    mine = jnp.where(own_class == 0, pairs, own_class + SLOTS * slot)
+    mirror = jnp.where(mine == 0, COARSE // 2, COARSE - mine)
+    for index, (h, c) in enumerate(PIECES):
+        for k, residue in enumerate((mine, mirror)):
+            hit = jnp.where(h * phi - COARSE * c == residue, 1.0, 0.0)
+            s_ref[pl.ds(index * PIECE + k * SLOTS, SLOTS), :] = hit.astype(BF16)
+
     bands, slots = start_ref.shape
     cell = [lax.broadcasted_iota(jnp.int32, (bands, bands), axis) for axis in range(2)]
     counts = jnp.where(cell[0] == cell[1], count_ref[...].astype(F32), 0.0)
@@ -128,29 +146,28 @@
     starts = jnp.where(slot < live, start_ref[...], -1).astype(F32)
     m_ref[...] = jnp.concatenate([starts] * (LANES // slots), axis=1)
 
+
+def first_kernel(x_ref, w_ref, o_ref):
     shards = x_ref.shape[0]
-    me = d_ref[0]
-    tiles = x_ref.shape[2] // LANES
+    tiles = x_ref.shape[1] // 2
+    flat = x_ref.reshape(shards * 2 * tiles, LANES)
     half = shards // 2
-    for r in range(1, half):
-        own = [shift_ref[me, part, r : r + 1, :] for part in range(2)]
-        twiddle = cmul((within_ref[0, r], within_ref[1, r]), own)
-        for part in range(2):
-            w_scr[part, r] = twiddle[part]
-    for u in range(tiles):
-        values = [(x_ref[t, :, u * LANES : (u + 1) * LANES], None) for t in range(shards)]
-        classes = sixteen(values)
-        for r in range(half):
-            if r:
-                value = cmul(classes[r], [w_scr[part, r, u : u + 1, :] for part in range(2)])
-            else:
-                value = classes[0][0], classes[half][0]
-            for part in range(2):
-                at = r * 4 * tiles + part * tiles + u
-                o_ref[pl.ds(at, 2, stride=2 * tiles), :] = value[part]
-
-
-def second_kernel(d_ref, x_ref, after_ref, middle_ref, between_ref, th_ref, tl_ref, o_ref, v_scr, x_scr, t_scr, dh_scr, dl_scr, r_scr, l_scr, s_scr, h_scr):
+    for row in range(2):
+        for k in range(tiles // SUB):
+            inner = slice(k * SUB, (k + 1) * SUB)
+            at = [(t * tiles + k * SUB) * 2 + row for t in range(shards)]
+            classes = sixteen([(flat[pl.ds(x, SUB, stride=2), :], None) for x in at])
+            for r in range(half):
+                if r:
+                    value = cmul(classes[r], [w_ref[part, r, inner, :] for part in range(2)])
+                else:
+                    value = classes[0][0], classes[half][0]
+                for part in range(2):
+                    to = part * tiles + k * SUB
+                    o_ref[2 * r + row, to : to + SUB, :] = value[part]
+
+
+def second_kernel(d_ref, x_ref, after_ref, middle_ref, between_ref, th_ref, tl_ref, s_ref, o_ref, v_scr, x_scr, t_scr, dh_scr, dl_scr, r_scr, l_scr, h_scr):
     shards = x_ref.shape[0]
     tiles = x_ref.shape[1] // 2
     half = LANES // 2
@@ -260,16 +277,7 @@
             cols = pl.ds(chunk * LANES, LANES)
             l_scr[pl.ds(g_pair * 16, 16), cols] = top
             l_scr[pl.ds(LANES + g_pair * 16, 16), cols] = rest
-    phi = lax.broadcasted_iota(jnp.int32, (SLOTS, COARSE), 1)
-    slot = lax.broadcasted_iota(jnp.int32, (SLOTS, COARSE), 0)
-    pairs = slot * SLOTS - jnp.where(slot < SUB, 0, SUB * SLOTS - SUB)
-    mine = jnp.where(is_first, pairs, own_class + SLOTS * slot)
-    mirror = jnp.where(mine == 0, COARSE // 2, COARSE - mine)
-    for index, (h, c) in enumerate(PIECES):
-        for k, residue in enumerate((mine, mirror)):
-            hit = jnp.where(h * phi - COARSE * c == residue, 1.0, 0.0)
-            s_scr[pl.ds(index * PIECE + k * SLOTS, SLOTS), :] = hit.astype(BF16)
-    both = jnp.dot(l_scr[...], s_scr[...], preferred_element_type=F32)
+    both = jnp.dot(l_scr[...], s_ref[...], preferred_element_type=F32)
     for tile in range(2):
         cols = slice(tile * LANES, (tile + 1) * LANES)
         h_scr[tile * LANES : (tile + 1) * LANES, :] = both[:LANES, cols] + both[LANES:, cols]
@@ -310,8 +318,10 @@
         msg_ref[e * ROWS + 2 * SUB : (e + 1) * ROWS, :] = m_ref[e : e + 1, :]
 
 
-def sift_kernel(x_ref, level_ref, bins_ref, o_ref, hs_ref):
-    hs_ref[...] = bins_ref[...]
+def sift_kernel(x_ref, level_ref, bins_ref, o_ref, hs_ref, out_scr, sems):
+    steps = sems.shape[0] - 1
+    bins_out = pltpu.make_async_copy(bins_ref, hs_ref, sems.at[steps])
+    bins_out.start()
     bands, slots = o_ref.shape[:2]
     level = level_ref[...]
     rows = bands * slots
@@ -320,22 +330,32 @@
     line = lax.broadcasted_iota(jnp.int32, (rows, LANES), 0)
     listed = [x_ref[d * ROWS + 2 * SUB : (d + 1) * ROWS, :] for d in range(bands)]
     listed = jnp.concatenate([jnp.broadcast_to(x, (slots, LANES)) for x in listed], axis=0)
-    start = jnp.sum(jnp.where(lane == line % slots, listed, 0.0), axis=1, keepdims=True).astype(jnp.int32)
+    start = jnp.sum(jnp.where(lane == line & (slots - 1), listed, 0.0), axis=1, keepdims=True)
+    start = jnp.broadcast_to(start, (rows, LANES)).astype(jnp.int32)
     block = jnp.maximum(start, 0)
-    tile_id, offset = block // LANES, block % LANES
+    tile_id, offset = block >> 7, block & (LANES - 1)
+    band = line & -slots
 
     def pick(which):
-        place = (line // slots) * (2 * SUB) + (which % 2) * SUB + which // 2
-        hit = jnp.logical_and(lane == place, which < 2 * SUB)
-        return jnp.where(hit, 1.0, 0.0).astype(BF16)
+        place = band + ((which & 1) << 3) + (which >> 1)
+        return jnp.where(lane == place, 1.0, 0.0).astype(BF16)
 
     both = jnp.concatenate([pick(tile_id), pick(tile_id + 1)], axis=0)
     parts = jnp.dot(both, jnp.concatenate(halves(diff), axis=1), preferred_element_type=F32)
     parts = parts[:, :LANES] + parts[:, LANES:]
-    joined = jnp.where(lane >= offset, parts[:rows], parts[rows:])
-    moved = jnp.take_along_axis(joined, (lane + offset) % LANES, axis=1)
-    moved = jnp.where(start >= 0, moved, 0.0)
-    o_ref[...] = moved.reshape(bands, slots, LANES)
+    copies = []
+    for step in range(steps):
+        part = slice(step * rows // steps, (step + 1) * rows // steps)
+        joined = jnp.where(lane[part] >= offset[part], parts[:rows][part], parts[rows:][part])
+        moved = jnp.take_along_axis(joined, (lane[part] + offset[part]) & (LANES - 1), axis=1)
+        moved = jnp.where(start[part] >= 0, moved, 0.0)
+        here = pl.ds(step * bands // steps, bands // steps)
+        out_scr[here] = moved.reshape(bands // steps, slots, LANES)
+        copies.append(pltpu.make_async_copy(out_scr.at[here], o_ref.at[here], sems.at[step]))
+        copies[-1].start()
+    for copy in copies:
+        copy.wait()
+    bins_out.wait()
 
 
 PARAMS = pltpu.CompilerParams(vmem_limit_bytes=16 * 2**20)
@@ -353,27 +373,38 @@
     return [pl.BlockSpec(memory_space=pltpu.SMEM if kind == "s" else pltpu.VMEM) for kind in kinds]
 
 
-def run_first(me, received, first, starts, counts):
+def run_prepare(me, first, starts, counts):
+    within, shift = map(jnp.asarray, first)
+    return pl.pallas_call(
+        prepare_kernel,
+        out_shape=(
+            shape(*within.shape),
+            pltpu.VMEM((CHUNKS * LANES, COARSE), BF16),
+            shape(starts.shape[0], LANES),
+        ),
+        in_specs=spaces("s", *"vvvv"),
+        out_specs=spaces(*"vvv"),
+        compiler_params=PARAMS,
+    )(me, *[near(x) for x in (within, shift, starts, counts)])
+
+
+def run_first(received, twiddles):
+    return pl.pallas_call(
+        first_kernel,
+        out_shape=shape(*received.shape),
+        in_specs=spaces(*"vv"),
+        out_specs=spaces("v")[0],
+        compiler_params=PARAMS,
+    )(near(received), near(twiddles))
+
+
+def run_second(me, received, second, mapping):
     shards = received.shape[0]
-    inputs = [near(x) for x in (received, *map(jnp.asarray, first), starts, counts)]
-    sent, markers = pl.pallas_call(
-        first_kernel,
-        out_shape=(shape(shards * 32, LANES), shape(starts.shape[0], LANES)),
-        in_specs=spaces("s", *"vvvvv"),
-        out_specs=spaces(*"vv"),
-        scratch_shapes=[pltpu.VMEM((2, SUB, SLOTS, LANES), F32)],
-        compiler_params=PARAMS,
-    )(me, *inputs)
-    return sent.reshape(shards, 32, LANES), markers
-
-
-def run_second(me, received, second):
-    shards = received.shape[0]
-    inputs = [near(x) for x in (received, *map(jnp.asarray, second))]
+    inputs = [near(x) for x in (received, *map(jnp.asarray, second), mapping)]
     sent = pl.pallas_call(
         second_kernel,
         out_shape=shape(shards * ROWS, LANES),
-        in_specs=spaces("s", *"vvvvvv"),
+        in_specs=spaces("s", *"vvvvvvv"),
         out_specs=spaces("v")[0],
         scratch_shapes=[
             pltpu.VMEM((2 * SLOTS * SLOTS, LANES), F32),
@@ -383,7 +414,6 @@
             pltpu.VMEM((SLOTS * PIECE, 2 * LANES), BF16),
             pltpu.VMEM((16 * LANES // 2, LANES), F32),
             pltpu.VMEM((2 * LANES, CHUNKS * LANES), BF16),
-            pltpu.VMEM((CHUNKS * LANES, COARSE), BF16),
             pltpu.VMEM((2 * LANES, LANES), F32),
         ],
         compiler_params=PARAMS,
@@ -405,6 +435,8 @@
 
 def run_sift(received, level, bins):
     bands = received.shape[0]
+    steps = bands // 2
+    anywhere = pl.BlockSpec(memory_space=pl.ANY)
     return pl.pallas_call(
         sift_kernel,
         out_shape=(
@@ -412,7 +444,11 @@
             jax.ShapeDtypeStruct(bins.shape, F32),
         ),
         in_specs=spaces(*"vvv"),
-        out_specs=spaces(*"vv"),
+        out_specs=[anywhere, anywhere],
+        scratch_shapes=[
+            pltpu.VMEM((bands, 2 * SUB, LANES), F32),
+            pltpu.SemaphoreType.DMA((steps + 1,)),
+        ],
         compiler_params=PARAMS,
     )(near(received.reshape(-1, LANES)), near(level), near(bins))
 
@@ -420,11 +456,13 @@
 def per_device(series, cand_start, cand_count):
     shards = lax.axis_size("tm")
     first, second = tables(shards, shards * series.shape[1])
-    me, series = lax.optimization_barrier((lax.axis_index("tm").astype(jnp.int32).reshape(1), series))
+    me = lax.axis_index("tm").astype(jnp.int32).reshape(1)
     swap = functools.partial(lax.all_to_all, split_axis=0, concat_axis=0, tiled=True)
-    samples = swap(jnp.swapaxes(series.reshape(2, shards, -1), 0, 1), "tm")
-    sent, markers = run_first(me, samples, first, cand_start[0, 0], cand_count[0])
-    sums = swap(run_second(me, swap(sent, "tm"), second), "tm")
+    blocks = series.reshape(2, shards, -1, LANES).transpose(1, 2, 0, 3).reshape(shards, -1, LANES)
+    samples = swap(blocks, "tm")
+    twiddles, mapping, markers = run_prepare(me, first, cand_start[0, 0], cand_count[0])
+    classes = swap(run_first(samples, twiddles), "tm")
+    sums = swap(run_second(me, classes, second, mapping), "tm")
     bins, message, level = run_third(sums, markers)
     sifted, harmonic_sum = run_sift(swap(message, "dm"), level, bins)
     return harmonic_sum, sifted[None, None]

time: 77.2 us -> 76.1 us (0.986)
  blocking collectives: 72.2 us -> 36.4 us
  starting transfers between devices: 0 us -> 23.9 us
  waiting for transfers between devices: 0 us -> 11.1 us
    all_to_all x3 -> x2, blocking collectives: 61.9 us -> 26.1 us  [the longest x1 14.2 us: per_device(): classes = swap(run_first(samples, twiddles), 'tm')]
    all_to_all x0 -> x1, starting transfers between devices: none -> 23.9 us  [per_device(): samples = swap(blocks, 'tm')]
    all_to_all x0 -> x1, waiting for transfers between devices: none -> 11.1 us  [per_device(): samples = swap(blocks, 'tm')]
  transfers between devices with their start and end apart: 0 -> 1, of which waited for: 0 -> 1; matrix products, arithmetic and copies ran while one was open for 0% -> 0% of each run, Pallas kernels for 0% -> 0%
where the time goes in v4:
time: 76.1 us; the launch traced here: 75.8 us
  blocking collectives  36.4 us (48%)
  starting transfers between devices  23.9 us (31%)
  waiting for transfers between devices  11.1 us (15%)
  Pallas kernels  2.96 us (4%)
    all_to_all x1, starting transfers between devices, per_device(): samples = swap(blocks, 'tm')  23.9 us
    all_to_all x1, blocking collectives, per_device(): classes = swap(run_first(samples, twiddles), 'tm')  14.2 us
    all_to_all x1, blocking collectives, per_device(): sums = swap(run_second(me, classes, second, mapping), 'tm')  11.9 us
    all_to_all x1, waiting for transfers between devices, per_device(): samples = swap(blocks, 'tm')  11.1 us
    all_to_all x1, blocking collectives, per_device(): sifted, harmonic_sum = run_sift(swap(message, 'dm'), level, bins)  10.3 us
  transfers between devices with their start and end apart: 1, of which 1 were waited for; matrix products, arithmetic and copies ran while one was open for 0% of the time, Pallas kernels for 0%

profile of v4, /device:TPU:513, one launch (start us, length us, event | category | flops | bytes accessed | tf_op | source)
XLA Modules:
  0.0 75.8 jit_solution(5253161916937313563)
XLA Ops:
  0.6 0.0 copy-start.4
  0.6 0.0 copy-start.5
  0.7 23.9 %all-to-all-start = ((f32[16,32,128]{2,1,0:T(8,128)}), f32[16,32,128]{2,1,0:T(8,128)S(1)}, u32[]{:S(2)}, u32[]{:S(2)}) async-start(f32[16,32,128]{2,1,0:T(8,128)} %bitcast.19), calls=%async_computation | async-start | bytes 524288 | tf_op jit(solution)/shard_map/all_to_all | solution.py:462
  24.5 0.0 copy-start.7
  24.6 0.0 copy-start.8
  24.6 0.0 copy-done.4
  24.6 0.0 copy-done.5
  24.6 0.6 copy-done.7
  25.2 0.0 copy-done.8
  25.2 0.2 shard_map.113
  25.4 11.1 %all-to-all-done.x_ref = f32[16,32,128]{2,1,0:T(8,128)S(1)} async-done(((f32[16,32,128]{2,1,0:T(8,128)}), f32[16,32,128]{2,1,0:T(8,128)S(1)}, u32[]{:S(2)}, u32[]{:S(2)}) %all-to-all-start) | async-done | bytes 262176 | tf_op jit(solution)/shard_map/all_to_all | solution.py:462
  36.5 0.0 copy-start.3
  36.5 0.0 copy-start.6
  36.5 0.1 shard_map.114
  36.6 0.0 copy-start
  36.6 0.0 copy-start.1
  36.6 0.0 copy-start.2
  36.7 14.2 %all_to_all.20.x_ref = f32[16,32,128]{2,1,0:T(8,128)S(1)} all-to-all(f32[16,32,128]{2,1,0:T(8,128)S(1)} %shard_map.114), channel_id=1, replica_groups=mesh['beam'=2,'tm'=16,'dm'=8] {'tm'}, dimensions={0} | all-to-all | bytes 524288 | tf_op jit(solution)/shard_map/all_to_all | solution.py:464
  50.9 0.0 copy-done.3
  50.9 0.0 copy-done.6
  50.9 0.0 copy-done
  50.9 0.0 copy-done.1
  50.9 0.0 copy-done.2
  50.9 1.5 %shard_map.115 = f32[272,128]{1,0:T(8,128)S(1)} custom-call(s32[1]{0:T(128)} %bitcast.d_ref, f32[16,32,128]{2,1,0:T(8,128)S(1)} %all_to_all.20.x_ref, f32[2,16,16,128]{3,2,1,0:T(8,128)S(1)} %copy-done, f32[2,8,16,128]{3,2,1,0:T(8,128)S(1)} %copy-done.3, f32[2,16,128]{2,1,0:T(8,128)S(1)} %copy-done.6, bf16[256,256]{1,0:T(8,128)(2,1)S(1)} %copy-done.2, ...), custom_call_target="tpu_custom_call" | custom-call | tf_op jit(solution)/shard_map/pallas_call | solution.py:404
  52.4 11.9 %all_to_all.21 = f32[16,1,2176]{2,1,0:T(1,128)S(1)} all-to-all(f32[16,1,2176]{2,1,0:T(1,128)S(1)} %bitcast.13), channel_id=1, replica_groups=mesh['beam'=2,'tm'=16,'dm'=8] {'tm'}, dimensions={0} | all-to-all | bytes 278528 | tf_op jit(solution)/shard_map/all_to_all | solution.py:465
  64.3 0.2 shard_map.116
  64.5 10.3 %all_to_all.22 = f32[8,1,2176]{2,1,0:T(1,128)S(1)} all-to-all(f32[8,1,2176]{2,1,0:T(1,128)S(1)} %bitcast.16), channel_id=1, replica_groups=mesh['beam'=2,'tm'=16,'dm'=8] {'dm'}, dimensions={0} | all-to-all | bytes 139264 | tf_op jit(solution)/shard_map/all_to_all | solution.py:467
  74.8 1.0 %shard_map.117 = (f32[8,16,128]{2,1,0:T(8,128)}, f32[2,2048]{1,0:T(2,128)}) custom-call(f32[136,128]{1,0:T(8,128)S(1)} %bitcast.15, f32[16,128]{1,0:T(8,128)S(1)} %get-tuple-element.14.level_ref, f32[2,2048]{1,0:T(2,128)S(1)} %get-tuple-element.15.bins_ref), custom_call_target="tpu_custom_call" | custom-call | tf_op jit(solution)/shard_map/pallas_call | solution.py:440
Async XLA Ops:
  0.6 23.9 %copy-start.4 = (f32[16,2,8,128]{3,2,1,0:T(8,128)S(1)}, f32[16,2,8,128]{3,2,1,0:T(8,128)}, u32[]{:S(2)}) copy-start(f32[16,2,8,128]{3,2,1,0:T(8,128)} %constant.21.clone.shift_ref) | copy-start | bytes 393220
  0.6 23.9 %copy-start.5 = (f32[2,8,16,128]{3,2,1,0:T(8,128)S(1)}, f32[2,8,16,128]{3,2,1,0:T(8,128)}, u32[]{:S(2)}) copy-start(f32[2,8,16,128]{3,2,1,0:T(8,128)} %constant.20.clone.within_ref) | copy-start | bytes 393220
  0.7 35.9 %all-to-all-start = ((f32[16,32,128]{2,1,0:T(8,128)}), f32[16,32,128]{2,1,0:T(8,128)S(1)}, u32[]{:S(2)}, u32[]{:S(2)}) async-start(f32[16,32,128]{2,1,0:T(8,128)} %bitcast.19), calls=%async_computation | async-start | bytes 524288 | tf_op jit(solution)/shard_map/all_to_all | solution.py:462
  24.5 0.7 copy-start.7
  24.6 0.7 copy-start.8
  36.5 14.4 %copy-start.3 = (f32[2,8,16,128]{3,2,1,0:T(8,128)S(1)}, f32[2,8,16,128]{3,2,1,0:T(8,128)}, u32[]{:S(2)}) copy-start(f32[2,8,16,128]{3,2,1,0:T(8,128)} %constant.23.clone.middle_ref) | copy-start | bytes 393220
  36.5 14.4 %copy-start.6 = (f32[2,16,128]{2,1,0:T(8,128)S(1)}, f32[2,16,128]{2,1,0:T(8,128)}, u32[]{:S(2)}) copy-start(f32[2,16,128]{2,1,0:T(8,128)} %constant.24.clone.between_ref) | copy-start | bytes 49156
  36.6 14.3 %copy-start = (f32[2,16,16,128]{3,2,1,0:T(8,128)S(1)}, f32[2,16,16,128]{3,2,1,0:T(8,128)}, u32[]{:S(2)}) copy-start(f32[2,16,16,128]{3,2,1,0:T(8,128)} %constant.22.clone.after_ref) | copy-start | bytes 786436
  36.6 14.3 %copy-start.1 = (bf16[256,256]{1,0:T(8,128)(2,1)S(1)}, bf16[256,256]{1,0:T(8,128)(2,1)}, u32[]{:S(2)}) copy-start(bf16[256,256]{1,0:T(8,128)(2,1)} %constant.26.clone.tl_ref) | copy-start | bytes 393220
  36.6 14.3 %copy-start.2 = (bf16[256,256]{1,0:T(8,128)(2,1)S(1)}, bf16[256,256]{1,0:T(8,128)(2,1)}, u32[]{:S(2)}) copy-start(bf16[256,256]{1,0:T(8,128)(2,1)} %constant.25.clone.th_ref) | copy-start | bytes 393220

commit v5 on v4

--- a/solution.py
+++ b/solution.py
@@ -51,9 +51,10 @@
     s = np.arange(shards)
     half = shards // 2
     r = np.arange(half)
-    within = np.stack(unit(r[:, None] * m[None, :], samples)).reshape(2, half, tiles, LANES)
-    shift = np.stack(unit(s[:, None] * r[None, :], shards * shards), axis=1)
-    shift = np.broadcast_to(shift[..., None], (shards, 2, half, LANES))
+    wide = np.arange(2 * part)
+    within = np.stack(unit(r[:, None] * wide[None, :], samples)).reshape(2, half, 2 * tiles, LANES)
+    shift = np.stack(unit(r[:, None] * r[None, :], samples // (2 * part)), axis=1)
+    shift = np.broadcast_to(shift[..., None], (half, 2, half, LANES))
     after = np.stack(unit(s[:, None] * m[None, :], samples // shards)).reshape(2, shards, tiles, LANES)
     middle = (half + shards * r)[:, None] * m[None, :]
     middle = np.stack(unit(middle, samples)).reshape(2, half, tiles, LANES)
@@ -120,10 +121,9 @@
 
 
 def prepare_kernel(d_ref, within_ref, shift_ref, start_ref, count_ref, w_ref, s_ref, m_ref):
-    me = d_ref[0]
-    own_class = me // 2
+    own_class = d_ref[0] % w_ref.shape[1]
     for r in range(1, w_ref.shape[1]):
-        own = [shift_ref[me, part, r : r + 1, :] for part in range(2)]
+        own = [shift_ref[own_class, part, r : r + 1, :] for part in range(2)]
         twiddle = cmul((within_ref[0, r], within_ref[1, r]), own)
         for part in range(2):
             w_ref[part, r] = twiddle[part]
@@ -147,31 +147,40 @@
     m_ref[...] = jnp.concatenate([starts] * (LANES // slots), axis=1)
 
 
+def separate_kernel(x_ref, o_ref, sems):
+    count = sems.shape[1]
+    size = x_ref.shape[0] // count
+    copies = []
+    for row in range(2):
+        for part in range(count):
+            here = pl.ds(part * size, size)
+            copies.append(pltpu.make_async_copy(x_ref.at[here, row], o_ref.at[row, here], sems.at[row, part]))
+            copies[-1].start()
+    for copy in copies:
+        copy.wait()
+
+
 def first_kernel(x_ref, w_ref, o_ref):
-    shards = x_ref.shape[0]
-    tiles = x_ref.shape[1] // 2
-    flat = x_ref.reshape(shards * 2 * tiles, LANES)
+    shards, tiles = x_ref.shape[:2]
     half = shards // 2
-    for row in range(2):
-        for k in range(tiles // SUB):
-            inner = slice(k * SUB, (k + 1) * SUB)
-            at = [(t * tiles + k * SUB) * 2 + row for t in range(shards)]
-            classes = sixteen([(flat[pl.ds(x, SUB, stride=2), :], None) for x in at])
-            for r in range(half):
-                if r:
-                    value = cmul(classes[r], [w_ref[part, r, inner, :] for part in range(2)])
-                else:
-                    value = classes[0][0], classes[half][0]
-                for part in range(2):
-                    to = part * tiles + k * SUB
-                    o_ref[2 * r + row, to : to + SUB, :] = value[part]
+    for k in range(tiles // SUB):
+        inner = slice(k * SUB, (k + 1) * SUB)
+        classes = sixteen([(x_ref[t, inner, :], None) for t in range(shards)])
+        for r in range(half):
+            if r:
+                value = cmul(classes[r], [w_ref[part, r, inner, :] for part in range(2)])
+            else:
+                value = classes[0][0], classes[half][0]
+            for part in range(2):
+                to = part * tiles + k * SUB
+                o_ref[r, to : to + SUB, :] = value[part]
 
 
 def second_kernel(d_ref, x_ref, after_ref, middle_ref, between_ref, th_ref, tl_ref, s_ref, o_ref, v_scr, x_scr, t_scr, dh_scr, dl_scr, r_scr, l_scr, h_scr):
-    shards = x_ref.shape[0]
-    tiles = x_ref.shape[1] // 2
+    shards = 2 * x_ref.shape[0]
+    tiles = x_ref.shape[1] // 4
     half = LANES // 2
-    own_class = d_ref[0] // 2
+    own_class = d_ref[0] % x_ref.shape[0]
     is_first = own_class == 0
     sub = lax.broadcasted_iota(jnp.int32, (SUB, LANES), 0)
     lead = jnp.logical_and(sub == 0, is_first)
@@ -180,8 +189,9 @@
         rows = slice(k * SUB, (k + 1) * SUB)
         main, middle = [], []
         for s in range(shards):
-            re = x_ref[s, k * SUB : (k + 1) * SUB, :]
-            im = x_ref[s, tiles + k * SUB : tiles + (k + 1) * SUB, :]
+            at = s % 2 * tiles + k * SUB
+            re = x_ref[s // 2, at : at + SUB, :]
+            im = x_ref[s // 2, 2 * tiles + at : 2 * tiles + at + SUB, :]
             main.append((re, jnp.where(is_first, 0.0, im)))
             c, sn = unit(np.float64(s), 2 * shards)
             middle.append((im * F32(c), im * F32(sn) if s else None))
@@ -293,7 +303,7 @@
     count = 2 * SLOTS * (LANES // 2) * SLOTS
     tiles = []
     for row in range(2):
-        blocks = [(2 * r + row) * ROWS for r in range(holders)]
+        blocks = [(row * holders + r) * ROWS for r in range(holders)]
         sums = [x_ref[at : at + 2 * SUB, :] for at in blocks]
         stats = [x_ref[at + 2 * SUB : at + ROWS, :] for at in blocks]
         total, both = sums[0], stats[0]
@@ -388,10 +398,25 @@
     )(me, *[near(x) for x in (within, shift, starts, counts)])
 
 
+def run_separate(series, shards):
+    tiles = series.shape[1] // LANES
+    anywhere = pl.BlockSpec(memory_space=pl.ANY)
+    rows = pl.pallas_call(
+        separate_kernel,
+        out_shape=jax.ShapeDtypeStruct((2, tiles, 1, LANES), F32),
+        in_specs=[anywhere],
+        out_specs=anywhere,
+        scratch_shapes=[pltpu.SemaphoreType.DMA((2, SUB))],
+    )(jnp.swapaxes(series.reshape(2, tiles, 1, LANES), 0, 1))
+    return rows.reshape(shards, 1, -1)
+
+
 def run_first(received, twiddles):
+    shards = received.shape[0]
+    received = received.reshape(shards, -1, LANES)
     return pl.pallas_call(
         first_kernel,
-        out_shape=shape(*received.shape),
+        out_shape=shape(received.shape[0] // 2, 2 * received.shape[1], LANES),
         in_specs=spaces(*"vv"),
         out_specs=spaces("v")[0],
         compiler_params=PARAMS,
@@ -399,7 +424,7 @@
 
 
 def run_second(me, received, second, mapping):
-    shards = received.shape[0]
+    shards = 2 * received.shape[0]
     inputs = [near(x) for x in (received, *map(jnp.asarray, second), mapping)]
     sent = pl.pallas_call(
         second_kernel,
@@ -458,10 +483,11 @@
     first, second = tables(shards, shards * series.shape[1])
     me = lax.axis_index("tm").astype(jnp.int32).reshape(1)
     swap = functools.partial(lax.all_to_all, split_axis=0, concat_axis=0, tiled=True)
-    blocks = series.reshape(2, shards, -1, LANES).transpose(1, 2, 0, 3).reshape(shards, -1, LANES)
-    samples = swap(blocks, "tm")
+    samples = swap(run_separate(series, shards), "tm")
     twiddles, mapping, markers = run_prepare(me, first, cand_start[0, 0], cand_count[0])
-    classes = swap(run_first(samples, twiddles), "tm")
+    half = shards // 2
+    by_row = [list(range(half)), list(range(half, shards))]
+    classes = swap(run_first(samples, twiddles), "tm", axis_index_groups=by_row)
     sums = swap(run_second(me, classes, second, mapping), "tm")
     bins, message, level = run_third(sums, markers)
     sifted, harmonic_sum = run_sift(swap(message, "dm"), level, bins)

time: 76.1 us -> 83.5 us (1.097)
  Pallas kernels: 2.96 us -> 12.2 us
  blocking collectives: 36.4 us -> 34.5 us
    pallas_call x1 -> x2, Pallas kernels: 0.09 us -> 9.28 us  [the longest x1 9.19 us: run_separate(): pl.pallas_call(separate_kernel, out_shape=jax.ShapeDtypeStruct((2, tiles,...]
    all_to_all x1, blocking collectives: 14.2 us -> 11.1 us  [per_device(): classes = swap(run_first(samples, twiddles), 'tm', axis_index_groups=by_row)]
    all_to_all x1, blocking collectives: 11.9 us -> 13.1 us  [per_device(): sums = swap(run_second(me, classes, second, mapping), 'tm')]
where the time goes in v5:
time: 83.5 us; the launch traced here: 83.1 us
  blocking collectives  34.5 us (41%)
  starting transfers between devices  23.9 us (29%)
  Pallas kernels  12.2 us (15%)
  waiting for transfers between devices  11.1 us (13%)
    all_to_all x1, starting transfers between devices, per_device(): samples = swap(run_separate(series, shards), 'tm')  23.9 us
    all_to_all x1, blocking collectives, per_device(): sums = swap(run_second(me, classes, second, mapping), 'tm')  13.1 us
    all_to_all x1, blocking collectives, per_device(): classes = swap(run_first(samples, twiddles), 'tm', axis_index_groups=by_row)  11.1 us
    all_to_all x1, waiting for transfers between devices, per_device(): samples = swap(run_separate(series, shards), 'tm')  11.1 us
    all_to_all x1, blocking collectives, per_device(): sifted, harmonic_sum = run_sift(swap(message, 'dm'), level, bins)  10.3 us
    pallas_call x1, Pallas kernels, run_separate(): pl.pallas_call(separate_kernel, out_shape=jax.ShapeDtypeStruct((2, tiles,...  9.19 us
  transfers between devices with their start and end apart: 1, of which 1 were waited for; matrix products, arithmetic and copies ran while one was open for 0% of the time, Pallas kernels for 0%

profile of v5, /device:TPU:513, one launch (start us, length us, event | category | flops | bytes accessed | tf_op | source)
XLA Modules:
  0.0 83.1 jit_solution(911975505597472565)
XLA Ops:
  0.6 9.2 %shard_map.114 = f32[2,256,1,128]{3,2,1,0:T(1,128)} custom-call(f32[256,2,1,128]{3,2,1,0:T(1,128)} %bitcast.21), custom_call_target="tpu_custom_call" | custom-call | tf_op jit(solution)/shard_map/pallas_call | solution.py:404
  9.8 0.0 copy-start
  9.8 0.0 copy-start.5
  9.8 23.9 %all-to-all-start = ((f32[16,1,4096]{2,1,0:T(1,128)}), f32[16,1,4096]{2,1,0:T(1,128)S(1)}, u32[]{:S(2)}, u32[]{:S(2)}) async-start(f32[16,1,4096]{2,1,0:T(1,128)} %bitcast.20), calls=%async_computation | async-start | bytes 524288 | tf_op jit(solution)/shard_map/all_to_all | solution.py:486
  33.7 0.0 copy-start.7
  33.7 0.0 copy-start.8
  33.8 0.0 copy-done
  33.8 0.0 copy-done.5
  33.8 0.6 copy-done.7
  34.4 0.0 copy-done.8
  34.4 0.2 shard_map.113
  34.6 11.1 %all-to-all-done = f32[16,1,4096]{2,1,0:T(1,128)S(1)} async-done(((f32[16,1,4096]{2,1,0:T(1,128)}), f32[16,1,4096]{2,1,0:T(1,128)S(1)}, u32[]{:S(2)}, u32[]{:S(2)}) %all-to-all-start) | async-done | bytes 262176 | tf_op jit(solution)/shard_map/all_to_all | solution.py:486
  45.7 0.0 copy-start.4
  45.7 0.0 copy-start.6
  45.7 0.1 shard_map.115
  45.8 0.0 copy-start.1
  45.8 0.0 copy-start.2
  45.8 0.0 copy-start.3
  45.9 11.1 %all_to_all.20.x_ref = f32[8,64,128]{2,1,0:T(8,128)S(1)} all-to-all(f32[8,64,128]{2,1,0:T(8,128)S(1)} %shard_map.115), channel_id=1, replica_groups={{0,8,16,24,32,40,48,56},{64,72,80,88,96,104,112,120},{1,9,17,25,33,41,4..., dimensions={0} | all-to-all | bytes 524288 | tf_op jit(solution)/shard_map/all_to_all | solution.py:490
  57.0 0.0 copy-done.4
  57.0 0.0 copy-done.6
  57.0 0.0 copy-done.1
  57.0 0.0 copy-done.2
  57.0 0.0 copy-done.3
  57.0 1.5 %shard_map.116 = f32[272,128]{1,0:T(8,128)S(1)} custom-call(s32[1]{0:T(128)} %bitcast.d_ref, f32[8,64,128]{2,1,0:T(8,128)S(1)} %all_to_all.20.x_ref, f32[2,16,16,128]{3,2,1,0:T(8,128)S(1)} %copy-done.1, f32[2,8,16,128]{3,2,1,0:T(8,128)S(1)} %copy-done.4, f32[2,16,128]{2,1,0:T(8,128)S(1)} %copy-done.6, bf16[256,256]{1,0:T(8,128)(2,1)S(1)} %copy-done.3, ...), custom_call_target="tpu_custom_call" | custom-call | tf_op jit(solution)/shard_map/pallas_call | solution.py:429
  58.5 13.1 %all_to_all.21 = f32[16,1,2176]{2,1,0:T(1,128)S(1)} all-to-all(f32[16,1,2176]{2,1,0:T(1,128)S(1)} %bitcast.14), channel_id=1, replica_groups=mesh['beam'=2,'tm'=16,'dm'=8] {'tm'}, dimensions={0} | all-to-all | bytes 278528 | tf_op jit(solution)/shard_map/all_to_all | solution.py:491
  71.6 0.2 shard_map.117
  71.8 10.3 %all_to_all.22 = f32[8,1,2176]{2,1,0:T(1,128)S(1)} all-to-all(f32[8,1,2176]{2,1,0:T(1,128)S(1)} %bitcast.17), channel_id=1, replica_groups=mesh['beam'=2,'tm'=16,'dm'=8] {'dm'}, dimensions={0} | all-to-all | bytes 139264 | tf_op jit(solution)/shard_map/all_to_all | solution.py:493
  82.1 1.0 %shard_map.118 = (f32[8,16,128]{2,1,0:T(8,128)}, f32[2,2048]{1,0:T(2,128)}) custom-call(f32[136,128]{1,0:T(8,128)S(1)} %bitcast.16, f32[16,128]{1,0:T(8,128)S(1)} %get-tuple-element.14.level_ref, f32[2,2048]{1,0:T(2,128)S(1)} %get-tuple-element.15.bins_ref), custom_call_target="tpu_custom_call" | custom-call | tf_op jit(solution)/shard_map/pallas_call | solution.py:465
Async XLA Ops:
  9.8 23.9 %copy-start = (f32[2,8,32,128]{3,2,1,0:T(8,128)S(1)}, f32[2,8,32,128]{3,2,1,0:T(8,128)}, u32[]{:S(2)}) copy-start(f32[2,8,32,128]{3,2,1,0:T(8,128)} %constant.20.clone.within_ref) | copy-start | bytes 786436
  9.8 23.9 %copy-start.5 = (f32[8,2,8,128]{3,2,1,0:T(8,128)S(1)}, f32[8,2,8,128]{3,2,1,0:T(8,128)}, u32[]{:S(2)}) copy-start(f32[8,2,8,128]{3,2,1,0:T(8,128)} %constant.21.clone.shift_ref) | copy-start | bytes 196612
  9.8 35.9 %all-to-all-start = ((f32[16,1,4096]{2,1,0:T(1,128)}), f32[16,1,4096]{2,1,0:T(1,128)S(1)}, u32[]{:S(2)}, u32[]{:S(2)}) async-start(f32[16,1,4096]{2,1,0:T(1,128)} %bitcast.20), calls=%async_computation | async-start | bytes 524288 | tf_op jit(solution)/shard_map/all_to_all | solution.py:486
  33.7 0.7 copy-start.7
  33.7 0.7 copy-start.8
  45.7 11.3 %copy-start.4 = (f32[2,8,16,128]{3,2,1,0:T(8,128)S(1)}, f32[2,8,16,128]{3,2,1,0:T(8,128)}, u32[]{:S(2)}) copy-start(f32[2,8,16,128]{3,2,1,0:T(8,128)} %constant.23.clone.middle_ref) | copy-start | bytes 393220
  45.7 11.3 %copy-start.6 = (f32[2,16,128]{2,1,0:T(8,128)S(1)}, f32[2,16,128]{2,1,0:T(8,128)}, u32[]{:S(2)}) copy-start(f32[2,16,128]{2,1,0:T(8,128)} %constant.24.clone.between_ref) | copy-start | bytes 49156
  45.8 11.2 %copy-start.1 = (f32[2,16,16,128]{3,2,1,0:T(8,128)S(1)}, f32[2,16,16,128]{3,2,1,0:T(8,128)}, u32[]{:S(2)}) copy-start(f32[2,16,16,128]{3,2,1,0:T(8,128)} %constant.22.clone.after_ref) | copy-start | bytes 786436
  45.8 11.2 %copy-start.2 = (bf16[256,256]{1,0:T(8,128)(2,1)S(1)}, bf16[256,256]{1,0:T(8,128)(2,1)}, u32[]{:S(2)}) copy-start(bf16[256,256]{1,0:T(8,128)(2,1)} %constant.26.clone.tl_ref) | copy-start | bytes 393220
  45.8 11.2 %copy-start.3 = (bf16[256,256]{1,0:T(8,128)(2,1)S(1)}, bf16[256,256]{1,0:T(8,128)(2,1)}, u32[]{:S(2)}) copy-start(bf16[256,256]{1,0:T(8,128)(2,1)} %constant.25.clone.th_ref) | copy-start | bytes 393220

commit v6 on v5

--- a/solution.py
+++ b/solution.py
@@ -120,14 +120,21 @@
     return out
 
 
-def prepare_kernel(d_ref, within_ref, shift_ref, start_ref, count_ref, w_ref, s_ref, m_ref):
-    own_class = d_ref[0] % w_ref.shape[1]
-    for r in range(1, w_ref.shape[1]):
-        own = [shift_ref[own_class, part, r : r + 1, :] for part in range(2)]
-        twiddle = cmul((within_ref[0, r], within_ref[1, r]), own)
-        for part in range(2):
-            w_ref[part, r] = twiddle[part]
-
+def prepare_kernel(d_ref, x_ref, start_ref, count_ref, o_ref, s_ref, m_ref, x_scr, start_scr, count_scr, sems):
+    small = [
+        pltpu.make_async_copy(start_ref, start_scr, sems.at[0]),
+        pltpu.make_async_copy(count_ref, count_scr, sems.at[1]),
+    ]
+    pieces = sems.shape[0] - 2
+    size = x_ref.shape[0] // pieces
+    copies = []
+    for piece in range(pieces):
+        here = pl.ds(piece * size, size)
+        copies.append(pltpu.make_async_copy(x_ref.at[here], x_scr.at[here], sems.at[2 + piece]))
+    for copy in copies + small:
+        copy.start()
+
+    own_class = d_ref[0] % SUB
     phi = lax.broadcasted_iota(jnp.int32, (SLOTS, COARSE), 1)
     slot = lax.broadcasted_iota(jnp.int32, (SLOTS, COARSE), 0)
     pairs = slot * SLOTS - jnp.where(slot < SUB, 0, SUB * SLOTS - SUB)
@@ -138,37 +145,35 @@
             hit = jnp.where(h * phi - COARSE * c == residue, 1.0, 0.0)
             s_ref[pl.ds(index * PIECE + k * SLOTS, SLOTS), :] = hit.astype(BF16)
 
+    tiles = x_ref.shape[0] // 2
+    for piece, copy in enumerate(copies):
+        copy.wait()
+        for at in range(piece * size // 2, (piece + 1) * size // 2, SUB):
+            for row in range(2):
+                o_ref[row * tiles + at : row * tiles + at + SUB, :] = x_scr[pl.ds(2 * at + row, SUB, stride=2), :]
+
+    for copy in small:
+        copy.wait()
     bands, slots = start_ref.shape
     cell = [lax.broadcasted_iota(jnp.int32, (bands, bands), axis) for axis in range(2)]
-    counts = jnp.where(cell[0] == cell[1], count_ref[...].astype(F32), 0.0)
+    counts = jnp.where(cell[0] == cell[1], count_scr[...].astype(F32), 0.0)
     live = jnp.sum(counts, axis=1, keepdims=True).astype(jnp.int32)
     slot = lax.broadcasted_iota(jnp.int32, (bands, slots), 1)
-    starts = jnp.where(slot < live, start_ref[...], -1).astype(F32)
+    starts = jnp.where(slot < live, start_scr[...], -1).astype(F32)
     m_ref[...] = jnp.concatenate([starts] * (LANES // slots), axis=1)
 
 
-def separate_kernel(x_ref, o_ref, sems):
-    count = sems.shape[1]
-    size = x_ref.shape[0] // count
-    copies = []
-    for row in range(2):
-        for part in range(count):
-            here = pl.ds(part * size, size)
-            copies.append(pltpu.make_async_copy(x_ref.at[here, row], o_ref.at[row, here], sems.at[row, part]))
-            copies[-1].start()
-    for copy in copies:
-        copy.wait()
-
-
-def first_kernel(x_ref, w_ref, o_ref):
+def first_kernel(d_ref, x_ref, within_ref, shift_ref, o_ref):
     shards, tiles = x_ref.shape[:2]
     half = shards // 2
+    me = d_ref[0] % half
     for k in range(tiles // SUB):
         inner = slice(k * SUB, (k + 1) * SUB)
         classes = sixteen([(x_ref[t, inner, :], None) for t in range(shards)])
         for r in range(half):
             if r:
-                value = cmul(classes[r], [w_ref[part, r, inner, :] for part in range(2)])
+                own = [shift_ref[me, part, r : r + 1, :] for part in range(2)]
+                value = cmul(classes[r], cmul([within_ref[part, r, inner, :] for part in range(2)], own))
             else:
                 value = classes[0][0], classes[half][0]
             for part in range(2):
@@ -383,44 +388,39 @@
     return [pl.BlockSpec(memory_space=pltpu.SMEM if kind == "s" else pltpu.VMEM) for kind in kinds]
 
 
-def run_prepare(me, first, starts, counts):
-    within, shift = map(jnp.asarray, first)
-    return pl.pallas_call(
+def run_prepare(me, series, starts, counts, shards):
+    tiles = series.shape[1] // LANES
+    lines = jnp.swapaxes(series.reshape(2, tiles, LANES), 0, 1).reshape(2 * tiles, LANES)
+    rows, mapping, markers = pl.pallas_call(
         prepare_kernel,
         out_shape=(
-            shape(*within.shape),
+            shape(2 * tiles, LANES),
             pltpu.VMEM((CHUNKS * LANES, COARSE), BF16),
             shape(starts.shape[0], LANES),
         ),
-        in_specs=spaces("s", *"vvvv"),
+        in_specs=spaces("s") + [pl.BlockSpec(memory_space=pl.ANY)] * 3,
         out_specs=spaces(*"vvv"),
+        scratch_shapes=[
+            pltpu.VMEM((2 * tiles, LANES), F32),
+            pltpu.VMEM(starts.shape, jnp.int32),
+            pltpu.VMEM(counts.shape, jnp.int32),
+            pltpu.SemaphoreType.DMA((6,)),
+        ],
         compiler_params=PARAMS,
-    )(me, *[near(x) for x in (within, shift, starts, counts)])
-
-
-def run_separate(series, shards):
-    tiles = series.shape[1] // LANES
-    anywhere = pl.BlockSpec(memory_space=pl.ANY)
-    rows = pl.pallas_call(
-        separate_kernel,
-        out_shape=jax.ShapeDtypeStruct((2, tiles, 1, LANES), F32),
-        in_specs=[anywhere],
-        out_specs=anywhere,
-        scratch_shapes=[pltpu.SemaphoreType.DMA((2, SUB))],
-    )(jnp.swapaxes(series.reshape(2, tiles, 1, LANES), 0, 1))
-    return rows.reshape(shards, 1, -1)
-
-
-def run_first(received, twiddles):
+    )(me, *[pltpu.with_memory_space_constraint(x, pltpu.HBM) for x in (lines, starts, counts)])
+    return rows.reshape(shards, -1, LANES), mapping, markers
+
+
+def run_first(me, received, first):
     shards = received.shape[0]
-    received = received.reshape(shards, -1, LANES)
+    within, shift = map(jnp.asarray, first)
     return pl.pallas_call(
         first_kernel,
-        out_shape=shape(received.shape[0] // 2, 2 * received.shape[1], LANES),
-        in_specs=spaces(*"vv"),
+        out_shape=shape(shards // 2, 2 * received.shape[1], LANES),
+        in_specs=spaces(*"svvv"),
         out_specs=spaces("v")[0],
         compiler_params=PARAMS,
-    )(near(received), near(twiddles))
+    )(me, *[near(x) for x in (received, within, shift)])
 
 
 def run_second(me, received, second, mapping):
@@ -483,11 +483,10 @@
     first, second = tables(shards, shards * series.shape[1])
     me = lax.axis_index("tm").astype(jnp.int32).reshape(1)
     swap = functools.partial(lax.all_to_all, split_axis=0, concat_axis=0, tiled=True)
-    samples = swap(run_separate(series, shards), "tm")
-    twiddles, mapping, markers = run_prepare(me, first, cand_start[0, 0], cand_count[0])
+    rows, mapping, markers = run_prepare(me, series, cand_start[0, 0], cand_count[0], shards)
     half = shards // 2
     by_row = [list(range(half)), list(range(half, shards))]
-    classes = swap(run_first(samples, twiddles), "tm", axis_index_groups=by_row)
+    classes = swap(run_first(me, swap(rows, "tm"), first), "tm", axis_index_groups=by_row)
     sums = swap(run_second(me, classes, second, mapping), "tm")
     bins, message, level = run_third(sums, markers)
     sifted, harmonic_sum = run_sift(swap(message, "dm"), level, bins)

time: 83.5 us -> 74.5 us (0.89)
  blocking collectives: 34.5 us -> 69.5 us
  starting transfers between devices: 23.9 us -> 0 us
  waiting for transfers between devices: 11.1 us -> 0 us
  Pallas kernels: 12.2 us -> 3.95 us
    all_to_all x1 -> x2, blocking collectives: 11.1 us -> 46.1 us  [the longest x1 34.9 us: per_device(): swap(rows, 'tm')]
    all_to_all x1 -> x0, starting transfers between devices: 23.9 us -> none  [per_device(): samples = swap(run_separate(series, shards), 'tm')]
    all_to_all x1 -> x0, waiting for transfers between devices: 11.1 us -> none  [per_device(): samples = swap(run_separate(series, shards), 'tm')]
    pallas_call x3 -> x2, Pallas kernels: 9.49 us -> 1.28 us  [the longest x1 1.16 us: run_prepare(): pl.pallas_call(prepare_kernel, out_shape=(shape(2 * tiles, LANES), pltpu....]
  transfers between devices with their start and end apart: 1 -> 0, of which waited for: 1 -> 0; matrix products, arithmetic and copies ran while one was open for 0% -> 0% of each run, Pallas kernels for 0% -> 0%
where the time goes in v6:
time: 74.5 us; the launch traced here: 74.2 us
  blocking collectives  69.5 us (93%)
  Pallas kernels  3.95 us (5%)
    all_to_all x1, blocking collectives, per_device(): swap(rows, 'tm')  34.9 us
    all_to_all x1, blocking collectives, per_device(): sums = swap(run_second(me, classes, second, mapping), 'tm')  13.1 us
    all_to_all x1, blocking collectives, per_device(): swap(run_first(me, swap(rows, 'tm'), first), 'tm', axis_index_groups=by_row)  11.1 us
    all_to_all x1, blocking collectives, per_device(): sifted, harmonic_sum = run_sift(swap(message, 'dm'), level, bins)  10.3 us

profile of v6, /device:TPU:513, one launch (start us, length us, event | category | flops | bytes accessed | tf_op | source)
XLA Modules:
  0.0 74.2 jit_solution(15132916037579368395)
XLA Ops:
  0.6 1.2 %shard_map.113 = (f32[512,128]{1,0:T(8,128)S(1)}, bf16[1152,256]{1,0:T(8,128)(2,1)S(1)}, f32[8,128]{1,0:T(8,128)S(1)}) custom-call(s32[1]{0:T(128)} %bitcast.d_ref, f32[512,128]{1,0:T(8,128)} %bitcast.19, s32[8,16]{1,0:T(8,128)} %bitcast.20, s32[1,8]{1,0:T(1,128)} %bitcast.21), custom_call_target="tpu_custom_call" | custom-call | tf_op jit(solution)/shard_map/pallas_call | solution.py:394
  1.8 0.0 copy-start
  1.8 0.0 copy-start.5
  1.8 34.9 %all_to_all.20.x_ref = f32[16,32,128]{2,1,0:T(8,128)S(1)} all-to-all(f32[16,32,128]{2,1,0:T(8,128)S(1)} %bitcast.17), channel_id=1, replica_groups=mesh['beam'=2,'tm'=16,'dm'=8] {'tm'}, dimensions={0} | all-to-all | bytes 524288 | tf_op jit(solution)/shard_map/all_to_all | solution.py:489
  36.8 0.0 copy-done
  36.8 0.0 copy-done.5
  36.8 0.0 copy-start.4
  36.8 0.0 copy-start.6
  36.8 0.1 shard_map.114
  36.9 0.0 copy-start.1
  36.9 0.0 copy-start.2
  36.9 0.0 copy-start.3
  36.9 11.1 %all_to_all.21.x_ref = f32[8,64,128]{2,1,0:T(8,128)S(1)} all-to-all(f32[8,64,128]{2,1,0:T(8,128)S(1)} %shard_map.114), channel_id=1, replica_groups={{0,8,16,24,32,40,48,56},{64,72,80,88,96,104,112,120},{1,9,17,25,33,41,4..., dimensions={0} | all-to-all | bytes 524288 | tf_op jit(solution)/shard_map/all_to_all | solution.py:489
  48.1 0.0 copy-done.4
  48.1 0.0 copy-done.6
  48.1 0.0 copy-done.1
  48.1 0.0 copy-done.2
  48.1 0.0 copy-done.3
  48.1 1.5 %shard_map.115 = f32[272,128]{1,0:T(8,128)S(1)} custom-call(s32[1]{0:T(128)} %bitcast.d_ref, f32[8,64,128]{2,1,0:T(8,128)S(1)} %all_to_all.21.x_ref, f32[2,16,16,128]{3,2,1,0:T(8,128)S(1)} %copy-done.1, f32[2,8,16,128]{3,2,1,0:T(8,128)S(1)} %copy-done.4, f32[2,16,128]{2,1,0:T(8,128)S(1)} %copy-done.6, bf16[256,256]{1,0:T(8,128)(2,1)S(1)} %copy-done.3, ...), custom_call_target="tpu_custom_call" | custom-call | tf_op jit(solution)/shard_map/pallas_call | solution.py:429
  49.6 13.1 %all_to_all.22 = f32[16,1,2176]{2,1,0:T(1,128)S(1)} all-to-all(f32[16,1,2176]{2,1,0:T(1,128)S(1)} %bitcast.14), channel_id=1, replica_groups=mesh['beam'=2,'tm'=16,'dm'=8] {'tm'}, dimensions={0} | all-to-all | bytes 278528 | tf_op jit(solution)/shard_map/all_to_all | solution.py:490
  62.7 0.2 shard_map.116
  62.9 10.3 %all_to_all.23 = f32[8,1,2176]{2,1,0:T(1,128)S(1)} all-to-all(f32[8,1,2176]{2,1,0:T(1,128)S(1)} %bitcast.18), channel_id=1, replica_groups=mesh['beam'=2,'tm'=16,'dm'=8] {'dm'}, dimensions={0} | all-to-all | bytes 139264 | tf_op jit(solution)/shard_map/all_to_all | solution.py:492
  73.2 1.0 %shard_map.117 = (f32[8,16,128]{2,1,0:T(8,128)}, f32[2,2048]{1,0:T(2,128)}) custom-call(f32[136,128]{1,0:T(8,128)S(1)} %bitcast.16, f32[16,128]{1,0:T(8,128)S(1)} %get-tuple-element.14.level_ref, f32[2,2048]{1,0:T(2,128)S(1)} %get-tuple-element.15.bins_ref), custom_call_target="tpu_custom_call" | custom-call | tf_op jit(solution)/shard_map/pallas_call | solution.py:465
Async XLA Ops:
  1.8 35.0 %copy-start = (f32[2,8,32,128]{3,2,1,0:T(8,128)S(1)}, f32[2,8,32,128]{3,2,1,0:T(8,128)}, u32[]{:S(2)}) copy-start(f32[2,8,32,128]{3,2,1,0:T(8,128)} %constant.20.clone.within_ref) | copy-start | bytes 786436
  1.8 35.0 %copy-start.5 = (f32[8,2,8,128]{3,2,1,0:T(8,128)S(1)}, f32[8,2,8,128]{3,2,1,0:T(8,128)}, u32[]{:S(2)}) copy-start(f32[8,2,8,128]{3,2,1,0:T(8,128)} %constant.21.clone.shift_ref) | copy-start | bytes 196612
  36.8 11.3 %copy-start.4 = (f32[2,8,16,128]{3,2,1,0:T(8,128)S(1)}, f32[2,8,16,128]{3,2,1,0:T(8,128)}, u32[]{:S(2)}) copy-start(f32[2,8,16,128]{3,2,1,0:T(8,128)} %constant.23.clone.middle_ref) | copy-start | bytes 393220
  36.8 11.3 %copy-start.6 = (f32[2,16,128]{2,1,0:T(8,128)S(1)}, f32[2,16,128]{2,1,0:T(8,128)}, u32[]{:S(2)}) copy-start(f32[2,16,128]{2,1,0:T(8,128)} %constant.24.clone.between_ref) | copy-start | bytes 49156
  36.9 11.2 %copy-start.1 = (f32[2,16,16,128]{3,2,1,0:T(8,128)S(1)}, f32[2,16,16,128]{3,2,1,0:T(8,128)}, u32[]{:S(2)}) copy-start(f32[2,16,16,128]{3,2,1,0:T(8,128)} %constant.22.clone.after_ref) | copy-start | bytes 786436
  36.9 11.2 %copy-start.2 = (bf16[256,256]{1,0:T(8,128)(2,1)S(1)}, bf16[256,256]{1,0:T(8,128)(2,1)}, u32[]{:S(2)}) copy-start(bf16[256,256]{1,0:T(8,128)(2,1)} %constant.26.clone.tl_ref) | copy-start | bytes 393220
  36.9 11.2 %copy-start.3 = (bf16[256,256]{1,0:T(8,128)(2,1)S(1)}, bf16[256,256]{1,0:T(8,128)(2,1)}, u32[]{:S(2)}) copy-start(bf16[256,256]{1,0:T(8,128)(2,1)} %constant.25.clone.th_ref) | copy-start | bytes 393220

commit v7 on v6

--- a/solution.py
+++ b/solution.py
@@ -131,7 +131,7 @@
     for piece in range(pieces):
         here = pl.ds(piece * size, size)
         copies.append(pltpu.make_async_copy(x_ref.at[here], x_scr.at[here], sems.at[2 + piece]))
-    for copy in copies + small:
+    for copy in small + copies:
         copy.start()
 
     own_class = d_ref[0] % SUB
@@ -145,13 +145,6 @@
             hit = jnp.where(h * phi - COARSE * c == residue, 1.0, 0.0)
             s_ref[pl.ds(index * PIECE + k * SLOTS, SLOTS), :] = hit.astype(BF16)
 
-    tiles = x_ref.shape[0] // 2
-    for piece, copy in enumerate(copies):
-        copy.wait()
-        for at in range(piece * size // 2, (piece + 1) * size // 2, SUB):
-            for row in range(2):
-                o_ref[row * tiles + at : row * tiles + at + SUB, :] = x_scr[pl.ds(2 * at + row, SUB, stride=2), :]
-
     for copy in small:
         copy.wait()
     bands, slots = start_ref.shape
@@ -161,6 +154,13 @@
     slot = lax.broadcasted_iota(jnp.int32, (bands, slots), 1)
     starts = jnp.where(slot < live, start_scr[...], -1).astype(F32)
     m_ref[...] = jnp.concatenate([starts] * (LANES // slots), axis=1)
+
+    tiles = x_ref.shape[0] // 2
+    for piece, copy in enumerate(copies):
+        copy.wait()
+        for at in range(piece * size // 2, (piece + 1) * size // 2, SUB):
+            for row in range(2):
+                o_ref[row * tiles + at : row * tiles + at + SUB, :] = x_scr[pl.ds(2 * at + row, SUB, stride=2), :]
 
 
 def first_kernel(d_ref, x_ref, within_ref, shift_ref, o_ref):
@@ -460,7 +460,7 @@
 
 def run_sift(received, level, bins):
     bands = received.shape[0]
-    steps = bands // 2
+    steps = 1
     anywhere = pl.BlockSpec(memory_space=pl.ANY)
     return pl.pallas_call(
         sift_kernel,

time: 74.5 us -> 74.4 us (level)
  no operation moved by 1% of the time
where the time goes in v7:
time: 74.4 us; the launch traced here: 74.1 us
  blocking collectives  69.5 us (93%)
  Pallas kernels  3.82 us (5%)
    all_to_all x1, blocking collectives, per_device(): swap(rows, 'tm')  34.9 us
    all_to_all x1, blocking collectives, per_device(): sums = swap(run_second(me, classes, second, mapping), 'tm')  13.1 us
    all_to_all x1, blocking collectives, per_device(): swap(run_first(me, swap(rows, 'tm'), first), 'tm', axis_index_groups=by_row)  11.1 us
    all_to_all x1, blocking collectives, per_device(): sifted, harmonic_sum = run_sift(swap(message, 'dm'), level, bins)  10.3 us

profile of v7, /device:TPU:513, one launch (start us, length us, event | category | flops | bytes accessed | tf_op | source)
XLA Modules:
  0.0 74.1 jit_solution(15573722144631601613)
XLA Ops:
  0.6 1.0 %shard_map.113 = (f32[512,128]{1,0:T(8,128)S(1)}, bf16[1152,256]{1,0:T(8,128)(2,1)S(1)}, f32[8,128]{1,0:T(8,128)S(1)}) custom-call(s32[1]{0:T(128)} %bitcast.d_ref, f32[512,128]{1,0:T(8,128)} %bitcast.19, s32[8,16]{1,0:T(8,128)} %bitcast.20, s32[1,8]{1,0:T(1,128)} %bitcast.21), custom_call_target="tpu_custom_call" | custom-call | tf_op jit(solution)/shard_map/pallas_call | solution.py:394
  1.7 0.0 copy-start
  1.7 0.0 copy-start.5
  1.7 34.9 %all_to_all.20.x_ref = f32[16,32,128]{2,1,0:T(8,128)S(1)} all-to-all(f32[16,32,128]{2,1,0:T(8,128)S(1)} %bitcast.17), channel_id=1, replica_groups=mesh['beam'=2,'tm'=16,'dm'=8] {'tm'}, dimensions={0} | all-to-all | bytes 524288 | tf_op jit(solution)/shard_map/all_to_all | solution.py:489
  36.6 0.0 copy-done
  36.6 0.0 copy-done.5
  36.6 0.0 copy-start.4
  36.6 0.0 copy-start.6
  36.7 0.1 shard_map.114
  36.8 0.0 copy-start.1
  36.8 0.0 copy-start.2
  36.8 0.0 copy-start.3
  36.8 11.1 %all_to_all.21.x_ref = f32[8,64,128]{2,1,0:T(8,128)S(1)} all-to-all(f32[8,64,128]{2,1,0:T(8,128)S(1)} %shard_map.114), channel_id=1, replica_groups={{0,8,16,24,32,40,48,56},{64,72,80,88,96,104,112,120},{1,9,17,25,33,41,4..., dimensions={0} | all-to-all | bytes 524288 | tf_op jit(solution)/shard_map/all_to_all | solution.py:489
  48.0 0.0 copy-done.4
  48.0 0.0 copy-done.6
  48.0 0.0 copy-done.1
  48.0 0.0 copy-done.2
  48.0 0.0 copy-done.3
  48.0 1.5 %shard_map.115 = f32[272,128]{1,0:T(8,128)S(1)} custom-call(s32[1]{0:T(128)} %bitcast.d_ref, f32[8,64,128]{2,1,0:T(8,128)S(1)} %all_to_all.21.x_ref, f32[2,16,16,128]{3,2,1,0:T(8,128)S(1)} %copy-done.1, f32[2,8,16,128]{3,2,1,0:T(8,128)S(1)} %copy-done.4, f32[2,16,128]{2,1,0:T(8,128)S(1)} %copy-done.6, bf16[256,256]{1,0:T(8,128)(2,1)S(1)} %copy-done.3, ...), custom_call_target="tpu_custom_call" | custom-call | tf_op jit(solution)/shard_map/pallas_call | solution.py:429
  49.5 13.1 %all_to_all.22 = f32[16,1,2176]{2,1,0:T(1,128)S(1)} all-to-all(f32[16,1,2176]{2,1,0:T(1,128)S(1)} %bitcast.14), channel_id=1, replica_groups=mesh['beam'=2,'tm'=16,'dm'=8] {'tm'}, dimensions={0} | all-to-all | bytes 278528 | tf_op jit(solution)/shard_map/all_to_all | solution.py:490
  62.6 0.2 shard_map.116
  62.8 10.3 %all_to_all.23 = f32[8,1,2176]{2,1,0:T(1,128)S(1)} all-to-all(f32[8,1,2176]{2,1,0:T(1,128)S(1)} %bitcast.18), channel_id=1, replica_groups=mesh['beam'=2,'tm'=16,'dm'=8] {'dm'}, dimensions={0} | all-to-all | bytes 139264 | tf_op jit(solution)/shard_map/all_to_all | solution.py:492
  73.1 1.0 %shard_map.117 = (f32[8,16,128]{2,1,0:T(8,128)}, f32[2,2048]{1,0:T(2,128)}) custom-call(f32[136,128]{1,0:T(8,128)S(1)} %bitcast.16, f32[16,128]{1,0:T(8,128)S(1)} %get-tuple-element.14.level_ref, f32[2,2048]{1,0:T(2,128)S(1)} %get-tuple-element.15.bins_ref), custom_call_target="tpu_custom_call" | custom-call | tf_op jit(solution)/shard_map/pallas_call | solution.py:465
Async XLA Ops:
  1.7 35.0 %copy-start = (f32[2,8,32,128]{3,2,1,0:T(8,128)S(1)}, f32[2,8,32,128]{3,2,1,0:T(8,128)}, u32[]{:S(2)}) copy-start(f32[2,8,32,128]{3,2,1,0:T(8,128)} %constant.20.clone.within_ref) | copy-start | bytes 786436
  1.7 35.0 %copy-start.5 = (f32[8,2,8,128]{3,2,1,0:T(8,128)S(1)}, f32[8,2,8,128]{3,2,1,0:T(8,128)}, u32[]{:S(2)}) copy-start(f32[8,2,8,128]{3,2,1,0:T(8,128)} %constant.21.clone.shift_ref) | copy-start | bytes 196612
  36.6 11.3 %copy-start.4 = (f32[2,8,16,128]{3,2,1,0:T(8,128)S(1)}, f32[2,8,16,128]{3,2,1,0:T(8,128)}, u32[]{:S(2)}) copy-start(f32[2,8,16,128]{3,2,1,0:T(8,128)} %constant.23.clone.middle_ref) | copy-start | bytes 393220
  36.6 11.3 %copy-start.6 = (f32[2,16,128]{2,1,0:T(8,128)S(1)}, f32[2,16,128]{2,1,0:T(8,128)}, u32[]{:S(2)}) copy-start(f32[2,16,128]{2,1,0:T(8,128)} %constant.24.clone.between_ref) | copy-start | bytes 49156
  36.8 11.2 %copy-start.1 = (f32[2,16,16,128]{3,2,1,0:T(8,128)S(1)}, f32[2,16,16,128]{3,2,1,0:T(8,128)}, u32[]{:S(2)}) copy-start(f32[2,16,16,128]{3,2,1,0:T(8,128)} %constant.22.clone.after_ref) | copy-start | bytes 786436
  36.8 11.2 %copy-start.2 = (bf16[256,256]{1,0:T(8,128)(2,1)S(1)}, bf16[256,256]{1,0:T(8,128)(2,1)}, u32[]{:S(2)}) copy-start(bf16[256,256]{1,0:T(8,128)(2,1)} %constant.26.clone.tl_ref) | copy-start | bytes 393220
  36.8 11.2 %copy-start.3 = (bf16[256,256]{1,0:T(8,128)(2,1)S(1)}, bf16[256,256]{1,0:T(8,128)(2,1)}, u32[]{:S(2)}) copy-start(bf16[256,256]{1,0:T(8,128)(2,1)} %constant.25.clone.th_ref) | copy-start | bytes 393220

commit v8 on v7

--- a/solution.py
+++ b/solution.py
@@ -18,7 +18,8 @@
 COARSE = 256
 SLOTS = 16
 PIECE = 32
-PIECES = [(h, c) for h in range(1, HARM + 1) for c in range(h)]
+ODD = {h: h // (h & -h) for h in range(1, HARM + 1)}
+PIECES = [(h, range(c, c + ODD[h])) for h in range(1, HARM + 1) for c in range(0, h, ODD[h])]
 CHUNKS = len(PIECES) // 4
 ROWS = 2 * SUB + 1
 
@@ -65,8 +66,17 @@
         c2, s2 = unit(q2[:, None] * v[None, :], LANES)
         rows += [np.concatenate([c2, -s2], axis=1), np.concatenate([s2, c2], axis=1)]
     last = np_halves(np.concatenate(rows, axis=0))
+    fitting = np.zeros((half, SUB, LANES), np.float32)
+    for own in range(half):
+        for lane in range(LANES):
+            slot = lane % SLOTS
+            residue = own + SLOTS * slot if own else SLOTS * (slot % SUB) + SUB * (slot // SUB)
+            if lane % PIECE >= SLOTS:
+                residue = COARSE - residue if residue else COARSE // 2
+            for odd in (3, 5, 7):
+                fitting[own, odd, lane] = next(c for c in range(odd) if (residue + COARSE * c) % odd == 0)
     first = [x.astype(np.float32) for x in (within, shift)]
-    second = [x.astype(np.float32) for x in (after, middle, between)] + list(last)
+    second = [x.astype(np.float32) for x in (after, middle, between, fitting)] + [np.concatenate(last)]
     return first, second
 
 
@@ -140,9 +150,11 @@
     pairs = slot * SLOTS - jnp.where(slot < SUB, 0, SUB * SLOTS - SUB)
     mine = jnp.where(own_class == 0, pairs, own_class + SLOTS * slot)
     mirror = jnp.where(mine == 0, COARSE // 2, COARSE - mine)
-    for index, (h, c) in enumerate(PIECES):
+    for index, (h, carries) in enumerate(PIECES):
         for k, residue in enumerate((mine, mirror)):
-            hit = jnp.where(h * phi - COARSE * c == residue, 1.0, 0.0)
+            gap = h * phi - residue
+            hit = functools.reduce(jnp.logical_or, [gap == COARSE * c for c in carries])
+            hit = jnp.where(hit, 1.0, 0.0)
             s_ref[pl.ds(index * PIECE + k * SLOTS, SLOTS), :] = hit.astype(BF16)
 
     for copy in small:
@@ -181,7 +193,7 @@
                 o_ref[r, to : to + SUB, :] = value[part]
 
 
-def second_kernel(d_ref, x_ref, after_ref, middle_ref, between_ref, th_ref, tl_ref, s_ref, o_ref, v_scr, x_scr, t_scr, dh_scr, dl_scr, r_scr, l_scr, h_scr):
+def second_kernel(d_ref, x_ref, after_ref, middle_ref, between_ref, fit_ref, table_ref, s_ref, o_ref, v_scr, x_scr, t_scr, dh_scr, dl_scr, r_scr, l_scr, h_scr):
     shards = 2 * x_ref.shape[0]
     tiles = x_ref.shape[1] // 4
     half = LANES // 2
@@ -250,7 +262,8 @@
     for part in range(2):
         top = dh_scr[part * 256 : (part + 1) * 256, :]
         rest = dl_scr[part * 256 : (part + 1) * 256, :]
-        z = dot_t(th_ref[...], top) + dot_t(th_ref[...], rest) + dot_t(tl_ref[...], top)
+        z = dot_t(table_ref[...], top)
+        z = z[:256] + z[256:] + dot_t(table_ref[:256, :], rest)
         z = z * z
         low = z[0:half] + z[half : 2 * half]
         high = z[2 * half : 3 * half] + z[3 * half :]
@@ -275,18 +288,25 @@
             at = (group * 4 + shift) * half
             r_scr[at : at + half, :] = pltpu.roll(value, shift * PIECE, 1) if shift else value
     lane8 = lax.broadcasted_iota(jnp.int32, (SUB, LANES), 1) // PIECE
+    fits = {}
+    for index, (h, _) in enumerate(PIECES):
+        if ODD[h] > 1:
+            fit = jnp.broadcast_to(fit_ref[own_class, ODD[h] : ODD[h] + 1, :], (SUB, LANES))
+            fits[index % 4, ODD[h]] = jnp.where(lane8 == index % 4, fit, -1.0).astype(jnp.int32)
     for chunk in range(CHUNKS):
         for g_pair in range(tiles // 2):
             parts = []
             for g0 in (2 * g_pair, 2 * g_pair + 1):
                 tile = None
                 for place in range(4):
-                    h, c = PIECES[chunk * 4 + place]
-                    rho, e = (h * g0 + c) % tiles, (h * g0 + c) // tiles
-                    shift = (place - rho % 4) % 4
-                    rows = pl.ds((rho // 4 * 4 + shift) * half + e, SUB, stride=h)
-                    got = r_scr[rows, :]
-                    tile = got if tile is None else jnp.where(lane8 == place, got, tile)
+                    h, carries = PIECES[chunk * 4 + place]
+                    for c in carries:
+                        rho, e = (h * g0 + c) % tiles, (h * g0 + c) // tiles
+                        shift = (place - rho % 4) % 4
+                        rows = pl.ds((rho // 4 * 4 + shift) * half + e, SUB, stride=h)
+                        got = r_scr[rows, :]
+                        here = lane8 == place if c == carries[0] else fits[place, ODD[h]] == c % ODD[h]
+                        tile = got if tile is None else jnp.where(here, got, tile)
                 parts.append(tile)
             top, rest = halves(jnp.concatenate(parts, axis=0))
             cols = pl.ds(chunk * LANES, LANES)

time: 74.4 us -> 74.2 us (level)
  no operation moved by 1% of the time
where the time goes in v8:
time: 74.2 us; the launch traced here: 73.9 us
  blocking collectives  69.5 us (94%)
  Pallas kernels  3.63 us (5%)
    all_to_all x1, blocking collectives, per_device(): swap(rows, 'tm')  34.9 us
    all_to_all x1, blocking collectives, per_device(): sums = swap(run_second(me, classes, second, mapping), 'tm')  13.1 us
    all_to_all x1, blocking collectives, per_device(): swap(run_first(me, swap(rows, 'tm'), first), 'tm', axis_index_groups=by_row)  11.1 us
    all_to_all x1, blocking collectives, per_device(): sifted, harmonic_sum = run_sift(swap(message, 'dm'), level, bins)  10.3 us

profile of v8, /device:TPU:513, one launch (start us, length us, event | category | flops | bytes accessed | tf_op | source)
XLA Modules:
  0.0 73.9 jit_solution(783844937612487900)
XLA Ops:
  0.6 1.0 %shard_map.113 = (f32[512,128]{1,0:T(8,128)S(1)}, bf16[640,256]{1,0:T(8,128)(2,1)S(1)}, f32[8,128]{1,0:T(8,128)S(1)}) custom-call(s32[1]{0:T(128)} %bitcast.d_ref, f32[512,128]{1,0:T(8,128)} %bitcast.19, s32[8,16]{1,0:T(8,128)} %bitcast.20, s32[1,8]{1,0:T(1,128)} %bitcast.21), custom_call_target="tpu_custom_call" | custom-call | tf_op jit(solution)/shard_map/pallas_call | solution.py:414
  1.7 0.0 copy-start
  1.7 0.0 copy-start.4
  1.7 34.9 %all_to_all.20.x_ref = f32[16,32,128]{2,1,0:T(8,128)S(1)} all-to-all(f32[16,32,128]{2,1,0:T(8,128)S(1)} %bitcast.17), channel_id=1, replica_groups=mesh['beam'=2,'tm'=16,'dm'=8] {'tm'}, dimensions={0} | all-to-all | bytes 524288 | tf_op jit(solution)/shard_map/all_to_all | solution.py:509
  36.6 0.0 copy-done
  36.6 0.0 copy-done.4
  36.6 0.0 copy-start.3
  36.6 0.0 copy-start.5
  36.7 0.0 copy-start.6
  36.7 0.1 shard_map.114
  36.8 0.0 copy-start.1
  36.8 0.0 copy-start.2
  36.8 11.1 %all_to_all.21.x_ref = f32[8,64,128]{2,1,0:T(8,128)S(1)} all-to-all(f32[8,64,128]{2,1,0:T(8,128)S(1)} %shard_map.114), channel_id=1, replica_groups={{0,8,16,24,32,40,48,56},{64,72,80,88,96,104,112,120},{1,9,17,25,33,41,4..., dimensions={0} | all-to-all | bytes 524288 | tf_op jit(solution)/shard_map/all_to_all | solution.py:509
  48.0 0.0 copy-done.3
  48.0 0.0 copy-done.5
  48.0 0.0 copy-done.6
  48.0 0.0 copy-done.1
  48.0 0.0 copy-done.2
  48.0 1.3 %shard_map.115 = f32[272,128]{1,0:T(8,128)S(1)} custom-call(s32[1]{0:T(128)} %bitcast.d_ref, f32[8,64,128]{2,1,0:T(8,128)S(1)} %all_to_all.21.x_ref, f32[2,16,16,128]{3,2,1,0:T(8,128)S(1)} %copy-done.2, f32[2,8,16,128]{3,2,1,0:T(8,128)S(1)} %copy-done.3, f32[2,16,128]{2,1,0:T(8,128)S(1)} %copy-done.6, f32[8,8,128]{2,1,0:T(8,128)S(1)} %copy-done.5, ...), custom_call_target="tpu_custom_call" | custom-call | tf_op jit(solution)/shard_map/pallas_call | solution.py:449
  49.3 13.1 %all_to_all.22 = f32[16,1,2176]{2,1,0:T(1,128)S(1)} all-to-all(f32[16,1,2176]{2,1,0:T(1,128)S(1)} %bitcast.15), channel_id=1, replica_groups=mesh['beam'=2,'tm'=16,'dm'=8] {'tm'}, dimensions={0} | all-to-all | bytes 278528 | tf_op jit(solution)/shard_map/all_to_all | solution.py:510
  62.4 0.2 shard_map.116
  62.6 10.3 %all_to_all.23 = f32[8,1,2176]{2,1,0:T(1,128)S(1)} all-to-all(f32[8,1,2176]{2,1,0:T(1,128)S(1)} %bitcast.18), channel_id=1, replica_groups=mesh['beam'=2,'tm'=16,'dm'=8] {'dm'}, dimensions={0} | all-to-all | bytes 139264 | tf_op jit(solution)/shard_map/all_to_all | solution.py:512
  72.9 1.0 %shard_map.117 = (f32[8,16,128]{2,1,0:T(8,128)}, f32[2,2048]{1,0:T(2,128)}) custom-call(f32[136,128]{1,0:T(8,128)S(1)} %bitcast.16, f32[16,128]{1,0:T(8,128)S(1)} %get-tuple-element.14.level_ref, f32[2,2048]{1,0:T(2,128)S(1)} %get-tuple-element.15.bins_ref), custom_call_target="tpu_custom_call" | custom-call | tf_op jit(solution)/shard_map/pallas_call | solution.py:485
Async XLA Ops:
  1.7 35.0 %copy-start = (f32[2,8,32,128]{3,2,1,0:T(8,128)S(1)}, f32[2,8,32,128]{3,2,1,0:T(8,128)}, u32[]{:S(2)}) copy-start(f32[2,8,32,128]{3,2,1,0:T(8,128)} %constant.20.clone.within_ref) | copy-start | bytes 786436
  1.7 35.0 %copy-start.4 = (f32[8,2,8,128]{3,2,1,0:T(8,128)S(1)}, f32[8,2,8,128]{3,2,1,0:T(8,128)}, u32[]{:S(2)}) copy-start(f32[8,2,8,128]{3,2,1,0:T(8,128)} %constant.21.clone.shift_ref) | copy-start | bytes 196612
  36.6 11.3 %copy-start.3 = (f32[2,8,16,128]{3,2,1,0:T(8,128)S(1)}, f32[2,8,16,128]{3,2,1,0:T(8,128)}, u32[]{:S(2)}) copy-start(f32[2,8,16,128]{3,2,1,0:T(8,128)} %constant.23.clone.middle_ref) | copy-start | bytes 393220
  36.6 11.3 %copy-start.5 = (f32[8,8,128]{2,1,0:T(8,128)S(1)}, f32[8,8,128]{2,1,0:T(8,128)}, u32[]{:S(2)}) copy-start(f32[8,8,128]{2,1,0:T(8,128)} %constant.25.clone.fit_ref) | copy-start | bytes 98308
  36.7 11.3 %copy-start.6 = (f32[2,16,128]{2,1,0:T(8,128)S(1)}, f32[2,16,128]{2,1,0:T(8,128)}, u32[]{:S(2)}) copy-start(f32[2,16,128]{2,1,0:T(8,128)} %constant.24.clone.between_ref) | copy-start | bytes 49156
  36.8 11.2 %copy-start.1 = (bf16[512,256]{1,0:T(8,128)(2,1)S(1)}, bf16[512,256]{1,0:T(8,128)(2,1)}, u32[]{:S(2)}) copy-start(bf16[512,256]{1,0:T(8,128)(2,1)} %constant.26.clone.table_ref) | copy-start | bytes 786436
  36.8 11.2 %copy-start.2 = (f32[2,16,16,128]{3,2,1,0:T(8,128)S(1)}, f32[2,16,16,128]{3,2,1,0:T(8,128)}, u32[]{:S(2)}) copy-start(f32[2,16,16,128]{3,2,1,0:T(8,128)} %constant.22.clone.after_ref) | copy-start | bytes 786436

commit v9 on v8

--- a/solution.py
+++ b/solution.py
@@ -353,10 +353,8 @@
         msg_ref[e * ROWS + 2 * SUB : (e + 1) * ROWS, :] = m_ref[e : e + 1, :]
 
 
-def sift_kernel(x_ref, level_ref, bins_ref, o_ref, hs_ref, out_scr, sems):
-    steps = sems.shape[0] - 1
-    bins_out = pltpu.make_async_copy(bins_ref, hs_ref, sems.at[steps])
-    bins_out.start()
+def sift_kernel(x_ref, level_ref, bins_ref, o_ref, hs_ref):
+    hs_ref[...] = bins_ref[...]
     bands, slots = o_ref.shape[:2]
     level = level_ref[...]
     rows = bands * slots
@@ -378,19 +376,9 @@
     both = jnp.concatenate([pick(tile_id), pick(tile_id + 1)], axis=0)
     parts = jnp.dot(both, jnp.concatenate(halves(diff), axis=1), preferred_element_type=F32)
     parts = parts[:, :LANES] + parts[:, LANES:]
-    copies = []
-    for step in range(steps):
-        part = slice(step * rows // steps, (step + 1) * rows // steps)
-        joined = jnp.where(lane[part] >= offset[part], parts[:rows][part], parts[rows:][part])
-        moved = jnp.take_along_axis(joined, (lane[part] + offset[part]) & (LANES - 1), axis=1)
-        moved = jnp.where(start[part] >= 0, moved, 0.0)
-        here = pl.ds(step * bands // steps, bands // steps)
-        out_scr[here] = moved.reshape(bands // steps, slots, LANES)
-        copies.append(pltpu.make_async_copy(out_scr.at[here], o_ref.at[here], sems.at[step]))
-        copies[-1].start()
-    for copy in copies:
-        copy.wait()
-    bins_out.wait()
+    joined = jnp.where(lane >= offset, parts[:rows], parts[rows:])
+    moved = jnp.take_along_axis(joined, (lane + offset) & (LANES - 1), axis=1)
+    o_ref[...] = jnp.where(start >= 0, moved, 0.0).reshape(bands, slots, LANES)
 
 
 PARAMS = pltpu.CompilerParams(vmem_limit_bytes=16 * 2**20)
@@ -480,8 +468,6 @@
 
 def run_sift(received, level, bins):
     bands = received.shape[0]
-    steps = 1
-    anywhere = pl.BlockSpec(memory_space=pl.ANY)
     return pl.pallas_call(
         sift_kernel,
         out_shape=(
@@ -489,11 +475,7 @@
             jax.ShapeDtypeStruct(bins.shape, F32),
         ),
         in_specs=spaces(*"vvv"),
-        out_specs=[anywhere, anywhere],
-        scratch_shapes=[
-            pltpu.VMEM((bands, 2 * SUB, LANES), F32),
-            pltpu.SemaphoreType.DMA((steps + 1,)),
-        ],
+        out_specs=spaces(*"vv"),
         compiler_params=PARAMS,
     )(near(received.reshape(-1, LANES)), near(level), near(bins))
 

time: 74.2 us -> 74.2 us (level)
  no operation moved by 1% of the time
where the time goes in v9:
time: 74.2 us; the launch traced here: 73.9 us
  blocking collectives  69.5 us (94%)
  Pallas kernels  3.62 us (5%)
    all_to_all x1, blocking collectives, per_device(): swap(rows, 'tm')  34.9 us
    all_to_all x1, blocking collectives, per_device(): sums = swap(run_second(me, classes, second, mapping), 'tm')  13.1 us
    all_to_all x1, blocking collectives, per_device(): swap(run_first(me, swap(rows, 'tm'), first), 'tm', axis_index_groups=by_row)  11.1 us
    all_to_all x1, blocking collectives, per_device(): sifted, harmonic_sum = run_sift(swap(message, 'dm'), level, bins)  10.3 us

profile of v9, /device:TPU:513, one launch (start us, length us, event | category | flops | bytes accessed | tf_op | source)
XLA Modules:
  0.0 73.9 jit_solution(18053402114947128693)
XLA Ops:
  0.6 1.0 %shard_map.113 = (f32[512,128]{1,0:T(8,128)S(1)}, bf16[640,256]{1,0:T(8,128)(2,1)S(1)}, f32[8,128]{1,0:T(8,128)S(1)}) custom-call(s32[1]{0:T(128)} %bitcast.d_ref, f32[512,128]{1,0:T(8,128)} %bitcast.19, s32[8,16]{1,0:T(8,128)} %bitcast.20, s32[1,8]{1,0:T(1,128)} %bitcast.21), custom_call_target="tpu_custom_call" | custom-call | tf_op jit(solution)/shard_map/pallas_call | solution.py:402
  1.7 0.0 copy-start
  1.7 0.0 copy-start.4
  1.7 34.9 %all_to_all.20.x_ref = f32[16,32,128]{2,1,0:T(8,128)S(1)} all-to-all(f32[16,32,128]{2,1,0:T(8,128)S(1)} %bitcast.17), channel_id=1, replica_groups=mesh['beam'=2,'tm'=16,'dm'=8] {'tm'}, dimensions={0} | all-to-all | bytes 524288 | tf_op jit(solution)/shard_map/all_to_all | solution.py:491
  36.6 0.0 copy-done
  36.6 0.0 copy-done.4
  36.6 0.0 copy-start.3
  36.6 0.0 copy-start.5
  36.7 0.0 copy-start.6
  36.7 0.1 shard_map.114
  36.8 0.0 copy-start.1
  36.8 0.0 copy-start.2
  36.8 11.1 %all_to_all.21.x_ref = f32[8,64,128]{2,1,0:T(8,128)S(1)} all-to-all(f32[8,64,128]{2,1,0:T(8,128)S(1)} %shard_map.114), channel_id=1, replica_groups={{0,8,16,24,32,40,48,56},{64,72,80,88,96,104,112,120},{1,9,17,25,33,41,4..., dimensions={0} | all-to-all | bytes 524288 | tf_op jit(solution)/shard_map/all_to_all | solution.py:491
  48.0 0.0 copy-done.3
  48.0 0.0 copy-done.5
  48.0 0.0 copy-done.6
  48.0 0.0 copy-done.1
  48.0 0.0 copy-done.2
  48.0 1.3 %shard_map.115 = f32[272,128]{1,0:T(8,128)S(1)} custom-call(s32[1]{0:T(128)} %bitcast.d_ref, f32[8,64,128]{2,1,0:T(8,128)S(1)} %all_to_all.21.x_ref, f32[2,16,16,128]{3,2,1,0:T(8,128)S(1)} %copy-done.2, f32[2,8,16,128]{3,2,1,0:T(8,128)S(1)} %copy-done.3, f32[2,16,128]{2,1,0:T(8,128)S(1)} %copy-done.6, f32[8,8,128]{2,1,0:T(8,128)S(1)} %copy-done.5, ...), custom_call_target="tpu_custom_call" | custom-call | tf_op jit(solution)/shard_map/pallas_call | solution.py:437
  49.3 13.1 %all_to_all.22 = f32[16,1,2176]{2,1,0:T(1,128)S(1)} all-to-all(f32[16,1,2176]{2,1,0:T(1,128)S(1)} %bitcast.15), channel_id=1, replica_groups=mesh['beam'=2,'tm'=16,'dm'=8] {'tm'}, dimensions={0} | all-to-all | bytes 278528 | tf_op jit(solution)/shard_map/all_to_all | solution.py:492
  62.4 0.2 shard_map.116
  62.6 10.3 %all_to_all.23 = f32[8,1,2176]{2,1,0:T(1,128)S(1)} all-to-all(f32[8,1,2176]{2,1,0:T(1,128)S(1)} %bitcast.18), channel_id=1, replica_groups=mesh['beam'=2,'tm'=16,'dm'=8] {'dm'}, dimensions={0} | all-to-all | bytes 139264 | tf_op jit(solution)/shard_map/all_to_all | solution.py:494
  72.9 1.0 %shard_map.117 = (f32[8,16,128]{2,1,0:T(8,128)}, f32[2,2048]{1,0:T(2,128)}) custom-call(f32[136,128]{1,0:T(8,128)S(1)} %bitcast.16, f32[16,128]{1,0:T(8,128)S(1)} %get-tuple-element.14.level_ref, f32[2,2048]{1,0:T(2,128)S(1)} %get-tuple-element.15.bins_ref), custom_call_target="tpu_custom_call" | custom-call | tf_op jit(solution)/shard_map/pallas_call | solution.py:471
Async XLA Ops:
  1.7 35.0 %copy-start = (f32[2,8,32,128]{3,2,1,0:T(8,128)S(1)}, f32[2,8,32,128]{3,2,1,0:T(8,128)}, u32[]{:S(2)}) copy-start(f32[2,8,32,128]{3,2,1,0:T(8,128)} %constant.20.clone.within_ref) | copy-start | bytes 786436
  1.7 35.0 %copy-start.4 = (f32[8,2,8,128]{3,2,1,0:T(8,128)S(1)}, f32[8,2,8,128]{3,2,1,0:T(8,128)}, u32[]{:S(2)}) copy-start(f32[8,2,8,128]{3,2,1,0:T(8,128)} %constant.21.clone.shift_ref) | copy-start | bytes 196612
  36.6 11.3 %copy-start.3 = (f32[2,8,16,128]{3,2,1,0:T(8,128)S(1)}, f32[2,8,16,128]{3,2,1,0:T(8,128)}, u32[]{:S(2)}) copy-start(f32[2,8,16,128]{3,2,1,0:T(8,128)} %constant.23.clone.middle_ref) | copy-start | bytes 393220
  36.6 11.3 %copy-start.5 = (f32[8,8,128]{2,1,0:T(8,128)S(1)}, f32[8,8,128]{2,1,0:T(8,128)}, u32[]{:S(2)}) copy-start(f32[8,8,128]{2,1,0:T(8,128)} %constant.25.clone.fit_ref) | copy-start | bytes 98308
  36.7 11.3 %copy-start.6 = (f32[2,16,128]{2,1,0:T(8,128)S(1)}, f32[2,16,128]{2,1,0:T(8,128)}, u32[]{:S(2)}) copy-start(f32[2,16,128]{2,1,0:T(8,128)} %constant.24.clone.between_ref) | copy-start | bytes 49156
  36.8 11.2 %copy-start.1 = (bf16[512,256]{1,0:T(8,128)(2,1)S(1)}, bf16[512,256]{1,0:T(8,128)(2,1)}, u32[]{:S(2)}) copy-start(bf16[512,256]{1,0:T(8,128)(2,1)} %constant.26.clone.table_ref) | copy-start | bytes 786436
  36.8 11.2 %copy-start.2 = (f32[2,16,16,128]{3,2,1,0:T(8,128)S(1)}, f32[2,16,16,128]{3,2,1,0:T(8,128)}, u32[]{:S(2)}) copy-start(f32[2,16,16,128]{3,2,1,0:T(8,128)} %constant.22.clone.after_ref) | copy-start | bytes 786436

commit v10 on v9

--- a/solution.py
+++ b/solution.py
@@ -412,7 +412,7 @@
             pltpu.VMEM((2 * tiles, LANES), F32),
             pltpu.VMEM(starts.shape, jnp.int32),
             pltpu.VMEM(counts.shape, jnp.int32),
-            pltpu.SemaphoreType.DMA((6,)),
+            pltpu.SemaphoreType.DMA((4,)),
         ],
         compiler_params=PARAMS,
     )(me, *[pltpu.with_memory_space_constraint(x, pltpu.HBM) for x in (lines, starts, counts)])

time: 74.2 us -> 74.2 us (level)
  no operation moved by 1% of the time
where the time goes in v10:
time: 74.2 us; the launch traced here: 73.9 us
  blocking collectives  69.5 us (94%)
  Pallas kernels  3.64 us (5%)
    all_to_all x1, blocking collectives, per_device(): swap(rows, 'tm')  34.9 us
    all_to_all x1, blocking collectives, per_device(): sums = swap(run_second(me, classes, second, mapping), 'tm')  13.1 us
    all_to_all x1, blocking collectives, per_device(): swap(run_first(me, swap(rows, 'tm'), first), 'tm', axis_index_groups=by_row)  11.1 us
    all_to_all x1, blocking collectives, per_device(): sifted, harmonic_sum = run_sift(swap(message, 'dm'), level, bins)  10.3 us

profile of v10, /device:TPU:513, one launch (start us, length us, event | category | flops | bytes accessed | tf_op | source)
XLA Modules:
  0.0 73.9 jit_solution(18051446653029910238)
XLA Ops:
  0.6 1.0 %shard_map.113 = (f32[512,128]{1,0:T(8,128)S(1)}, bf16[640,256]{1,0:T(8,128)(2,1)S(1)}, f32[8,128]{1,0:T(8,128)S(1)}) custom-call(s32[1]{0:T(128)} %bitcast.d_ref, f32[512,128]{1,0:T(8,128)} %bitcast.19, s32[8,16]{1,0:T(8,128)} %bitcast.20, s32[1,8]{1,0:T(1,128)} %bitcast.21), custom_call_target="tpu_custom_call" | custom-call | tf_op jit(solution)/shard_map/pallas_call | solution.py:402
  1.7 0.0 copy-start
  1.7 0.0 copy-start.4
  1.7 34.9 %all_to_all.20.x_ref = f32[16,32,128]{2,1,0:T(8,128)S(1)} all-to-all(f32[16,32,128]{2,1,0:T(8,128)S(1)} %bitcast.17), channel_id=1, replica_groups=mesh['beam'=2,'tm'=16,'dm'=8] {'tm'}, dimensions={0} | all-to-all | bytes 524288 | tf_op jit(solution)/shard_map/all_to_all | solution.py:491
  36.7 0.0 copy-done
  36.7 0.0 copy-done.4
  36.7 0.0 copy-start.3
  36.7 0.0 copy-start.5
  36.7 0.0 copy-start.6
  36.7 0.1 shard_map.114
  36.8 0.0 copy-start.1
  36.8 0.0 copy-start.2
  36.8 11.1 %all_to_all.21.x_ref = f32[8,64,128]{2,1,0:T(8,128)S(1)} all-to-all(f32[8,64,128]{2,1,0:T(8,128)S(1)} %shard_map.114), channel_id=1, replica_groups={{0,8,16,24,32,40,48,56},{64,72,80,88,96,104,112,120},{1,9,17,25,33,41,4..., dimensions={0} | all-to-all | bytes 524288 | tf_op jit(solution)/shard_map/all_to_all | solution.py:491
  48.0 0.0 copy-done.3
  48.0 0.0 copy-done.5
  48.0 0.0 copy-done.6
  48.0 0.0 copy-done.1
  48.0 0.0 copy-done.2
  48.0 1.3 %shard_map.115 = f32[272,128]{1,0:T(8,128)S(1)} custom-call(s32[1]{0:T(128)} %bitcast.d_ref, f32[8,64,128]{2,1,0:T(8,128)S(1)} %all_to_all.21.x_ref, f32[2,16,16,128]{3,2,1,0:T(8,128)S(1)} %copy-done.2, f32[2,8,16,128]{3,2,1,0:T(8,128)S(1)} %copy-done.3, f32[2,16,128]{2,1,0:T(8,128)S(1)} %copy-done.6, f32[8,8,128]{2,1,0:T(8,128)S(1)} %copy-done.5, ...), custom_call_target="tpu_custom_call" | custom-call | tf_op jit(solution)/shard_map/pallas_call | solution.py:437
  49.3 13.1 %all_to_all.22 = f32[16,1,2176]{2,1,0:T(1,128)S(1)} all-to-all(f32[16,1,2176]{2,1,0:T(1,128)S(1)} %bitcast.15), channel_id=1, replica_groups=mesh['beam'=2,'tm'=16,'dm'=8] {'tm'}, dimensions={0} | all-to-all | bytes 278528 | tf_op jit(solution)/shard_map/all_to_all | solution.py:492
  62.4 0.2 shard_map.116
  62.6 10.3 %all_to_all.23 = f32[8,1,2176]{2,1,0:T(1,128)S(1)} all-to-all(f32[8,1,2176]{2,1,0:T(1,128)S(1)} %bitcast.18), channel_id=1, replica_groups=mesh['beam'=2,'tm'=16,'dm'=8] {'dm'}, dimensions={0} | all-to-all | bytes 139264 | tf_op jit(solution)/shard_map/all_to_all | solution.py:494
  72.9 1.0 %shard_map.117 = (f32[8,16,128]{2,1,0:T(8,128)}, f32[2,2048]{1,0:T(2,128)}) custom-call(f32[136,128]{1,0:T(8,128)S(1)} %bitcast.16, f32[16,128]{1,0:T(8,128)S(1)} %get-tuple-element.14.level_ref, f32[2,2048]{1,0:T(2,128)S(1)} %get-tuple-element.15.bins_ref), custom_call_target="tpu_custom_call" | custom-call | tf_op jit(solution)/shard_map/pallas_call | solution.py:471
Async XLA Ops:
  1.7 35.0 %copy-start = (f32[2,8,32,128]{3,2,1,0:T(8,128)S(1)}, f32[2,8,32,128]{3,2,1,0:T(8,128)}, u32[]{:S(2)}) copy-start(f32[2,8,32,128]{3,2,1,0:T(8,128)} %constant.20.clone.within_ref) | copy-start | bytes 786436
  1.7 35.0 %copy-start.4 = (f32[8,2,8,128]{3,2,1,0:T(8,128)S(1)}, f32[8,2,8,128]{3,2,1,0:T(8,128)}, u32[]{:S(2)}) copy-start(f32[8,2,8,128]{3,2,1,0:T(8,128)} %constant.21.clone.shift_ref) | copy-start | bytes 196612
  36.7 11.3 %copy-start.3 = (f32[2,8,16,128]{3,2,1,0:T(8,128)S(1)}, f32[2,8,16,128]{3,2,1,0:T(8,128)}, u32[]{:S(2)}) copy-start(f32[2,8,16,128]{3,2,1,0:T(8,128)} %constant.23.clone.middle_ref) | copy-start | bytes 393220
  36.7 11.3 %copy-start.5 = (f32[8,8,128]{2,1,0:T(8,128)S(1)}, f32[8,8,128]{2,1,0:T(8,128)}, u32[]{:S(2)}) copy-start(f32[8,8,128]{2,1,0:T(8,128)} %constant.25.clone.fit_ref) | copy-start | bytes 98308
  36.7 11.3 %copy-start.6 = (f32[2,16,128]{2,1,0:T(8,128)S(1)}, f32[2,16,128]{2,1,0:T(8,128)}, u32[]{:S(2)}) copy-start(f32[2,16,128]{2,1,0:T(8,128)} %constant.24.clone.between_ref) | copy-start | bytes 49156
  36.8 11.2 %copy-start.1 = (bf16[512,256]{1,0:T(8,128)(2,1)S(1)}, bf16[512,256]{1,0:T(8,128)(2,1)}, u32[]{:S(2)}) copy-start(bf16[512,256]{1,0:T(8,128)(2,1)} %constant.26.clone.table_ref) | copy-start | bytes 786436
  36.8 11.2 %copy-start.2 = (f32[2,16,16,128]{3,2,1,0:T(8,128)S(1)}, f32[2,16,16,128]{3,2,1,0:T(8,128)}, u32[]{:S(2)}) copy-start(f32[2,16,16,128]{3,2,1,0:T(8,128)} %constant.22.clone.after_ref) | copy-start | bytes 786436

commit v11 on v10

--- a/solution.py
+++ b/solution.py
@@ -412,7 +412,7 @@
             pltpu.VMEM((2 * tiles, LANES), F32),
             pltpu.VMEM(starts.shape, jnp.int32),
             pltpu.VMEM(counts.shape, jnp.int32),
-            pltpu.SemaphoreType.DMA((4,)),
+            pltpu.SemaphoreType.DMA((3,)),
         ],
         compiler_params=PARAMS,
     )(me, *[pltpu.with_memory_space_constraint(x, pltpu.HBM) for x in (lines, starts, counts)])

time: 74.2 us -> 74.2 us (level)
  no operation moved by 1% of the time
where the time goes in v11:
time: 74.2 us; the launch traced here: 73.9 us
  blocking collectives  69.5 us (94%)
  Pallas kernels  3.62 us (5%)
    all_to_all x1, blocking collectives, per_device(): swap(rows, 'tm')  34.9 us
    all_to_all x1, blocking collectives, per_device(): sums = swap(run_second(me, classes, second, mapping), 'tm')  13.1 us
    all_to_all x1, blocking collectives, per_device(): swap(run_first(me, swap(rows, 'tm'), first), 'tm', axis_index_groups=by_row)  11.1 us
    all_to_all x1, blocking collectives, per_device(): sifted, harmonic_sum = run_sift(swap(message, 'dm'), level, bins)  10.3 us

profile of v11, /device:TPU:513, one launch (start us, length us, event | category | flops | bytes accessed | tf_op | source)
XLA Modules:
  0.0 73.9 jit_solution(4786675612149341424)
XLA Ops:
  0.6 1.0 %shard_map.113 = (f32[512,128]{1,0:T(8,128)S(1)}, bf16[640,256]{1,0:T(8,128)(2,1)S(1)}, f32[8,128]{1,0:T(8,128)S(1)}) custom-call(s32[1]{0:T(128)} %bitcast.d_ref, f32[512,128]{1,0:T(8,128)} %bitcast.19, s32[8,16]{1,0:T(8,128)} %bitcast.20, s32[1,8]{1,0:T(1,128)} %bitcast.21), custom_call_target="tpu_custom_call" | custom-call | tf_op jit(solution)/shard_map/pallas_call | solution.py:402
  1.7 0.0 copy-start
  1.7 0.0 copy-start.4
  1.7 34.9 %all_to_all.20.x_ref = f32[16,32,128]{2,1,0:T(8,128)S(1)} all-to-all(f32[16,32,128]{2,1,0:T(8,128)S(1)} %bitcast.17), channel_id=1, replica_groups=mesh['beam'=2,'tm'=16,'dm'=8] {'tm'}, dimensions={0} | all-to-all | bytes 524288 | tf_op jit(solution)/shard_map/all_to_all | solution.py:491
  36.6 0.0 copy-done
  36.6 0.0 copy-done.4
  36.6 0.0 copy-start.3
  36.6 0.0 copy-start.5
  36.7 0.0 copy-start.6
  36.7 0.1 shard_map.114
  36.8 0.0 copy-start.1
  36.8 0.0 copy-start.2
  36.8 11.1 %all_to_all.21.x_ref = f32[8,64,128]{2,1,0:T(8,128)S(1)} all-to-all(f32[8,64,128]{2,1,0:T(8,128)S(1)} %shard_map.114), channel_id=1, replica_groups={{0,8,16,24,32,40,48,56},{64,72,80,88,96,104,112,120},{1,9,17,25,33,41,4..., dimensions={0} | all-to-all | bytes 524288 | tf_op jit(solution)/shard_map/all_to_all | solution.py:491
  48.0 0.0 copy-done.3
  48.0 0.0 copy-done.5
  48.0 0.0 copy-done.6
  48.0 0.0 copy-done.1
  48.0 0.0 copy-done.2
  48.0 1.3 %shard_map.115 = f32[272,128]{1,0:T(8,128)S(1)} custom-call(s32[1]{0:T(128)} %bitcast.d_ref, f32[8,64,128]{2,1,0:T(8,128)S(1)} %all_to_all.21.x_ref, f32[2,16,16,128]{3,2,1,0:T(8,128)S(1)} %copy-done.2, f32[2,8,16,128]{3,2,1,0:T(8,128)S(1)} %copy-done.3, f32[2,16,128]{2,1,0:T(8,128)S(1)} %copy-done.6, f32[8,8,128]{2,1,0:T(8,128)S(1)} %copy-done.5, ...), custom_call_target="tpu_custom_call" | custom-call | tf_op jit(solution)/shard_map/pallas_call | solution.py:437
  49.3 13.1 %all_to_all.22 = f32[16,1,2176]{2,1,0:T(1,128)S(1)} all-to-all(f32[16,1,2176]{2,1,0:T(1,128)S(1)} %bitcast.15), channel_id=1, replica_groups=mesh['beam'=2,'tm'=16,'dm'=8] {'tm'}, dimensions={0} | all-to-all | bytes 278528 | tf_op jit(solution)/shard_map/all_to_all | solution.py:492
  62.4 0.2 shard_map.116
  62.6 10.3 %all_to_all.23 = f32[8,1,2176]{2,1,0:T(1,128)S(1)} all-to-all(f32[8,1,2176]{2,1,0:T(1,128)S(1)} %bitcast.18), channel_id=1, replica_groups=mesh['beam'=2,'tm'=16,'dm'=8] {'dm'}, dimensions={0} | all-to-all | bytes 139264 | tf_op jit(solution)/shard_map/all_to_all | solution.py:494
  72.9 1.0 %shard_map.117 = (f32[8,16,128]{2,1,0:T(8,128)}, f32[2,2048]{1,0:T(2,128)}) custom-call(f32[136,128]{1,0:T(8,128)S(1)} %bitcast.16, f32[16,128]{1,0:T(8,128)S(1)} %get-tuple-element.14.level_ref, f32[2,2048]{1,0:T(2,128)S(1)} %get-tuple-element.15.bins_ref), custom_call_target="tpu_custom_call" | custom-call | tf_op jit(solution)/shard_map/pallas_call | solution.py:471
Async XLA Ops:
  1.7 35.0 %copy-start = (f32[2,8,32,128]{3,2,1,0:T(8,128)S(1)}, f32[2,8,32,128]{3,2,1,0:T(8,128)}, u32[]{:S(2)}) copy-start(f32[2,8,32,128]{3,2,1,0:T(8,128)} %constant.20.clone.within_ref) | copy-start | bytes 786436
  1.7 35.0 %copy-start.4 = (f32[8,2,8,128]{3,2,1,0:T(8,128)S(1)}, f32[8,2,8,128]{3,2,1,0:T(8,128)}, u32[]{:S(2)}) copy-start(f32[8,2,8,128]{3,2,1,0:T(8,128)} %constant.21.clone.shift_ref) | copy-start | bytes 196612
  36.6 11.3 %copy-start.3 = (f32[2,8,16,128]{3,2,1,0:T(8,128)S(1)}, f32[2,8,16,128]{3,2,1,0:T(8,128)}, u32[]{:S(2)}) copy-start(f32[2,8,16,128]{3,2,1,0:T(8,128)} %constant.23.clone.middle_ref) | copy-start | bytes 393220
  36.6 11.3 %copy-start.5 = (f32[8,8,128]{2,1,0:T(8,128)S(1)}, f32[8,8,128]{2,1,0:T(8,128)}, u32[]{:S(2)}) copy-start(f32[8,8,128]{2,1,0:T(8,128)} %constant.25.clone.fit_ref) | copy-start | bytes 98308
  36.7 11.3 %copy-start.6 = (f32[2,16,128]{2,1,0:T(8,128)S(1)}, f32[2,16,128]{2,1,0:T(8,128)}, u32[]{:S(2)}) copy-start(f32[2,16,128]{2,1,0:T(8,128)} %constant.24.clone.between_ref) | copy-start | bytes 49156
  36.8 11.2 %copy-start.1 = (bf16[512,256]{1,0:T(8,128)(2,1)S(1)}, bf16[512,256]{1,0:T(8,128)(2,1)}, u32[]{:S(2)}) copy-start(bf16[512,256]{1,0:T(8,128)(2,1)} %constant.26.clone.table_ref) | copy-start | bytes 786436
  36.8 11.2 %copy-start.2 = (f32[2,16,16,128]{3,2,1,0:T(8,128)S(1)}, f32[2,16,16,128]{3,2,1,0:T(8,128)}, u32[]{:S(2)}) copy-start(f32[2,16,16,128]{3,2,1,0:T(8,128)} %constant.22.clone.after_ref) | copy-start | bytes 786436
